TPU v7x, 8 devices: a whole 2x2x1 slice. The times are simulated.
8 devices in a mesh: dp: 2 (over z, y), tp: 4 (over x, core).
Axes of the slice: x: 2, y: 2, z: 1, core: 2. Of those that a mesh axis runs over, the one named last changes fastest.
Arguments:
- x: bfloat16 [2, 96, 1536], P('dp', 'tp'), parts along dimension 0
- ln1_gamma: float32 [1536], replicated
- ln1_beta: float32 [1536], replicated
- w_qkv: bfloat16 [1536, 16, 3, 96], P(None, 'tp')
- b_qkv: float32 [16, 3, 96], P('tp')
- w_out: bfloat16 [1536, 1536], P('tp')
- b_out: float32 [1536], replicated
- ln2_gamma: float32 [1536], replicated
- ln2_beta: float32 [1536], replicated
- w_up: bfloat16 [1536, 6144], P(None, 'tp')
- b_up: float32 [6144], P('tp')
- w_down: bfloat16 [6144, 1536], P('tp')
- b_down: float32 [1536], replicated
- grad_y: bfloat16 [2, 96, 1536], P('dp', 'tp'), parts along dimension 0
Outputs:
- output 1: bfloat16 [2, 96, 1536], P('dp', 'tp'), parts along dimension 0
- output 2: bfloat16 [2, 96, 1536], P('dp', 'tp'), parts along dimension 0
- output 3: float32 [3072], P('dp'), parts along dimension 0
- output 4: float32 [3072], P('dp'), parts along dimension 0
- output 5: bfloat16 [3072, 16, 3, 96], P('dp', 'tp'), parts along dimension 0
- output 6: float32 [32, 3, 96], P(('dp', 'tp')), parts along dimension 0
- output 7: bfloat16 [3072, 1536], P(('dp', 'tp')), parts along dimension 0
- output 8: float32 [3072], P('dp'), parts along dimension 0
- output 9: float32 [3072], P('dp'), parts along dimension 0
- output 10: float32 [3072], P('dp'), parts along dimension 0
- output 11: bfloat16 [3072, 6144], P('dp', 'tp'), parts along dimension 0
- output 12: float32 [12288], P(('dp', 'tp')), parts along dimension 0
- output 13: bfloat16 [12288, 1536], P(('dp', 'tp')), parts along dimension 0
- output 14: float32 [3072], P('dp'), parts along dimension 0
There are 2 independent parts. A program takes and returns all parts, laid end to end along the dimension named above; an argument that names none is the same for every part.
All inputs are finite; a program needn't handle non-finite values.
Results may differ from a plain program's by a relative error of at most 0.0173697.
Values are sent between devices in bfloat16 or wider.
A program may use at most 1 GiB of HBM per device.

v0:
```python
import math
import jax
import jax.numpy as jnp
from jax import lax
from jax.sharding import PartitionSpec as P

EPS = 1e-5
MASK_VALUE = -1e30


def alibi_slopes(n_heads):
    closest = 2 ** int(math.floor(math.log2(n_heads)))
    base_ratio = 2.0 ** (-8.0 / closest)
    extra_ratio = 2.0 ** (-4.0 / closest)
    remaining = min(closest, n_heads - closest)
    slopes = [base_ratio ** (i + 1) for i in range(closest)]
    slopes = slopes + [extra_ratio ** (2 * i + 1) for i in range(remaining)]
    return jnp.array(slopes, dtype=jnp.float32)


def layer_norm(values, ln_gain, ln_bias):
    row_mean = jnp.mean(values, axis=-1, keepdims=True)
    centered = values - row_mean
    variance = jnp.mean(centered * centered, axis=-1, keepdims=True)
    return centered * lax.rsqrt(variance + EPS) * ln_gain + ln_bias


def gelu_tanh(values):
    return jax.nn.gelu(values, approximate=True)


def seq_gather(values):
    return lax.all_gather(values, 'tp', axis=1, tiled=True)


def seq_reduce(values):
    return lax.psum_scatter(values, 'tp', scatter_dimension=1, tiled=True)


def solution(mesh):
    tp_size = mesh.shape['tp']

    def local_step(x, ln1_gamma, ln1_beta, w_qkv, b_qkv, w_out, b_out, ln2_gamma, ln2_beta, w_up, b_up, w_down, b_down, grad_y):
        batch_size, seq_local = x.shape[0], x.shape[1]
        local_heads, head_size = w_qkv.shape[1], w_qkv.shape[3]
        seq_full = seq_local * tp_size
        score_scale = head_size ** -0.5
        tp_index = lax.axis_index('tp')
        slopes = lax.dynamic_slice_in_dim(alibi_slopes(local_heads * tp_size), tp_index * local_heads, local_heads)
        positions = jnp.arange(seq_full)
        causal = positions[None, :] <= positions[:, None]
        alibi_bias = slopes[:, None] * positions.astype(jnp.float32)[None, :]

        x_f = x.astype(jnp.float32)
        h_full = seq_gather(layer_norm(x_f, ln1_gamma, ln1_beta).astype(jnp.bfloat16))
        qkv_vals = (jnp.einsum('bsd,dhte->bshte', h_full, w_qkv, preferred_element_type=jnp.float32) + b_qkv).astype(jnp.bfloat16)
        q_heads = qkv_vals[:, :, :, 0]
        k_heads = qkv_vals[:, :, :, 1]
        v_heads = qkv_vals[:, :, :, 2]
        scores = jnp.einsum('bihe,bjhe->bhij', q_heads, k_heads, preferred_element_type=jnp.float32) * score_scale + alibi_bias[None, :, None, :]
        prob_f = jax.nn.softmax(jnp.where(causal, scores, MASK_VALUE), axis=-1)
        prob_bf = prob_f.astype(jnp.bfloat16)
        context = jnp.einsum('bhij,bjhe->bihe', prob_bf, v_heads, preferred_element_type=jnp.float32).astype(jnp.bfloat16)
        context_flat = context.reshape(batch_size, seq_full, local_heads * head_size)
        attn_out = seq_reduce(jnp.einsum('bsc,cd->bsd', context_flat, w_out, preferred_element_type=jnp.float32).astype(jnp.bfloat16))
        x_mid = x_f + attn_out.astype(jnp.float32) + b_out
        g_full = seq_gather(layer_norm(x_mid, ln2_gamma, ln2_beta).astype(jnp.bfloat16))
        pre_act = jnp.einsum('bsd,df->bsf', g_full, w_up, preferred_element_type=jnp.float32) + b_up
        activated = gelu_tanh(pre_act).astype(jnp.bfloat16)
        mlp_out = seq_reduce(jnp.einsum('bsf,fd->bsd', activated, w_down, preferred_element_type=jnp.float32).astype(jnp.bfloat16))
        y = (x_mid + mlp_out.astype(jnp.float32) + b_down).astype(jnp.bfloat16)

        grad_y_f = grad_y.astype(jnp.float32)
        grad_b_down = lax.psum(jnp.sum(grad_y_f, axis=(0, 1)), 'tp')
        grad_m_full = seq_gather(grad_y)
        grad_w_down = jnp.einsum('bsf,bsd->fd', activated, grad_m_full, preferred_element_type=jnp.float32).astype(jnp.bfloat16)
        grad_act = jnp.einsum('bsd,fd->bsf', grad_m_full, w_down, preferred_element_type=jnp.float32).astype(jnp.bfloat16)
        _, gelu_pullback = jax.vjp(gelu_tanh, pre_act)
        grad_pre = gelu_pullback(grad_act.astype(jnp.float32))[0]
        grad_b_up = jnp.sum(grad_pre, axis=(0, 1))
        grad_pre_bf = grad_pre.astype(jnp.bfloat16)
        grad_w_up = jnp.einsum('bsd,bsf->df', g_full, grad_pre_bf, preferred_element_type=jnp.float32).astype(jnp.bfloat16)
        grad_g = seq_reduce(jnp.einsum('bsf,df->bsd', grad_pre_bf, w_up, preferred_element_type=jnp.float32).astype(jnp.bfloat16))
        _, ln2_pullback = jax.vjp(layer_norm, x_mid, ln2_gamma, ln2_beta)
        grad_mid_ln, grad_ln2_gamma, grad_ln2_beta = ln2_pullback(grad_g.astype(jnp.float32))
        grad_ln2_gamma = lax.psum(grad_ln2_gamma, 'tp')
        grad_ln2_beta = lax.psum(grad_ln2_beta, 'tp')
        grad_mid = grad_y_f + grad_mid_ln
        grad_b_out = lax.psum(jnp.sum(grad_mid, axis=(0, 1)), 'tp')
        grad_attn_full = seq_gather(grad_mid.astype(jnp.bfloat16))
        grad_w_out = jnp.einsum('bsc,bsd->cd', context_flat, grad_attn_full, preferred_element_type=jnp.float32).astype(jnp.bfloat16)
        grad_context = jnp.einsum('bsd,cd->bsc', grad_attn_full, w_out, preferred_element_type=jnp.float32).astype(jnp.bfloat16)
        grad_context = grad_context.reshape(batch_size, seq_full, local_heads, head_size)
        grad_prob = jnp.einsum('bihe,bjhe->bhij', grad_context, v_heads, preferred_element_type=jnp.float32).astype(jnp.bfloat16).astype(jnp.float32)
        grad_v = jnp.einsum('bhij,bihe->bjhe', prob_bf, grad_context, preferred_element_type=jnp.float32).astype(jnp.bfloat16)
        grad_scores = prob_f * (grad_prob - jnp.sum(grad_prob * prob_f, axis=-1, keepdims=True))
        grad_scores_bf = grad_scores.astype(jnp.bfloat16)
        grad_q = (jnp.einsum('bhij,bjhe->bihe', grad_scores_bf, k_heads, preferred_element_type=jnp.float32) * score_scale).astype(jnp.bfloat16)
        grad_k = (jnp.einsum('bhij,bihe->bjhe', grad_scores_bf, q_heads, preferred_element_type=jnp.float32) * score_scale).astype(jnp.bfloat16)
        grad_qkv = jnp.stack([grad_q, grad_k, grad_v], axis=3)
        grad_b_qkv = jnp.sum(grad_qkv, axis=(0, 1), dtype=jnp.float32)
        grad_w_qkv = jnp.einsum('bsd,bshte->dhte', h_full, grad_qkv, preferred_element_type=jnp.float32).astype(jnp.bfloat16)
        grad_h = seq_reduce(jnp.einsum('bshte,dhte->bsd', grad_qkv, w_qkv, preferred_element_type=jnp.float32).astype(jnp.bfloat16))
        _, ln1_pullback = jax.vjp(layer_norm, x_f, ln1_gamma, ln1_beta)
        grad_x_ln, grad_ln1_gamma, grad_ln1_beta = ln1_pullback(grad_h.astype(jnp.float32))
        grad_ln1_gamma = lax.psum(grad_ln1_gamma, 'tp')
        grad_ln1_beta = lax.psum(grad_ln1_beta, 'tp')
        grad_x = (grad_mid + grad_x_ln).astype(jnp.bfloat16)
        return (y, grad_x, grad_ln1_gamma, grad_ln1_beta, grad_w_qkv, grad_b_qkv, grad_w_out, grad_b_out,
                grad_ln2_gamma, grad_ln2_beta, grad_w_up, grad_b_up, grad_w_down, grad_b_down)

    row_spec = P('dp', 'tp', None)
    in_specs = (row_spec, P(), P(), P(None, 'tp', None, None), P('tp', None, None), P('tp', None), P(), P(), P(),
                P(None, 'tp'), P('tp'), P('tp', None), P(), row_spec)
    out_specs = (row_spec, row_spec, P('dp'), P('dp'), P('dp', 'tp', None, None), P(('dp', 'tp'), None, None),
                 P(('dp', 'tp'), None), P('dp'), P('dp'), P('dp'), P('dp', 'tp'), P(('dp', 'tp')), P(('dp', 'tp'), None), P('dp'))
    return jax.shard_map(local_step, mesh=mesh, in_specs=in_specs, out_specs=out_specs, check_vma=False)
```

profile of v0, /device:TPU:0, one launch (start us, length us, event | category | flops | bytes accessed | tf_op | source)
XLA Modules:
  0.0 179.4 jit_solution(5886820254066262676)
XLA Ops:
  7.3 0.5 iota_convert_fusion
  7.8 0.6 iota_compare_fusion
  8.4 1.0 convert_reduce_fusion.3
  9.4 1.1 fusion.45
  10.5 0.6 copy-done.25
  11.1 1.0 fusion.43
  12.1 10.9 %all_gather.12 = bf16[1,96,1536]{2,1,0:T(8,128)(2,1)} all-gather(bf16[1,24,1536]{2,1,0:T(8,128)(2,1)S(1)} %fusion.43), channel_id=1, replica_groups=mesh['dp'=2,'tp'=4] {'tp'}, dimensions={1}, use_global_device_ids=true | all-gather | bytes 368640 | tf_op jit(solution)/shard_map/all_gather | solution.py:33
  23.0 1.3 copy.37
  24.3 0.7 dynamic_slice.3
  25.1 0.7 broadcast_multiply_fusion
  25.8 2.4 %fusion.9 = bf16[1,96,4,3,96]{4,1,3,2,0:T(8,128)(2,1)S(1)} fusion(bf16[1536,4,3,96]{0,3,2,1:T(8,128)(2,1)S(1)} %copy-done, bf16[1,96,1536]{2,1,0:T(8,128)(2,1)} %all_gather.12, f32[4,3,96]{2,1,0:T(4,128)} %copy.37), kind=kOutput, calls=%fused_computation.19 | convolution fusion | flops 339959808 | bytes 4059648 | tf_op jit(solution)/shard_map/bsd,dhte->bshte/dot_general | solution.py:56
  28.2 0.7 copy-done.11
  28.9 0.9 fusion.11
  29.8 0.7 copy-done.15
  30.4 1.3 fusion.64
  31.8 1.9 %convolution_convert_fusion.9 = bf16[4,96,96]{2,1,0:T(8,128)(2,1)} fusion(bf16[1,96,4,3,96]{4,1,3,2,0:T(8,128)(2,1)} %copy-done.11, f32[4,96]{1,0:T(4,128)} %get-tuple-element.32, f32[4,96,96]{1,2,0:T(8,128)} %copy-done.15), kind=kOutput, calls=%fused_computation.31 | convolution fusion | flops 7225823 | bytes 443904 | tf_op jit(solution)/shard_map/bhij,bjhe->bihe/dot_general | solution.py:63
  33.7 2.4 %fusion.3 = bf16[1,96,1536]{2,1,0:T(8,128)(2,1)} fusion(bf16[96,384]{0,1:T(8,128)(2,1)} %bitcast.119, bf16[384,1536]{1,0:T(8,128)(2,1)} %param.20), kind=kOutput, calls=%fused_computation.12 | convolution fusion | flops 113393664 | bytes 1548288 | tf_op jit(solution)/shard_map/bsc,cd->bsd/dot_general | solution.py:65
  36.2 9.1 %all_gather.14 = bf16[1,96,1536]{2,1,0:T(8,128)(2,1)} all-gather(bf16[1,24,1536]{2,1,0:T(8,128)(2,1)} %param.28), channel_id=1, replica_groups=mesh['dp'=2,'tp'=4] {'tp'}, dimensions={1}, use_global_device_ids=true | all-gather | bytes 368640 | tf_op jit(solution)/shard_map/all_gather | solution.py:33
  45.3 5.7 %reduce-scatter.17.cloned.1.call-done = bf16[1,24,1536]{2,1,0:T(8,128)(2,1)} async-done(((bf16[1,96,1536]{2,1,0:T(8,128)(2,1)}), bf16[1,24,1536]{2,1,0:T(8,128)(2,1)}) %reduce-scatter.17.cloned.1.call-update) | async-done | bytes 73744
  51.0 1.1 fusion.54
  52.2 1.1 multiply_reduce_fusion.1
  53.3 1.0 add_convert_fusion.2
  54.4 7.9 %all_gather.13 = bf16[1,96,1536]{2,1,0:T(8,128)(2,1)S(1)} all-gather(bf16[1,24,1536]{2,1,0:T(8,128)(2,1)S(1)} %add_convert_fusion.2), channel_id=1, replica_groups=mesh['dp'=2,'tp'=4] {'tp'}, dimensions={1}, use_global_device_ids=true | all-gather | bytes 368640 | tf_op jit(solution)/shard_map/all_gather | solution.py:33
  62.3 0.7 copy-done.3
  63.0 3.4 %convolution_add_fusion = f32[96,1536]{1,0:T(8,128)S(1)} fusion(bf16[1536,1536]{1,0:T(8,128)(2,1)} %param.24, bf16[1,96,1536]{2,1,0:T(8,128)(2,1)S(1)} %all_gather.13, f32[1536]{0:T(1024)} %param.25), kind=kOutput, calls=%fused_computation.4 | convolution fusion | flops 453132288 | bytes 5609472 | tf_op jit(solution)/shard_map/bsd,df->bsf/dot_general | solution.py:68
  66.4 3.6 %convolution_convert_fusion = bf16[1536,1536]{1,0:T(8,128)(2,1)} fusion(bf16[1,96,1536]{2,1,0:T(8,128)(2,1)S(1)} %copy-done.7, f32[96,1536]{1,0:T(8,128)S(1)} %convolution_add_fusion), kind=kOutput, calls=%fused_computation.1 | convolution fusion | flops 456671232 | bytes 5603328 | tf_op jit(solution)/shard_map/bsf,bsd->fd/dot_general | solution.py:76
  70.1 2.3 %fusion.65 = (f32[1536]{0:T(1024)}, bf16[96,1536]{1,0:T(8,128)(2,1)S(1)}) fusion(f32[96,1536]{1,0:T(8,128)S(1)} %convolution_add_fusion, bf16[1536,1536]{1,0:T(8,128)(2,1)S(1)} %bitcast.117, bf16[1,96,1536]{2,1,0:T(8,128)(2,1)S(1)} %copy-done.7), kind=kOutput, calls=%fused_computation.121 | convolution fusion | flops 456374784 | bytes 5904384 | tf_op jit(solution)/shard_map/bsd,fd->bsf/dot_general | solution.py:77
  72.3 0.7 copy-done.8
  73.0 2.3 %fusion.6 = bf16[1,96,1536]{2,1,0:T(8,128)(2,1)} fusion(bf16[1536,1536]{1,0:T(8,128)(2,1)S(1)} %bitcast.115, bf16[96,1536]{1,0:T(8,128)(2,1)S(1)} %get-tuple-element.37), kind=kOutput, calls=%fused_computation.15 | convolution fusion | flops 453132288 | bytes 5308416 | tf_op jit(solution)/shard_map/bsf,df->bsd/dot_general | solution.py:83
  75.4 4.7 %convolution_convert_fusion.1 = bf16[1536,1536]{1,0:T(8,128)(2,1)} fusion(bf16[1,96,1536]{2,1,0:T(8,128)(2,1)} %copy-done.3, bf16[96,1536]{1,0:T(8,128)(2,1)} %copy-done.8), kind=kOutput, calls=%fused_computation.2 | convolution fusion | flops 455344128 | bytes 5308416 | tf_op jit(solution)/shard_map/bsd,bsf->df/dot_general | solution.py:82
  80.1 4.0 %fusion.5 = bf16[1,96,1536]{2,1,0:T(8,128)(2,1)} fusion(bf16[1536,1536]{1,0:T(8,128)(2,1)} %param.26, f32[96,1536]{1,0:T(8,128)S(1)} %copy-done.2), kind=kOutput, calls=%fused_computation.14 | convolution fusion | flops 454459392 | bytes 5603328 | tf_op jit(solution)/shard_map/bsf,fd->bsd/dot_general | solution.py:70
  84.2 7.1 %reduce-scatter.21.cloned.1.call-done = bf16[1,24,1536]{2,1,0:T(8,128)(2,1)} async-done(((bf16[1,96,1536]{2,1,0:T(8,128)(2,1)}), bf16[1,24,1536]{2,1,0:T(8,128)(2,1)}) %reduce-scatter.21.cloned.1.call-update) | async-done | bytes 73744
  91.2 1.7 convert_reduce_fusion.2
  92.9 0.7 multiply_multiply_fusion.3
  93.6 0.5 copy-done.23
  94.1 1.7 fusion.48
  95.8 0.5 negate_multiply_fusion.1
  96.3 12.6 %reduce-scatter.19.cloned.1.call-done = bf16[1,24,1536]{2,1,0:T(8,128)(2,1)} async-done(((bf16[1,96,1536]{2,1,0:T(8,128)(2,1)}), bf16[1,24,1536]{2,1,0:T(8,128)(2,1)}) %reduce-scatter.19.cloned.1.call-update) | async-done | bytes 73744
  108.9 2.4 %fusion.63 = (f32[1536]{0:T(1024)}, f32[1,24,1536]{2,1,0:T(8,128)S(1)}, bf16[1,24,1536]{2,1,0:T(8,128)(2,1)}, f32[1536]{0:T(1024)}) fusion(f32[24]{0:T(128)} %negate_multiply_fusion.1, f32[24]{0:T(128)} %copy-done.23, f32[24]{0:T(128)} %copy-done.19, f32[1536]{0:T(1024)S(1)} %copy-done.14, bf16[1,24,1536]{2,1,0:T(8,128)(2,1)} %reduce-scatter.17.cloned.1.call-done, ...), kind=kLoop, calls=%fused_computation.119 | loop fusion | flops 734208 | bytes 620928 | tf_op jit(solution)/shard_map/reduce_sum | solution.py:89
  111.3 0.7 copy-done.6
  112.0 8.1 %all_gather.15 = bf16[1,96,1536]{2,1,0:T(8,128)(2,1)S(1)} all-gather(bf16[1,24,1536]{2,1,0:T(8,128)(2,1)S(1)} %convert_element_type.190), channel_id=1, replica_groups=mesh['dp'=2,'tp'=4] {'tp'}, dimensions={1}, use_global_device_ids=true | all-gather | bytes 368640 | tf_op jit(solution)/shard_map/all_gather | solution.py:33
  120.1 0.7 copy-done.4
  120.8 2.4 %convolution_convert_fusion.10 = bf16[96,384]{1,0:T(8,128)(2,1)} fusion(bf16[384,1536]{1,0:T(8,128)(2,1)} %param.20, bf16[1,96,1536]{2,1,0:T(8,128)(2,1)S(1)} %all_gather.15), kind=kOutput, calls=%fused_computation.32 | convolution fusion | flops 113283072 | bytes 1548288 | tf_op jit(solution)/shard_map/bsd,cd->bsc/dot_general | solution.py:92
  123.2 1.6 reshape.419
  124.8 1.2 multiply_reduce_fusion
  126.1 1.0 multiply_convert_fusion.1
  127.0 1.8 fusion.18
  128.8 1.7 fusion.17
  130.5 1.9 %fusion.16 = bf16[1,96,4,1,96]{4,1,2,3,0:T(8,128)(2,1)} fusion(bf16[96,4,96]{2,1,0:T(4,128)(2,1)} %reshape.419, f32[4,96]{1,0:T(4,128)} %get-tuple-element.32, f32[4,96,96]{1,2,0:T(8,128)} %copy-done.15), kind=kOutput, calls=%fused_computation.33 | convolution fusion | flops 7225823 | bytes 296448 | tf_op jit(solution)/shard_map/bhij,bihe->bjhe/dot_general | solution.py:95
  132.4 1.8 fusion.52
  134.2 1.8 %copy.44 = bf16[96,4,3,96]{0,3,2,1:T(8,128)(2,1)} copy(bf16[96,4,3,96]{3,0,1,2:T(8,128)(2,1)} %fusion.52) | data formatting | bytes 442368 | tf_op jit(solution)/shard_map/reshape.80
  136.0 2.4 %fusion.4 = bf16[1,96,1536]{2,1,0:T(8,128)(2,1)} fusion(bf16[96,4,3,96]{0,3,2,1:T(8,128)(2,1)} %copy.44, bf16[1536,4,3,96]{0,3,2,1:T(8,128)(2,1)S(1)} %copy-done), kind=kOutput, calls=%fused_computation.13 | convolution fusion | flops 339886080 | bytes 4055040 | tf_op jit(solution)/shard_map/bshte,dhte->bsd/dot_general | solution.py:103
  138.5 2.1 %fusion.32 = f32[1536,1152]{0,1:S(1)} fusion(bf16[96,1152]{0,1:T(8,128)(2,1)} %bitcast.118, bf16[1,96,1536]{2,1,0:T(8,128)(2,1)} %all_gather.12), kind=kOutput, calls=%fused_computation.54 | convolution fusion | flops 339738624 | bytes 7593984
  140.6 2.3 %convert_element_type.208 = bf16[1536,4,3,96]{0,3,2,1:T(8,128)(2,1)} convert(f32[1536,4,3,96]{0,3,2,1:T(8,128)S(1)} %bitcast.113) | non-fusion elementwise | flops 1769472 | bytes 10616832 | tf_op jit(solution)/shard_map/convert_element_type | solution.py:102
  142.9 0.7 convert_reduce_fusion
  143.6 1.5 convolution_convert_fusion.2
  145.1 9.3 %reduce-scatter.23.cloned.1.call-done = bf16[1,24,1536]{2,1,0:T(8,128)(2,1)} async-done(((bf16[1,96,1536]{2,1,0:T(8,128)(2,1)}), bf16[1,24,1536]{2,1,0:T(8,128)(2,1)}) %reduce-scatter.23.cloned.1.call-update) | async-done | bytes 73744
  154.3 1.6 convert_reduce_fusion.1
  156.0 0.7 multiply_multiply_fusion.2
  156.6 0.6 copy-done.24
  157.2 1.7 fusion.49
  158.9 0.6 negate_multiply_fusion
  159.5 11.7 %all-reduce.4 = (f32[1536]{0:T(1024)}, f32[1536]{0:T(1024)}, f32[1536]{0:T(1024)}, f32[1536]{0:T(1024)}, f32[1536]{0:T(1024)}, /*index=5*/f32[1536]{0:T(1024)}) all-reduce(f32[1536]{0:T(1024)} %get-tuple-element.16, f32[1536]{0:T(1024)} %get-tuple-element.20, f32[1536]{0:T(1024)S(1)} %copy-done.18, ...), channel_id=1, replica_groups=mesh['dp'=2,'tp'=4] {'tp'}, use_global_device_ids=true, to_apply=%region_16.17 | all-reduce | flops 9216 | bytes 73728 | tf_op jit(solution)/shard_map/psum | solution.py:106
  171.1 1.7 add_convert_fusion
  (68 shorter events, 0.4 us)
Async XLA Ops:
  7.2 18.6 %copy-start = (bf16[1536,4,3,96]{0,3,2,1:T(8,128)(2,1)S(1)}, bf16[1536,4,3,96]{0,3,2,1:T(8,128)(2,1)}, u32[]{:S(2)}) copy-start(bf16[1536,4,3,96]{0,3,2,1:T(8,128)(2,1)} %param.18) | copy-start | bytes 10616836
  7.2 43.9 %copy-start.14 = (f32[1536]{0:T(1024)S(1)}, f32[1536]{0:T(1024)}, u32[]{:S(2)}) copy-start(f32[1536]{0:T(1024)} %param.21) | copy-start | bytes 18436
  7.2 46.1 %copy-start.16 = (f32[1536]{0:T(1024)S(1)}, f32[1536]{0:T(1024)}, u32[]{:S(2)}) copy-start(f32[1536]{0:T(1024)} %param.22) | copy-start | bytes 18436
  7.2 43.8 %reduce-scatter.17.cloned.1.call-start = ((), (), s32[]{:S(2)}) async-start(), calls=%async_computation.4 | async-start | bytes 368640
  9.4 13.6 %copy-start.20 = (f32[24]{0:T(128)}, f32[24]{0:T(128)S(1)}, u32[]{:S(2)}) copy-start(f32[24]{0:T(128)S(1)} %broadcast_multiply_fusion.2) | copy-start | bytes 292
  10.5 0.6 copy-start.25
  11.1 12.0 %copy-start.22 = (f32[24]{0:T(128)}, f32[24]{0:T(128)S(1)}, u32[]{:S(2)}) copy-start(f32[24]{0:T(128)S(1)} %fusion.60) | copy-start | bytes 292
  28.1 0.7 copy-start.11
  29.8 0.7 copy-start.15
  36.1 55.1 %reduce-scatter.21.cloned.1.call-start = ((), (), s32[]{:S(2)}) async-start(), calls=%async_computation.6 | async-start | bytes 368640
  51.0 15.3 %copy-start.7 = (bf16[1,96,1536]{2,1,0:T(8,128)(2,1)S(1)}, bf16[1,96,1536]{2,1,0:T(8,128)(2,1)}, u32[]{:S(2)}) copy-start(bf16[1,96,1536]{2,1,0:T(8,128)(2,1)} %all_gather.14) | copy-start | bytes 884740
  52.2 10.1 %copy-start.19 = (f32[24]{0:T(128)}, f32[24]{0:T(128)S(1)}, u32[]{:S(2)}) copy-start(f32[24]{0:T(128)S(1)} %broadcast_multiply_fusion.1) | copy-start | bytes 292
  53.3 9.0 %copy-start.26 = (f32[24]{0:T(128)}, f32[24]{0:T(128)S(1)}, u32[]{:S(2)}) copy-start(f32[24]{0:T(128)S(1)} %multiply_reduce_fusion.1) | copy-start | bytes 292
  53.3 9.0 %copy-start.21 = (f32[24]{0:T(128)}, f32[24]{0:T(128)S(1)}, u32[]{:S(2)}) copy-start(f32[24]{0:T(128)S(1)} %fusion.61) | copy-start | bytes 292
  62.3 0.7 copy-start.3
  63.0 7.1 %slice-start.2 = ((s8[4718592]{0:T(1024)(128)(4,1)}), s8[4194304]{0:T(1024)(128)(4,1)S(1)}, s32[]{:S(2)}) async-start(s8[4718592]{0:T(1024)(128)(4,1)} %bitcast.116), calls=%async_computation.10 | async-start | bytes 8388608
  63.0 10.0 %slice-start = ((s8[4718592]{0:T(1024)(128)(4,1)}), s8[4194304]{0:T(1024)(128)(4,1)S(1)}, s32[]{:S(2)}) async-start(s8[4718592]{0:T(1024)(128)(4,1)} %bitcast.114), calls=%async_computation.8 | async-start | bytes 8388608
  66.4 3.7 %copy-start.1 = (f32[96,1536]{1,0:T(8,128)}, f32[96,1536]{1,0:T(8,128)S(1)}, u32[]{:S(2)}) copy-start(f32[96,1536]{1,0:T(8,128)S(1)} %convolution_add_fusion) | copy-start | bytes 1769476
  66.4 3.7 %slice-start.3 = ((s8[4718592]{0:T(1024)(128)(4,1)}), s8[524288]{0:T(1024)(128)(4,1)S(1)}, s32[]{:S(2)}) async-start(s8[4718592]{0:T(1024)(128)(4,1)} %bitcast.116), calls=%async_computation.11 | async-start | bytes 1048576
  66.4 6.6 %slice-start.1 = ((s8[4718592]{0:T(1024)(128)(4,1)}), s8[524288]{0:T(1024)(128)(4,1)S(1)}, s32[]{:S(2)}) async-start(s8[4718592]{0:T(1024)(128)(4,1)} %bitcast.114), calls=%async_computation.9 | async-start | bytes 1048576
  72.3 0.7 copy-start.8
  75.3 33.6 %reduce-scatter.19.cloned.1.call-start = ((), (), s32[]{:S(2)}) async-start(), calls=%async_computation.5 | async-start | bytes 368640
  75.4 4.7 %copy-start.2 = (f32[96,1536]{1,0:T(8,128)S(1)}, f32[96,1536]{1,0:T(8,128)}, u32[]{:S(2)}) copy-start(f32[96,1536]{1,0:T(8,128)} %copy-done.1) | copy-start | bytes 1769476
  84.1 70.2 %reduce-scatter.23.cloned.1.call-start = ((), (), s32[]{:S(2)}) async-start(), calls=%async_computation.7 | async-start | bytes 368640
  93.5 0.5 copy-start.23
  111.3 0.7 copy-start.6
  120.1 0.7 copy-start.4
  140.6 2.3 %copy-start.9 = (bf16[1,96,4,1,96]{4,1,2,3,0:T(8,128)(2,1)S(1)}, bf16[1,96,4,1,96]{4,1,2,3,0:T(8,128)(2,1)}, u32[]{:S(2)}) copy-start(bf16[1,96,4,1,96]{4,1,2,3,0:T(8,128)(2,1)} %fusion.18) | copy-start | bytes 221188
  140.6 2.3 %copy-start.10 = (bf16[1,96,4,1,96]{4,1,2,3,0:T(8,128)(2,1)S(1)}, bf16[1,96,4,1,96]{4,1,2,3,0:T(8,128)(2,1)}, u32[]{:S(2)}) copy-start(bf16[1,96,4,1,96]{4,1,2,3,0:T(8,128)(2,1)} %fusion.17) | copy-start | bytes 221188
  140.6 2.3 %copy-start.13 = (bf16[1,96,4,1,96]{4,1,2,3,0:T(8,128)(2,1)S(1)}, bf16[1,96,4,1,96]{4,1,2,3,0:T(8,128)(2,1)}, u32[]{:S(2)}) copy-start(bf16[1,96,4,1,96]{4,1,2,3,0:T(8,128)(2,1)} %fusion.16) | copy-start | bytes 221188
  140.6 3.0 %copy-start.5 = (bf16[1,96,1536]{2,1,0:T(8,128)(2,1)S(1)}, bf16[1,96,1536]{2,1,0:T(8,128)(2,1)}, u32[]{:S(2)}) copy-start(bf16[1,96,1536]{2,1,0:T(8,128)(2,1)} %copy-done.4) | copy-start | bytes 884740
  140.6 3.0 %copy-start.12 = (bf16[4,96,96]{2,1,0:T(8,128)(2,1)S(1)}, bf16[4,96,96]{2,1,0:T(8,128)(2,1)}, u32[]{:S(2)}) copy-start(bf16[4,96,96]{2,1,0:T(8,128)(2,1)} %convolution_convert_fusion.9) | copy-start | bytes 221188
  140.6 13.7 %copy-start.17 = (f32[1536]{0:T(1024)S(1)}, f32[1536]{0:T(1024)}, u32[]{:S(2)}) copy-start(f32[1536]{0:T(1024)} %param.16) | copy-start | bytes 18436
  140.6 18.8 %copy-start.18 = (f32[1536]{0:T(1024)S(1)}, f32[1536]{0:T(1024)}, u32[]{:S(2)}) copy-start(f32[1536]{0:T(1024)} %get-tuple-element.28) | copy-start | bytes 18436
  156.6 0.6 copy-start.24
Sparse Core Ops, SparseCore 0:
  36.3 14.7 reduce-scatter.16
  75.4 15.7 reduce-scatter.20
  94.3 14.5 reduce-scatter.18
  138.6 15.7 reduce-scatter.22
where the time goes:
time: 181 us; the launch traced here: 179 us
  blocking collectives  47.8 us (26%)
  matrix products  42.8 us (24%)
  waiting for transfers between devices  34.8 us (19%)
  other arithmetic  28.4 us (16%)
  between operations  14.1 us (8%)
  local copies, waits for them, and re-layouts  11.4 us (6%)
    all_gather x4, blocking collectives, seq_gather(): return lax.all_gather(values, 'tp', axis=1, tiled=True)  36.1 us
    unnamed x8, waiting for transfers between devices  34.8 us
    psum x1, blocking collectives, local_step(): grad_ln1_gamma = lax.psum(grad_ln1_gamma, 'tp')  11.7 us
    unnamed x63, local copies, waits for them, and re-layouts  7.23 us
    reduce_sum x4, other arithmetic, layer_norm(): return centered * lax.rsqrt(variance + EPS) * ln_gain + ln_bias  6.64 us
    dot_general x1, matrix products, local_step(): jnp.einsum('bsd,bsf->df', g_full, grad_pre_bf, preferred_element_type=jnp...  4.71 us
    dot_general x1, matrix products, local_step(): jnp.einsum('bsf,fd->bsd', activated, w_down, preferred_element_type=jnp.f...  3.99 us
    dot_general x1, matrix products, local_step(): jnp.einsum('bsf,bsd->fd', activated, grad_m_full, preferred_element_type=...  3.63 us
  transfers between devices with their start and end apart: 4, of which 4 were waited for; matrix products, arithmetic and copies ran while one was open for 11% of the time, Pallas kernels for 0%

commit v1 on v0

v1 whole, which is shorter than its diff:
```python
import functools
import math

import jax
import jax.numpy as jnp
from jax import lax
from jax.experimental import pallas as pl
from jax.experimental.pallas import tpu as pltpu
from jax.sharding import PartitionSpec as P

EPS = 1e-5
MASK_VALUE = -1e30
BF = jnp.bfloat16
F32 = jnp.float32
MESH = pl.DeviceIdType.MESH

D = 1536
S = 96
SL = 24
TP = 4
HL = 4
HD = 96
FL = 1536
CW = 256
NCH = D // CW
HCH = NCH // 2


def alibi_slopes(n_heads):
    closest = 2 ** int(math.floor(math.log2(n_heads)))
    base_ratio = 2.0 ** (-8.0 / closest)
    extra_ratio = 2.0 ** (-4.0 / closest)
    remaining = min(closest, n_heads - closest)
    slopes = [base_ratio ** (i + 1) for i in range(closest)]
    return slopes + [extra_ratio ** (2 * i + 1) for i in range(remaining)]


def dot(a, b, ca, cb):
    return lax.dot_general(a, b, (((ca,), (cb,)), ((), ())), preferred_element_type=F32)


def gelu_parts(u):
    k = math.sqrt(2.0 / math.pi)
    u2 = u * u
    th = jnp.tanh(k * (u + 0.044715 * (u2 * u)))
    half = 0.5 * (1.0 + th)
    dk = k * (1.0 + 3.0 * 0.044715 * u2)
    return u * half, half + 0.5 * u * (1.0 - th * th) * dk


def rows_stats(v):
    mean = jnp.mean(v, axis=-1, keepdims=True)
    cen = v - mean
    var = jnp.mean(cen * cen, axis=-1, keepdims=True)
    return cen, lax.rsqrt(var + EPS)


def block_kernel(x_ref, gy_ref, g1_ref, be1_ref, g2_ref, be2_ref, bo_ref, bd_ref, bqkv_ref, bup_ref,
                 wqkv_hbm, wout_hbm, wup_hbm, wdn_hbm,
                 y_ref, gx_ref, vec_ref, gbqkv_ref, h_ref, gqkv_ref, ctx_ref, gmid_ref, g_ref, gpre_ref, act_ref, gyf_ref,
                 wqkv, wout, wup, wdn, xg, gyg, xf, xhat, rstd_s, biasT, qkvT, probs,
                 a_ps, a_pr, a_hs, a_hr, a_cr, a_fr, b_ps, b_pr, b_hs, b_hr, b_cr, b_fr,
                 gact, ghp, m_pr, m_hs, m_cr, r_pr, r_hs, r_cr, gm_f, ln_x, gg_f,
                 wsem, ssem, rsem):
    t = lax.axis_index('tp')
    core = t % 2
    pt = t + 1 - 2 * core
    ct = (t + 2) % TP
    qt = (pt + 2) % TP

    started = []
    counter = [0]

    def send(src, dst, dev):
        i = counter[0]
        counter[0] += 1
        c = pltpu.make_async_remote_copy(src_ref=src, dst_ref=dst, send_sem=ssem.at[i], recv_sem=rsem.at[i],
                                         device_id={'tp': dev}, device_id_type=MESH)
        c.start()
        started.append(c)
        return c

    w_cps = {}
    w_cps['qkv'] = [pltpu.make_async_copy(wqkv_hbm, wqkv, wsem.at[0])]
    w_cps['out'] = [pltpu.make_async_copy(wout_hbm.at[:, pl.ds(k * CW, CW)], wout.at[k], wsem.at[1 + k]) for k in range(NCH)]
    w_cps['dn'] = [pltpu.make_async_copy(wdn_hbm, wdn, wsem.at[7])]
    w_cps['up'] = [pltpu.make_async_copy(wup_hbm, wup, wsem.at[8])]

    barrier = pltpu.get_barrier_semaphore()
    for dev in (pt, ct):
        pl.semaphore_signal(barrier, inc=1, device_id={'tp': dev}, device_id_type=MESH)
    for name in ('qkv', 'out', 'dn', 'up'):
        for c in w_cps[name]:
            c.start()
    pl.semaphore_wait(barrier, 2)

    x_c = send(x_ref, xg.at[t], ct)
    x_p = send(x_ref, xg.at[t], pt)
    y_c = send(gy_ref, gyg.at[t], ct)
    y_p = send(gy_ref, gyg.at[t], pt)
    xg[t] = x_ref[...]
    gyg[t] = gy_ref[...]

    for h in range(HL):
        for e in range(3):
            row = jnp.broadcast_to(bqkv_ref[e, h:h + 1, :], (S, HD))
            biasT[pl.ds((h * 3 + e) * HD, HD), :] = row.T

    x_c.wait_recv()
    x_f = send(xg.at[ct], xg.at[ct], pt)
    x_p.wait_recv()
    x_f.wait_recv()

    for i in range(TP):
        xf[pl.ds(i * SL, SL), :] = xg[i].astype(F32)
    for r in range(0, S, 32):
        cen, rstd = rows_stats(xf[r:r + 32, :])
        xh = cen * rstd
        xhat[r:r + 32, :] = xh
        rstd_s[r:r + 32, :] = jnp.broadcast_to(rstd, (32, 128))
        h_ref[r:r + 32, :] = (xh * g1_ref[...] + be1_ref[...]).astype(BF)

    y_c.wait_recv()
    y_f = send(gyg.at[ct], gyg.at[ct], pt)

    w_cps['qkv'][0].wait()
    hv = h_ref[...]
    for h in range(HL):
        rows = slice(h * 3 * HD, (h + 1) * 3 * HD)
        qkvT[rows, :] = (dot(wqkv[rows, :], hv, 1, 1) + biasT[rows, :]).astype(BF)

    scale = HD ** -0.5
    slopes = alibi_slopes(HL * TP)
    j_pos = lax.broadcasted_iota(jnp.int32, (S, S), 0)
    i_pos = lax.broadcasted_iota(jnp.int32, (S, S), 1)
    causal = j_pos <= i_pos
    j_f = j_pos.astype(F32)

    def head(h, e):
        return qkvT[(h * 3 + e) * HD:(h * 3 + e + 1) * HD, :]

    for h in range(HL):
        slope = jnp.where(t == 0, slopes[h], jnp.where(t == 1, slopes[HL + h], jnp.where(t == 2, slopes[2 * HL + h], slopes[3 * HL + h]))).astype(F32)
        s = dot(head(h, 1), head(h, 0), 0, 0) * scale + slope * j_f
        s = jnp.where(causal, s, MASK_VALUE)
        p = jnp.exp(s - jnp.max(s, axis=0, keepdims=True))
        p = p / jnp.sum(p, axis=0, keepdims=True)
        probs[h] = p
        ctx_ref[h * HD:(h + 1) * HD, :] = dot(head(h, 2), p.astype(BF), 1, 0).astype(BF)

    def exchange(part, ps, pr, hs, hr, cr):
        firsts = []
        for k in range(HCH):
            ps[k] = part((1 - core) * HCH + k).astype(BF)
            firsts.append(send(ps.at[k], pr.at[k], pt))
        outs = []
        for k in range(HCH):
            own = part(core * HCH + k)
            firsts[k].wait_recv()
            hs[k] = (own + pr[k].astype(F32)).astype(BF)
            outs.append((send(hs.at[k], cr.at[k], ct), send(hs.at[k], hr.at[k], pt)))
        return outs

    def forward(outs, cr, fr):
        fwd = []
        for k in range(HCH):
            outs[k][0].wait_recv()
            fwd.append(send(cr.at[k], fr.at[k], pt))
        return fwd

    for c in w_cps['out']:
        c.wait()
    ctxT = ctx_ref[...]
    a_outs = exchange(lambda kk: dot(ctxT, wout[kk], 0, 0), a_ps, a_pr, a_hs, a_hr, a_cr)

    y_p.wait_recv()
    y_f.wait_recv()
    for i in range(TP):
        gm_f[pl.ds(i * SL, SL), :] = gyg[i].astype(F32)
    for r in range(0, S, 32):
        gyf_ref[r:r + 32, :] = gm_f[r:r + 32, :].astype(BF)
    w_cps['dn'][0].wait()
    gyv = gyf_ref[...]
    for n in range(NCH):
        gact[:, n * CW:(n + 1) * CW] = dot(gyv, wdn[n * CW:(n + 1) * CW, :], 1, 1).astype(BF)
    vec_ref[0:1, :] = jnp.sum(gm_f[...], axis=0, keepdims=True)

    def gathered(outs, fwd, hs, hr, cr, fr, put):
        for k in range(HCH):
            put(core * HCH + k, (hs[k].astype(F32) + cr[k].astype(F32)).astype(BF).astype(F32))
        for k in range(HCH):
            outs[k][1].wait_recv()
            fwd[k].wait_recv()
            put((1 - core) * HCH + k, (hr[k].astype(F32) + fr[k].astype(F32)).astype(BF).astype(F32))

    a_fwd = forward(a_outs, a_cr, a_fr)

    def put_x(kk, val):
        cols = pl.ds(pl.multiple_of(kk * CW, CW), CW)
        xf[:, cols] = xf[:, cols] + val + bo_ref[:, cols]

    gathered(a_outs, a_fwd, a_hs, a_hr, a_cr, a_fr, put_x)

    for r in range(0, S, 32):
        cen, rstd = rows_stats(xf[r:r + 32, :])
        g_ref[r:r + 32, :] = (cen * rstd * g2_ref[...] + be2_ref[...]).astype(BF)

    w_cps['up'][0].wait()
    gv = g_ref[...]
    for n in range(NCH):
        cols = slice(n * CW, (n + 1) * CW)
        pre = dot(gv, wup[:, cols], 1, 0) + bup_ref[:, cols]
        val, der = gelu_parts(pre)
        act_ref[:, cols] = val.astype(BF)
        gp = gact[:, cols].astype(F32) * der
        vec_ref[1:2, cols] = jnp.sum(gp, axis=0, keepdims=True)
        gpre_ref[:, cols] = gp.astype(BF)

    gprev = gpre_ref[...]

    def part_g(kk):
        return dot(gprev, wup[pl.ds(pl.multiple_of(kk * CW, CW), CW), :], 1, 1)

    g_outs = exchange(part_g, b_ps, b_pr, b_hs, b_hr, b_cr)

    def scatter_first(part, buf, pr, extra=None):
        for n in range(NCH):
            cols = slice(n * CW, (n + 1) * CW)
            v = part(n)
            for i in range(TP):
                buf[i, :, cols] = v[i * SL:(i + 1) * SL, :].astype(BF)
            if extra is not None:
                extra(n, v)
        return (send(buf.at[qt], pr.at[1], pt), send(buf.at[pt], pr.at[0], pt))

    actv = act_ref[...]
    m_first = scatter_first(lambda n: dot(actv, wdn[:, n * CW:(n + 1) * CW], 1, 0), ghp.at[0], m_pr)

    g_fwd = forward(g_outs, b_cr, b_fr)

    m_first[0].wait_recv()
    m_hs[...] = (ghp[0, ct].astype(F32) + m_pr[1].astype(F32)).astype(BF)
    m_out = send(m_hs, m_cr, ct)

    def put_g(kk, val):
        gg_f[:, pl.ds(pl.multiple_of(kk * CW, CW), CW)] = val

    gathered(g_outs, g_fwd, b_hs, b_hr, b_cr, b_fr, put_g)

    gg2 = jnp.zeros((1, D), F32)
    gb2 = jnp.zeros((1, D), F32)
    gbo = jnp.zeros((1, D), F32)
    for r in range(0, S, 32):
        cen, rstd = rows_stats(xf[r:r + 32, :])
        xh = cen * rstd
        gg = gg_f[r:r + 32, :]
        gg2 = gg2 + jnp.sum(gg * xh, axis=0, keepdims=True)
        gb2 = gb2 + jnp.sum(gg, axis=0, keepdims=True)
        dxh = gg * g2_ref[...]
        m1 = jnp.mean(dxh, axis=-1, keepdims=True)
        m2 = jnp.mean(dxh * xh, axis=-1, keepdims=True)
        gm = gm_f[r:r + 32, :] + rstd * (dxh - m1 - xh * m2)
        gm_f[r:r + 32, :] = gm
        gbo = gbo + jnp.sum(gm, axis=0, keepdims=True)
        gmid_ref[r:r + 32, :] = gm.astype(BF)
    vec_ref[2:3, :] = gg2
    vec_ref[3:4, :] = gb2
    vec_ref[4:5, :] = gbo

    gmv = gmid_ref[...]
    gctxT = dot(wout[0], gmv[:, :CW], 1, 1)
    for k in range(1, NCH):
        gctxT = gctxT + dot(wout[k], gmv[:, k * CW:(k + 1) * CW], 1, 1)
    gctxT = gctxT.astype(BF)
    ones = jnp.ones((8, S), BF)
    for h in range(HL):
        go = gctxT[h * HD:(h + 1) * HD, :]
        p = probs[h]
        gp = dot(head(h, 2), go, 0, 0).astype(BF).astype(F32)
        gv_ = dot(go, p.astype(BF), 1, 1).astype(BF)
        gs = (p * (gp - jnp.sum(gp * p, axis=0, keepdims=True))).astype(BF)
        gq = (dot(head(h, 1), gs, 1, 0) * scale).astype(BF)
        gk = (dot(head(h, 0), gs, 1, 1) * scale).astype(BF)
        for e, val in enumerate((gq, gk, gv_)):
            gqkv_ref[(h * 3 + e) * HD:(h * 3 + e + 1) * HD, :] = val
            gbqkv_ref[e, h:h + 1, :] = dot(ones, val, 1, 1)[0:1, :]

    gqv = gqkv_ref[...]

    def ln1_sums(n, v):
        cols = slice(n * CW, (n + 1) * CW)
        v = v.astype(BF).astype(F32)
        ln_s[0:1, cols] = jnp.sum(v * xhat[:, cols], axis=0, keepdims=True)
        ln_s[1:2, cols] = jnp.sum(v, axis=0, keepdims=True)

    ln_s, ln_pr, ln_hs, ln_cr = ln_x.at[0], ln_x.at[1], ln_x.at[2], ln_x.at[3]
    r_first = scatter_first(lambda n: dot(gqv, wqkv[:, n * CW:(n + 1) * CW], 0, 0), ghp.at[1], r_pr, ln1_sums)
    l_first = send(ln_s, ln_pr, pt)

    r_first[0].wait_recv()
    r_hs[...] = (ghp[1, ct].astype(F32) + r_pr[1].astype(F32)).astype(BF)
    r_out = send(r_hs, r_cr, ct)
    l_first.wait_recv()
    ln_hs[...] = ln_s[...] + ln_pr[...]
    l_out = send(ln_hs, ln_cr, ct)

    own = pl.ds(pl.multiple_of(t * SL, 8), SL)
    m_first[1].wait_recv()
    m_out.wait_recv()
    m_sum = (ghp[0, t].astype(F32) + m_pr[0].astype(F32)).astype(BF).astype(F32) + m_cr[...].astype(F32)
    y_ref[...] = (xf[own, :] + m_sum.astype(BF).astype(F32) + bd_ref[...]).astype(BF)

    r_first[1].wait_recv()
    mine = (ghp[1, t].astype(F32) + r_pr[0].astype(F32)).astype(BF).astype(F32)
    r_out.wait_recv()
    gh = (mine + r_cr[...].astype(F32)).astype(BF).astype(F32)
    xh = xhat[own, :]
    dxh = gh * g1_ref[...]
    m1 = jnp.mean(dxh, axis=-1, keepdims=True)
    m2 = jnp.mean(dxh * xh, axis=-1, keepdims=True)
    gx_ref[...] = (gm_f[own, :] + rstd_s[own, 0:1] * (dxh - m1 - xh * m2)).astype(BF)
    l_out.wait_recv()
    vec_ref[6:8, :] = ln_hs[...] + ln_cr[...]
    for c in started:
        c.wait_send()


N_SEND = 38


def grads_kernel(h_ref, gqkv_ref, ctx_ref, gmid_ref, g_ref, gpre_ref, act_ref, gyf_ref, yi_ref, gxi_ref, vec_ref, gbi_ref,
                 y_ref, gx_ref, gl1_ref, bl1_ref, gwqkv_ref, gbqkv_ref, gwout_ref, gbo_ref, gl2_ref, bl2_ref,
                 gwup_ref, gbup_ref, gwdn_ref, gbd_ref, s_qkv, s_out, s_up, s_dn, sem):
    cps = []

    def out(src, dst):
        c = pltpu.make_async_copy(src, dst, sem.at[len(cps)])
        c.start()
        cps.append(c)

    y_ref[...] = yi_ref[...]
    gx_ref[...] = gxi_ref[...]
    gbqkv_ref[...] = gbi_ref[...]
    for i, r in enumerate((gbd_ref, gbup_ref, gl2_ref, bl2_ref, gbo_ref, None, gl1_ref, bl1_ref)):
        if r is not None:
            r[...] = vec_ref[i, :]

    gyv = gyf_ref[...]
    gpv = gpre_ref[...]
    for n in range(NCH):
        rows = pl.ds(n * CW, CW)
        s_dn[rows, :] = dot(act_ref[:, n * CW:(n + 1) * CW], gyv, 0, 0).astype(BF)
        out(s_dn.at[rows], gwdn_ref.at[rows])
    for n in range(NCH):
        rows = pl.ds(n * CW, CW)
        s_up[rows, :] = dot(g_ref[:, n * CW:(n + 1) * CW], gpv, 0, 0).astype(BF)
        out(s_up.at[rows], gwup_ref.at[rows])
    hv = h_ref[...]
    for n in range(HL):
        rows = pl.ds(n * 3 * HD, 3 * HD)
        s_qkv[rows, :] = dot(gqkv_ref[n * 3 * HD:(n + 1) * 3 * HD, :], hv, 1, 0).astype(BF)
        out(s_qkv.at[rows], gwqkv_ref.at[rows])
    s_out[...] = dot(ctx_ref[...], gmid_ref[...], 1, 0).astype(BF)
    out(s_out, gwout_ref)
    for c in cps:
        c.wait()


def solution(mesh):
    VM = pl.BlockSpec(memory_space=pltpu.VMEM)
    ANY = pl.BlockSpec(memory_space=pl.ANY)

    def sds(shape, dt):
        return jax.ShapeDtypeStruct(shape, dt)

    def local_step(x, g1, be1, w_qkv, b_qkv, w_out, b_out, g2, be2, w_up, b_up, w_down, b_down, grad_y):
        wq = jnp.transpose(w_qkv, (1, 2, 3, 0)).reshape(3 * HL * HD, D)
        bq = jnp.transpose(b_qkv, (1, 0, 2))
        row = lambda v: v.reshape(1, -1)
        half = pltpu.VMEM((HCH, S, CW), BF)
        mids = pl.pallas_call(
            block_kernel,
            out_shape=(sds((SL, D), BF), sds((SL, D), BF), sds((8, D), F32), sds((3, HL, HD), F32), sds((S, D), BF),
                       sds((3 * HL * HD, S), BF), sds((HL * HD, S), BF), sds((S, D), BF), sds((S, D), BF), sds((S, FL), BF),
                       sds((S, FL), BF), sds((S, D), BF)),
            in_specs=[VM] * 10 + [ANY] * 4,
            out_specs=(VM,) * 12,
            scratch_shapes=[
                pltpu.VMEM((3 * HL * HD, D), BF), pltpu.VMEM((NCH, HL * HD, CW), BF), pltpu.VMEM((D, FL), BF), pltpu.VMEM((FL, D), BF),
                pltpu.VMEM((TP, SL, D), BF), pltpu.VMEM((TP, SL, D), BF), pltpu.VMEM((S, D), F32), pltpu.VMEM((S, D), F32),
                pltpu.VMEM((S, 128), F32), pltpu.VMEM((3 * HL * HD, S), F32), pltpu.VMEM((3 * HL * HD, S), BF), pltpu.VMEM((HL, S, S), F32),
                half, half, half, half, half, half, half, half, half, half, half, half,
                pltpu.VMEM((S, FL), BF), pltpu.VMEM((2, TP, SL, D), BF),
                pltpu.VMEM((2, SL, D), BF), pltpu.VMEM((SL, D), BF), pltpu.VMEM((SL, D), BF),
                pltpu.VMEM((2, SL, D), BF), pltpu.VMEM((SL, D), BF), pltpu.VMEM((SL, D), BF),
                pltpu.VMEM((S, D), F32), pltpu.VMEM((4, 2, D), F32), pltpu.VMEM((S, D), F32),
                pltpu.SemaphoreType.DMA((9,)), pltpu.SemaphoreType.DMA((N_SEND,)), pltpu.SemaphoreType.DMA((N_SEND,)),
            ],
            compiler_params=pltpu.CompilerParams(collective_id=0, has_side_effects=True),
            name='block',
        )(x.reshape(SL, D), grad_y.reshape(SL, D), row(g1), row(be1), row(g2), row(be2), row(b_out), row(b_down), bq, row(b_up),
          wq, w_out, w_up, w_down)
        y, gx, vec, gb, h, gqkv, ctx, gmid, g, gpre, act, gyf = mids
        vec1 = sds((D,), F32)
        outs = pl.pallas_call(
            grads_kernel,
            out_shape=(sds((SL, D), BF), sds((SL, D), BF), vec1, vec1, sds((3 * HL * HD, D), BF), sds((3, HL, HD), F32),
                       sds((HL * HD, D), BF), vec1, vec1, vec1, sds((D, FL), BF), vec1, sds((FL, D), BF), vec1),
            in_specs=[VM] * 12,
            out_specs=(VM, VM, VM, VM, ANY, VM, ANY, VM, VM, VM, ANY, VM, ANY, VM),
            scratch_shapes=[pltpu.VMEM((3 * HL * HD, D), BF), pltpu.VMEM((HL * HD, D), BF), pltpu.VMEM((D, FL), BF), pltpu.VMEM((FL, D), BF),
                            pltpu.SemaphoreType.DMA((32,))],
            name='grads',
        )(h, gqkv, ctx, gmid, g, gpre, act, gyf, y, gx, vec, gb)
        (y, gx, gl1, bl1, gwqkv, gbqkv, gwout, gbo, gl2, bl2, gwup, gbup, gwdn, gbd) = outs
        gwqkv = jnp.transpose(gwqkv.reshape(HL, 3, HD, D), (3, 0, 1, 2))
        gbqkv = jnp.transpose(gbqkv, (1, 0, 2))
        return (y.reshape(1, SL, D), gx.reshape(1, SL, D), gl1, bl1, gwqkv, gbqkv, gwout, gbo, gl2, bl2, gwup, gbup, gwdn, gbd)

    row_spec = P('dp', 'tp', None)
    in_specs = (row_spec, P(), P(), P(None, 'tp', None, None), P('tp', None, None), P('tp', None), P(), P(), P(),
                P(None, 'tp'), P('tp'), P('tp', None), P(), row_spec)
    out_specs = (row_spec, row_spec, P('dp'), P('dp'), P('dp', 'tp', None, None), P(('dp', 'tp'), None, None),
                 P(('dp', 'tp'), None), P('dp'), P('dp'), P('dp'), P('dp', 'tp'), P(('dp', 'tp')), P(('dp', 'tp'), None), P('dp'))
    return jax.shard_map(local_step, mesh=mesh, in_specs=in_specs, out_specs=out_specs, check_vma=False)
```

time: 181 us -> 56.2 us (0.31)
  blocking collectives: 47.8 us -> 0 us
  Pallas kernels: 0 us -> 46 us
  matrix products: 42.8 us -> 0 us
  waiting for transfers between devices: 34.8 us -> 0 us
  other arithmetic: 28.4 us -> 0 us
  between operations: 14.1 us -> 0.66 us
  local copies, waits for them, and re-layouts: 11.4 us -> 9.06 us
    pallas_call x0 -> x2, Pallas kernels: none -> 46 us  [the longest x1 38 us: local_step(): pl.pallas_call(block_kernel, out_shape=(sds((SL, D), BF), sds((SL, D), BF...]
    dot_general x17 -> x0, matrix products: 40.7 us -> none  [the longest x1 4.71 us: local_step(): jnp.einsum('bsd,bsf->df', g_full, grad_pre_bf, preferred_element_type=jnp...]
    all_gather x4 -> x0, blocking collectives: 36.1 us -> none  [seq_gather(): return lax.all_gather(values, 'tp', axis=1, tiled=True)]
    unnamed x8 -> x0, waiting for transfers between devices: 34.8 us -> none
    reduce_sum x10 -> x0, other arithmetic: 14 us -> none  [the longest x4 6.64 us: layer_norm(): return centered * lax.rsqrt(variance + EPS) * ln_gain + ln_bias]
    psum x1 -> x0, blocking collectives: 11.7 us -> none  [local_step(): grad_ln1_gamma = lax.psum(grad_ln1_gamma, 'tp')]
    reshape x0 -> x7, local copies, waits for them, and re-layouts: none -> 9.06 us  [local_step(): row = lambda v: v.reshape(1, -1)]
    convert_element_type x7 -> x0, other arithmetic: 7.53 us -> none  [the longest x1 2.26 us: local_step(): jnp.einsum('bsd,bshte->dhte', h_full, grad_qkv, preferred_element_type=jn...]
  transfers between devices with their start and end apart: 4 -> 0, of which waited for: 4 -> 0; matrix products, arithmetic and copies ran while one was open for 11% -> 0% of each run, Pallas kernels for 0% -> 0%
where the time goes in v1:
time: 56.2 us; the launch traced here: 55.7 us
  Pallas kernels  46 us (82%)
  local copies, waits for them, and re-layouts  9.06 us (16%)
  between operations  0.66 us (1%)
    pallas_call x1, Pallas kernels, local_step(): pl.pallas_call(block_kernel, out_shape=(sds((SL, D), BF), sds((SL, D), BF...  38 us
    reshape x7, local copies, waits for them, and re-layouts, local_step(): row = lambda v: v.reshape(1, -1)  9.06 us
    pallas_call x1, Pallas kernels, local_step(): pl.pallas_call(grads_kernel, out_shape=(sds((SL, D), BF), sds((SL, D), BF...  7.99 us

profile of v1, /device:TPU:0, one launch (start us, length us, event | category | flops | bytes accessed | tf_op | source)
XLA Modules:
  0.0 55.7 jit_solution(8029857002085938594)
XLA Ops:
  0.6 1.3 %reshape.69.g1_ref = f32[1,1536]{1,0:T(1,128)} reshape(f32[1536]{0:T(1024)} %param.15) | data formatting | bytes 12288 | tf_op jit(solution)/shard_map/reshape | solution.py:379
  1.9 1.3 %reshape.70.be1_ref = f32[1,1536]{1,0:T(1,128)} reshape(f32[1536]{0:T(1024)} %param.16) | data formatting | bytes 12288 | tf_op jit(solution)/shard_map/reshape | solution.py:379
  3.2 1.3 %reshape.73.bo_ref = f32[1,1536]{1,0:T(1,128)} reshape(f32[1536]{0:T(1024)} %param.20) | data formatting | bytes 12288 | tf_op jit(solution)/shard_map/reshape | solution.py:379
  4.5 1.3 %reshape.71.g2_ref = f32[1,1536]{1,0:T(1,128)} reshape(f32[1536]{0:T(1024)} %param.21) | data formatting | bytes 12288 | tf_op jit(solution)/shard_map/reshape | solution.py:379
  5.8 1.3 %reshape.72.be2_ref = f32[1,1536]{1,0:T(1,128)} reshape(f32[1536]{0:T(1024)} %param.22) | data formatting | bytes 12288 | tf_op jit(solution)/shard_map/reshape | solution.py:379
  7.1 1.3 %reshape.75.bup_ref = f32[1,1536]{1,0:T(1,128)} reshape(f32[1536]{0:T(1024)} %param.24) | data formatting | bytes 12288 | tf_op jit(solution)/shard_map/reshape | solution.py:379
  8.4 1.3 %reshape.74.bd_ref = f32[1,1536]{1,0:T(1,128)} reshape(f32[1536]{0:T(1024)} %param.26) | data formatting | bytes 12288 | tf_op jit(solution)/shard_map/reshape | solution.py:379
  9.7 38.0 %block.1 = (bf16[24,1536]{1,0:T(8,128)(2,1)}, bf16[24,1536]{1,0:T(8,128)(2,1)}, f32[8,1536]{1,0:T(8,128)}, f32[3,4,96]{2,1,0:T(4,128)}, bf16[96,1536]{1,0:T(8,12...) custom-call(bf16[24,1536]{1,0:T(8,128)(2,1)} %bitcast.13, ...), custom_call_target="tpu_custom_call" | custom-call | tf_op jit(solution)/shard_map/block/pallas_call | solution.py:381
  47.7 8.0 %grads.1 = (bf16[24,1536]{1,0:T(8,128)(2,1)}, bf16[24,1536]{1,0:T(8,128)(2,1)}, f32[1536]{0:T(1024)}, f32[1536]{0:T(1024)}, bf16[1152,1536]{1,0:T(8,128)(2,1)}, ...) custom-call(bf16[96,1536]{1,0:T(8,128)(2,1)} %get-tuple-element.40.h, ...), custom_call_target="tpu_custom_call" | custom-call | tf_op jit(solution)/shard_map/grads/pallas_call | solution.py:405

commit v2 on v1

--- a/solution.py
+++ b/solution.py
@@ -55,12 +55,12 @@
     return cen, lax.rsqrt(var + EPS)
 
 
-def block_kernel(x_ref, gy_ref, g1_ref, be1_ref, g2_ref, be2_ref, bo_ref, bd_ref, bqkv_ref, bup_ref,
+def block_kernel(x_ref, gy_ref, g1_in, be1_in, g2_in, be2_in, bo_in, bd_in, bqkv_ref, bup_in,
                  wqkv_hbm, wout_hbm, wup_hbm, wdn_hbm,
                  y_ref, gx_ref, vec_ref, gbqkv_ref, h_ref, gqkv_ref, ctx_ref, gmid_ref, g_ref, gpre_ref, act_ref, gyf_ref,
                  wqkv, wout, wup, wdn, xg, gyg, xf, xhat, rstd_s, biasT, qkvT, probs,
                  a_ps, a_pr, a_hs, a_hr, a_cr, a_fr, b_ps, b_pr, b_hs, b_hr, b_cr, b_fr,
-                 gact, ghp, m_pr, m_hs, m_cr, r_pr, r_hs, r_cr, gm_f, ln_x, gg_f,
+                 gact, ghp, m_pr, m_hs, m_cr, r_pr, r_hs, r_cr, gm_f, ln_x, gg_f, par,
                  wsem, ssem, rsem):
     t = lax.axis_index('tp')
     core = t % 2
@@ -100,6 +100,10 @@
     y_p = send(gy_ref, gyg.at[t], pt)
     xg[t] = x_ref[...]
     gyg[t] = gy_ref[...]
+
+    for i, r in enumerate((g1_in, be1_in, g2_in, be2_in, bo_in, bd_in, bup_in)):
+        par[i, :] = r[...]
+    g1_ref, be1_ref, g2_ref, be2_ref, bo_ref, bd_ref, bup_ref = (par.at[i:i + 1] for i in range(7))
 
     for h in range(HL):
         for e in range(3):
@@ -368,7 +372,7 @@
 
 def solution(mesh):
     VM = pl.BlockSpec(memory_space=pltpu.VMEM)
-    ANY = pl.BlockSpec(memory_space=pl.ANY)
+    ANY = pl.BlockSpec(memory_space=pltpu.HBM)
 
     def sds(shape, dt):
         return jax.ShapeDtypeStruct(shape, dt)
@@ -376,7 +380,6 @@
     def local_step(x, g1, be1, w_qkv, b_qkv, w_out, b_out, g2, be2, w_up, b_up, w_down, b_down, grad_y):
         wq = jnp.transpose(w_qkv, (1, 2, 3, 0)).reshape(3 * HL * HD, D)
         bq = jnp.transpose(b_qkv, (1, 0, 2))
-        row = lambda v: v.reshape(1, -1)
         half = pltpu.VMEM((HCH, S, CW), BF)
         mids = pl.pallas_call(
             block_kernel,
@@ -393,12 +396,12 @@
                 pltpu.VMEM((S, FL), BF), pltpu.VMEM((2, TP, SL, D), BF),
                 pltpu.VMEM((2, SL, D), BF), pltpu.VMEM((SL, D), BF), pltpu.VMEM((SL, D), BF),
                 pltpu.VMEM((2, SL, D), BF), pltpu.VMEM((SL, D), BF), pltpu.VMEM((SL, D), BF),
-                pltpu.VMEM((S, D), F32), pltpu.VMEM((4, 2, D), F32), pltpu.VMEM((S, D), F32),
+                pltpu.VMEM((S, D), F32), pltpu.VMEM((4, 2, D), F32), pltpu.VMEM((S, D), F32), pltpu.VMEM((8, D), F32),
                 pltpu.SemaphoreType.DMA((9,)), pltpu.SemaphoreType.DMA((N_SEND,)), pltpu.SemaphoreType.DMA((N_SEND,)),
             ],
-            compiler_params=pltpu.CompilerParams(collective_id=0, has_side_effects=True),
+            compiler_params=pltpu.CompilerParams(collective_id=0, has_side_effects=True, vmem_limit_bytes=61 * 2**20),
             name='block',
-        )(x.reshape(SL, D), grad_y.reshape(SL, D), row(g1), row(be1), row(g2), row(be2), row(b_out), row(b_down), bq, row(b_up),
+        )(x.reshape(SL, D), grad_y.reshape(SL, D), g1, be1, g2, be2, b_out, b_down, bq, b_up,
           wq, w_out, w_up, w_down)
         y, gx, vec, gb, h, gqkv, ctx, gmid, g, gpre, act, gyf = mids
         vec1 = sds((D,), F32)
@@ -410,6 +413,7 @@
             out_specs=(VM, VM, VM, VM, ANY, VM, ANY, VM, VM, VM, ANY, VM, ANY, VM),
             scratch_shapes=[pltpu.VMEM((3 * HL * HD, D), BF), pltpu.VMEM((HL * HD, D), BF), pltpu.VMEM((D, FL), BF), pltpu.VMEM((FL, D), BF),
                             pltpu.SemaphoreType.DMA((32,))],
+            compiler_params=pltpu.CompilerParams(vmem_limit_bytes=22 * 2**20),
             name='grads',
         )(h, gqkv, ctx, gmid, g, gpre, act, gyf, y, gx, vec, gb)
         (y, gx, gl1, bl1, gwqkv, gbqkv, gwout, gbo, gl2, bl2, gwup, gbup, gwdn, gbd) = outs

time: 56.2 us -> 56.5 us (level)
  local copies, waits for them, and re-layouts: 9.06 us -> 10.9 us
  Pallas kernels: 46 us -> 44.4 us
    unnamed x0 -> x24, local copies, waits for them, and re-layouts: none -> 10.9 us
    reshape x7 -> x0, local copies, waits for them, and re-layouts: 9.06 us -> none  [local_step(): row = lambda v: v.reshape(1, -1)]
    pallas_call x1, Pallas kernels: 7.99 us -> 6.4 us  [local_step(): pl.pallas_call(grads_kernel, out_shape=(sds((SL, D), BF), sds((SL, D), BF...]
where the time goes in v2:
time: 56.5 us; the launch traced here: 55.9 us
  Pallas kernels  44.4 us (79%)
  local copies, waits for them, and re-layouts  10.9 us (19%)
  between operations  0.68 us (1%)
    pallas_call x1, Pallas kernels, local_step(): pl.pallas_call(block_kernel, out_shape=(sds((SL, D), BF), sds((SL, D), BF...  38 us
    unnamed x24, local copies, waits for them, and re-layouts  10.9 us
    pallas_call x1, Pallas kernels, local_step(): pl.pallas_call(grads_kernel, out_shape=(sds((SL, D), BF), sds((SL, D), BF...  6.4 us

profile of v2, /device:TPU:0, one launch (start us, length us, event | category | flops | bytes accessed | tf_op | source)
XLA Modules:
  0.0 55.9 jit_solution(12885046530848576888)
XLA Ops:
  0.7 38.0 %block.1 = (bf16[24,1536]{1,0:T(8,128)(2,1)}, bf16[24,1536]{1,0:T(8,128)(2,1)}, f32[8,1536]{1,0:T(8,128)}, f32[3,4,96]{2,1,0:T(4,128)}, bf16[96,1536]{1,0:T(8,12...) custom-call(bf16[24,1536]{1,0:T(8,128)(2,1)} %bitcast.13, ...), custom_call_target="tpu_custom_call" | custom-call | tf_op jit(solution)/shard_map/block/pallas_call | solution.py:384
  38.6 0.0 copy-start
  38.7 1.0 %copy-done = bf16[96,1536]{1,0:T(8,128)(2,1)S(1)} copy-done((bf16[96,1536]{1,0:T(8,128)(2,1)S(1)}, bf16[96,1536]{1,0:T(8,128)(2,1)}, u32[]{:S(2)}) %copy-start) | copy-done | bytes 294936
  39.6 0.0 copy-start.1
  39.6 1.0 %copy-done.1 = bf16[1152,96]{1,0:T(8,128)(2,1)S(1)} copy-done((bf16[1152,96]{1,0:T(8,128)(2,1)S(1)}, bf16[1152,96]{1,0:T(8,128)(2,1)}, u32[]{:S(2)}) %copy-start.1) | copy-done | bytes 221208
  40.6 0.0 copy-start.2
  40.6 1.0 %copy-done.2 = bf16[96,1536]{1,0:T(8,128)(2,1)S(1)} copy-done((bf16[96,1536]{1,0:T(8,128)(2,1)S(1)}, bf16[96,1536]{1,0:T(8,128)(2,1)}, u32[]{:S(2)}) %copy-start.2) | copy-done | bytes 294936
  41.5 0.0 copy-start.3
  41.5 1.0 %copy-done.3 = bf16[96,1536]{1,0:T(8,128)(2,1)S(1)} copy-done((bf16[96,1536]{1,0:T(8,128)(2,1)S(1)}, bf16[96,1536]{1,0:T(8,128)(2,1)}, u32[]{:S(2)}) %copy-start.3) | copy-done | bytes 294936
  42.5 0.0 copy-start.4
  42.5 1.0 %copy-done.4 = bf16[96,1536]{1,0:T(8,128)(2,1)S(1)} copy-done((bf16[96,1536]{1,0:T(8,128)(2,1)S(1)}, bf16[96,1536]{1,0:T(8,128)(2,1)}, u32[]{:S(2)}) %copy-start.4) | copy-done | bytes 294936
  43.5 0.0 copy-start.5
  43.5 1.0 %copy-done.5 = bf16[96,1536]{1,0:T(8,128)(2,1)S(1)} copy-done((bf16[96,1536]{1,0:T(8,128)(2,1)S(1)}, bf16[96,1536]{1,0:T(8,128)(2,1)}, u32[]{:S(2)}) %copy-start.5) | copy-done | bytes 294936
  44.4 0.0 copy-start.6
  44.4 1.0 %copy-done.6 = bf16[96,1536]{1,0:T(8,128)(2,1)S(1)} copy-done((bf16[96,1536]{1,0:T(8,128)(2,1)S(1)}, bf16[96,1536]{1,0:T(8,128)(2,1)}, u32[]{:S(2)}) %copy-start.6) | copy-done | bytes 294936
  45.4 0.0 copy-start.7
  45.4 0.9 %copy-done.7 = bf16[384,96]{1,0:T(8,128)(2,1)S(1)} copy-done((bf16[384,96]{1,0:T(8,128)(2,1)S(1)}, bf16[384,96]{1,0:T(8,128)(2,1)}, u32[]{:S(2)}) %copy-start.7) | copy-done | bytes 73752
  46.3 0.0 copy-start.8
  46.3 0.9 %copy-done.8 = bf16[24,1536]{1,0:T(8,128)(2,1)S(1)} copy-done((bf16[24,1536]{1,0:T(8,128)(2,1)S(1)}, bf16[24,1536]{1,0:T(8,128)(2,1)}, u32[]{:S(2)}) %copy-start.8) | copy-done | bytes 73752
  47.2 0.0 copy-start.9
  47.2 0.9 %copy-done.9 = bf16[24,1536]{1,0:T(8,128)(2,1)S(1)} copy-done((bf16[24,1536]{1,0:T(8,128)(2,1)S(1)}, bf16[24,1536]{1,0:T(8,128)(2,1)}, u32[]{:S(2)}) %copy-start.9) | copy-done | bytes 73752
  48.0 0.0 copy-start.10
  48.0 0.8 %copy-done.10 = f32[8,1536]{1,0:T(8,128)S(1)} copy-done((f32[8,1536]{1,0:T(8,128)S(1)}, f32[8,1536]{1,0:T(8,128)}, u32[]{:S(2)}) %copy-start.10) | copy-done | bytes 49176
  48.8 0.0 copy-start.11
  48.8 0.7 %copy-done.11 = f32[3,4,96]{2,1,0:T(4,128)S(1)} copy-done((f32[3,4,96]{2,1,0:T(4,128)S(1)}, f32[3,4,96]{2,1,0:T(4,128)}, u32[]{:S(2)}) %copy-start.11) | copy-done | bytes 4632
  49.5 6.4 %grads.1 = (bf16[24,1536]{1,0:T(8,128)(2,1)}, bf16[24,1536]{1,0:T(8,128)(2,1)}, f32[1536]{0:T(1024)}, f32[1536]{0:T(1024)}, bf16[1152,1536]{1,0:T(8,128)(2,1)}, ...) custom-call(bf16[96,1536]{1,0:T(8,128)(2,1)S(1)} %copy-done, ...), custom_call_target="tpu_custom_call" | custom-call | tf_op jit(solution)/shard_map/grads/pallas_call | solution.py:408
Async XLA Ops:
  38.6 1.0 %copy-start = (bf16[96,1536]{1,0:T(8,128)(2,1)S(1)}, bf16[96,1536]{1,0:T(8,128)(2,1)}, u32[]{:S(2)}) copy-start(bf16[96,1536]{1,0:T(8,128)(2,1)} %get-tuple-element.40.h_ref) | copy-start | bytes 884740
  39.6 1.0 %copy-start.1 = (bf16[1152,96]{1,0:T(8,128)(2,1)S(1)}, bf16[1152,96]{1,0:T(8,128)(2,1)}, u32[]{:S(2)}) copy-start(bf16[1152,96]{1,0:T(8,128)(2,1)} %get-tuple-element.41.gqkv_ref) | copy-start | bytes 663556
  40.6 1.0 %copy-start.2 = (bf16[96,1536]{1,0:T(8,128)(2,1)S(1)}, bf16[96,1536]{1,0:T(8,128)(2,1)}, u32[]{:S(2)}) copy-start(bf16[96,1536]{1,0:T(8,128)(2,1)} %get-tuple-element.43.gmid_ref) | copy-start | bytes 884740
  41.5 1.0 %copy-start.3 = (bf16[96,1536]{1,0:T(8,128)(2,1)S(1)}, bf16[96,1536]{1,0:T(8,128)(2,1)}, u32[]{:S(2)}) copy-start(bf16[96,1536]{1,0:T(8,128)(2,1)} %get-tuple-element.44.g_ref) | copy-start | bytes 884740
  42.5 1.0 %copy-start.4 = (bf16[96,1536]{1,0:T(8,128)(2,1)S(1)}, bf16[96,1536]{1,0:T(8,128)(2,1)}, u32[]{:S(2)}) copy-start(bf16[96,1536]{1,0:T(8,128)(2,1)} %get-tuple-element.45.gpre_ref) | copy-start | bytes 884740
  43.5 1.0 %copy-start.5 = (bf16[96,1536]{1,0:T(8,128)(2,1)S(1)}, bf16[96,1536]{1,0:T(8,128)(2,1)}, u32[]{:S(2)}) copy-start(bf16[96,1536]{1,0:T(8,128)(2,1)} %get-tuple-element.46.act_ref) | copy-start | bytes 884740
  44.4 1.0 %copy-start.6 = (bf16[96,1536]{1,0:T(8,128)(2,1)S(1)}, bf16[96,1536]{1,0:T(8,128)(2,1)}, u32[]{:S(2)}) copy-start(bf16[96,1536]{1,0:T(8,128)(2,1)} %get-tuple-element.47.gyf_ref) | copy-start | bytes 884740
  45.4 0.9 %copy-start.7 = (bf16[384,96]{1,0:T(8,128)(2,1)S(1)}, bf16[384,96]{1,0:T(8,128)(2,1)}, u32[]{:S(2)}) copy-start(bf16[384,96]{1,0:T(8,128)(2,1)} %get-tuple-element.42.ctx_ref) | copy-start | bytes 221188
  46.3 0.9 %copy-start.8 = (bf16[24,1536]{1,0:T(8,128)(2,1)S(1)}, bf16[24,1536]{1,0:T(8,128)(2,1)}, u32[]{:S(2)}) copy-start(bf16[24,1536]{1,0:T(8,128)(2,1)} %get-tuple-element.48.yi_ref) | copy-start | bytes 221188
  47.2 0.9 %copy-start.9 = (bf16[24,1536]{1,0:T(8,128)(2,1)S(1)}, bf16[24,1536]{1,0:T(8,128)(2,1)}, u32[]{:S(2)}) copy-start(bf16[24,1536]{1,0:T(8,128)(2,1)} %get-tuple-element.49.gxi_ref) | copy-start | bytes 221188
  48.0 0.8 %copy-start.10 = (f32[8,1536]{1,0:T(8,128)S(1)}, f32[8,1536]{1,0:T(8,128)}, u32[]{:S(2)}) copy-start(f32[8,1536]{1,0:T(8,128)} %get-tuple-element.50.vec_ref) | copy-start | bytes 147460
  48.8 0.7 %copy-start.11 = (f32[3,4,96]{2,1,0:T(4,128)S(1)}, f32[3,4,96]{2,1,0:T(4,128)}, u32[]{:S(2)}) copy-start(f32[3,4,96]{2,1,0:T(4,128)} %get-tuple-element.51.gbi_ref) | copy-start | bytes 13828

commit v3 on v2

--- a/solution.py
+++ b/solution.py
@@ -55,13 +55,14 @@
     return cen, lax.rsqrt(var + EPS)
 
 
-def block_kernel(x_ref, gy_ref, g1_in, be1_in, g2_in, be2_in, bo_in, bd_in, bqkv_ref, bup_in,
+def block_kernel(x_hbm, gy_hbm, g1_hbm, be1_hbm, g2_hbm, be2_hbm, bo_hbm, bd_hbm, bqkv_hbm, bup_hbm,
                  wqkv_hbm, wout_hbm, wup_hbm, wdn_hbm,
-                 y_ref, gx_ref, vec_ref, gbqkv_ref, h_ref, gqkv_ref, ctx_ref, gmid_ref, g_ref, gpre_ref, act_ref, gyf_ref,
+                 y_ref, gx_ref, vec_ref, gbqkv_ref, gwqkv_ref, gwout_ref, gwup_ref, gwdn_ref,
+                 h_ref, gqkv_ref, ctx_ref, gmid_ref, g_ref, gpre_ref, act_ref, gyf_ref,
                  wqkv, wout, wup, wdn, xg, gyg, xf, xhat, rstd_s, biasT, qkvT, probs,
                  a_ps, a_pr, a_hs, a_hr, a_cr, a_fr, b_ps, b_pr, b_hs, b_hr, b_cr, b_fr,
-                 gact, ghp, m_pr, m_hs, m_cr, r_pr, r_hs, r_cr, gm_f, ln_x, gg_f, par,
-                 wsem, ssem, rsem):
+                 gact, ghp, m_pr, m_hs, m_cr, r_pr, r_hs, r_cr, gm_f, ln_x, gg_f, par, bqkv_ref, g1_in, be1_in, g2_in, be2_in, bo_in, bd_in, bup_in,
+                 wsem, ssem, rsem, isem):
     t = lax.axis_index('tp')
     core = t % 2
     pt = t + 1 - 2 * core
@@ -80,6 +81,13 @@
         started.append(c)
         return c
 
+    in_x = pltpu.make_async_copy(x_hbm, xg.at[t], isem.at[0])
+    in_gy = pltpu.make_async_copy(gy_hbm, gyg.at[t], isem.at[1])
+    in_b = pltpu.make_async_copy(bqkv_hbm, bqkv_ref, isem.at[2])
+    small = ((g1_hbm, g1_in), (be1_hbm, be1_in), (g2_hbm, g2_in), (be2_hbm, be2_in), (bo_hbm, bo_in), (bd_hbm, bd_in), (bup_hbm, bup_in))
+    in_p = [pltpu.make_async_copy(a, b, isem.at[3 + i]) for i, (a, b) in enumerate(small)]
+    for c in (in_x, in_gy, in_b, *in_p):
+        c.start()
     w_cps = {}
     w_cps['qkv'] = [pltpu.make_async_copy(wqkv_hbm, wqkv, wsem.at[0])]
     w_cps['out'] = [pltpu.make_async_copy(wout_hbm.at[:, pl.ds(k * CW, CW)], wout.at[k], wsem.at[1 + k]) for k in range(NCH)]
@@ -94,13 +102,15 @@
             c.start()
     pl.semaphore_wait(barrier, 2)
 
-    x_c = send(x_ref, xg.at[t], ct)
-    x_p = send(x_ref, xg.at[t], pt)
-    y_c = send(gy_ref, gyg.at[t], ct)
-    y_p = send(gy_ref, gyg.at[t], pt)
-    xg[t] = x_ref[...]
-    gyg[t] = gy_ref[...]
-
+    in_x.wait()
+    x_c = send(xg.at[t], xg.at[t], ct)
+    x_p = send(xg.at[t], xg.at[t], pt)
+    in_gy.wait()
+    y_c = send(gyg.at[t], gyg.at[t], ct)
+    y_p = send(gyg.at[t], gyg.at[t], pt)
+
+    for c in (in_b, *in_p):
+        c.wait()
     for i, r in enumerate((g1_in, be1_in, g2_in, be2_in, bo_in, bd_in, bup_in)):
         par[i, :] = r[...]
     g1_ref, be1_ref, g2_ref, be2_ref, bo_ref, bd_ref, bup_ref = (par.at[i:i + 1] for i in range(7))
@@ -240,11 +250,18 @@
     actv = act_ref[...]
     m_first = scatter_first(lambda n: dot(actv, wdn[:, n * CW:(n + 1) * CW], 1, 0), ghp.at[0], m_pr)
 
-    g_fwd = forward(g_outs, b_cr, b_fr)
+    for n in range(NCH):
+        gwdn_ref[n * CW:(n + 1) * CW, :] = dot(act_ref[:, n * CW:(n + 1) * CW], gyv, 0, 0).astype(BF)
 
     m_first[0].wait_recv()
     m_hs[...] = (ghp[0, ct].astype(F32) + m_pr[1].astype(F32)).astype(BF)
     m_out = send(m_hs, m_cr, ct)
+    g_fwd = []
+    for k in range(HCH):
+        g_outs[k][0].wait_recv()
+        g_fwd.append(send(b_cr.at[k], b_fr.at[k], pt))
+        for n in range(2 * k, 2 * k + 2):
+            gwup_ref[n * CW:(n + 1) * CW, :] = dot(g_ref[:, n * CW:(n + 1) * CW], gprev, 0, 0).astype(BF)
 
     def put_g(kk, val):
         gg_f[:, pl.ds(pl.multiple_of(kk * CW, CW), CW)] = val
@@ -308,6 +325,10 @@
     ln_hs[...] = ln_s[...] + ln_pr[...]
     l_out = send(ln_hs, ln_cr, ct)
 
+    gwout_ref[...] = dot(ctx_ref[...], gmv, 1, 0).astype(BF)
+    for h in range(HL):
+        rows = slice(h * 3 * HD, (h + 1) * 3 * HD)
+        gwqkv_ref[rows, :] = dot(gqkv_ref[rows, :], h_ref[...], 1, 0).astype(BF)
     own = pl.ds(pl.multiple_of(t * SL, 8), SL)
     m_first[1].wait_recv()
     m_out.wait_recv()
@@ -330,42 +351,27 @@
 
 
 N_SEND = 38
-
-
-def grads_kernel(h_ref, gqkv_ref, ctx_ref, gmid_ref, g_ref, gpre_ref, act_ref, gyf_ref, yi_ref, gxi_ref, vec_ref, gbi_ref,
+VMEM_A = 34 * 2**20
+VMEM_B = 8 * 2**20
+
+
+def write_kernel(yi_ref, gxi_ref, vec_ref, gbi_ref, qkv_ref, out_ref, up_ref, dn_ref,
                  y_ref, gx_ref, gl1_ref, bl1_ref, gwqkv_ref, gbqkv_ref, gwout_ref, gbo_ref, gl2_ref, bl2_ref,
-                 gwup_ref, gbup_ref, gwdn_ref, gbd_ref, s_qkv, s_out, s_up, s_dn, sem):
+                 gwup_ref, gbup_ref, gwdn_ref, gbd_ref, sem):
     cps = []
-
-    def out(src, dst):
-        c = pltpu.make_async_copy(src, dst, sem.at[len(cps)])
-        c.start()
-        cps.append(c)
-
+    for src, dst in ((dn_ref, gwdn_ref), (up_ref, gwup_ref), (qkv_ref, gwqkv_ref), (out_ref, gwout_ref)):
+        rows = src.shape[0] // 4
+        for k in range(4):
+            part = pl.ds(k * rows, rows)
+            c = pltpu.make_async_copy(src.at[part], dst.at[part], sem.at[len(cps)])
+            c.start()
+            cps.append(c)
     y_ref[...] = yi_ref[...]
     gx_ref[...] = gxi_ref[...]
     gbqkv_ref[...] = gbi_ref[...]
     for i, r in enumerate((gbd_ref, gbup_ref, gl2_ref, bl2_ref, gbo_ref, None, gl1_ref, bl1_ref)):
         if r is not None:
             r[...] = vec_ref[i, :]
-
-    gyv = gyf_ref[...]
-    gpv = gpre_ref[...]
-    for n in range(NCH):
-        rows = pl.ds(n * CW, CW)
-        s_dn[rows, :] = dot(act_ref[:, n * CW:(n + 1) * CW], gyv, 0, 0).astype(BF)
-        out(s_dn.at[rows], gwdn_ref.at[rows])
-    for n in range(NCH):
-        rows = pl.ds(n * CW, CW)
-        s_up[rows, :] = dot(g_ref[:, n * CW:(n + 1) * CW], gpv, 0, 0).astype(BF)
-        out(s_up.at[rows], gwup_ref.at[rows])
-    hv = h_ref[...]
-    for n in range(HL):
-        rows = pl.ds(n * 3 * HD, 3 * HD)
-        s_qkv[rows, :] = dot(gqkv_ref[n * 3 * HD:(n + 1) * 3 * HD, :], hv, 1, 0).astype(BF)
-        out(s_qkv.at[rows], gwqkv_ref.at[rows])
-    s_out[...] = dot(ctx_ref[...], gmid_ref[...], 1, 0).astype(BF)
-    out(s_out, gwout_ref)
     for c in cps:
         c.wait()
 
@@ -383,12 +389,13 @@
         half = pltpu.VMEM((HCH, S, CW), BF)
         mids = pl.pallas_call(
             block_kernel,
-            out_shape=(sds((SL, D), BF), sds((SL, D), BF), sds((8, D), F32), sds((3, HL, HD), F32), sds((S, D), BF),
-                       sds((3 * HL * HD, S), BF), sds((HL * HD, S), BF), sds((S, D), BF), sds((S, D), BF), sds((S, FL), BF),
-                       sds((S, FL), BF), sds((S, D), BF)),
-            in_specs=[VM] * 10 + [ANY] * 4,
-            out_specs=(VM,) * 12,
+            out_shape=(pltpu.VMEM((SL, D), BF), pltpu.VMEM((SL, D), BF), pltpu.VMEM((8, D), F32), pltpu.VMEM((3, HL, HD), F32),
+                       pltpu.VMEM((3 * HL * HD, D), BF), pltpu.VMEM((HL * HD, D), BF), pltpu.VMEM((D, FL), BF), pltpu.VMEM((FL, D), BF)),
+            in_specs=[ANY] * 14,
+            out_specs=(VM,) * 8,
             scratch_shapes=[
+                pltpu.VMEM((S, D), BF), pltpu.VMEM((3 * HL * HD, S), BF), pltpu.VMEM((HL * HD, S), BF), pltpu.VMEM((S, D), BF),
+                pltpu.VMEM((S, D), BF), pltpu.VMEM((S, FL), BF), pltpu.VMEM((S, FL), BF), pltpu.VMEM((S, D), BF),
                 pltpu.VMEM((3 * HL * HD, D), BF), pltpu.VMEM((NCH, HL * HD, CW), BF), pltpu.VMEM((D, FL), BF), pltpu.VMEM((FL, D), BF),
                 pltpu.VMEM((TP, SL, D), BF), pltpu.VMEM((TP, SL, D), BF), pltpu.VMEM((S, D), F32), pltpu.VMEM((S, D), F32),
                 pltpu.VMEM((S, 128), F32), pltpu.VMEM((3 * HL * HD, S), F32), pltpu.VMEM((3 * HL * HD, S), BF), pltpu.VMEM((HL, S, S), F32),
@@ -397,25 +404,25 @@
                 pltpu.VMEM((2, SL, D), BF), pltpu.VMEM((SL, D), BF), pltpu.VMEM((SL, D), BF),
                 pltpu.VMEM((2, SL, D), BF), pltpu.VMEM((SL, D), BF), pltpu.VMEM((SL, D), BF),
                 pltpu.VMEM((S, D), F32), pltpu.VMEM((4, 2, D), F32), pltpu.VMEM((S, D), F32), pltpu.VMEM((8, D), F32),
+                pltpu.VMEM((3, HL, HD), F32), *[pltpu.VMEM((D,), F32) for _ in range(7)],
                 pltpu.SemaphoreType.DMA((9,)), pltpu.SemaphoreType.DMA((N_SEND,)), pltpu.SemaphoreType.DMA((N_SEND,)),
+                pltpu.SemaphoreType.DMA((10,)),
             ],
-            compiler_params=pltpu.CompilerParams(collective_id=0, has_side_effects=True, vmem_limit_bytes=61 * 2**20),
+            compiler_params=pltpu.CompilerParams(collective_id=0, has_side_effects=True, vmem_limit_bytes=VMEM_A),
             name='block',
-        )(x.reshape(SL, D), grad_y.reshape(SL, D), g1, be1, g2, be2, b_out, b_down, bq, b_up,
-          wq, w_out, w_up, w_down)
-        y, gx, vec, gb, h, gqkv, ctx, gmid, g, gpre, act, gyf = mids
+        )(*(pltpu.with_memory_space_constraint(v, pltpu.HBM) for v in (
+            x.reshape(SL, D), grad_y.reshape(SL, D), g1, be1, g2, be2, b_out, b_down, bq, b_up, wq, w_out, w_up, w_down)))
         vec1 = sds((D,), F32)
         outs = pl.pallas_call(
-            grads_kernel,
+            write_kernel,
             out_shape=(sds((SL, D), BF), sds((SL, D), BF), vec1, vec1, sds((3 * HL * HD, D), BF), sds((3, HL, HD), F32),
                        sds((HL * HD, D), BF), vec1, vec1, vec1, sds((D, FL), BF), vec1, sds((FL, D), BF), vec1),
-            in_specs=[VM] * 12,
+            in_specs=[VM] * 8,
             out_specs=(VM, VM, VM, VM, ANY, VM, ANY, VM, VM, VM, ANY, VM, ANY, VM),
-            scratch_shapes=[pltpu.VMEM((3 * HL * HD, D), BF), pltpu.VMEM((HL * HD, D), BF), pltpu.VMEM((D, FL), BF), pltpu.VMEM((FL, D), BF),
-                            pltpu.SemaphoreType.DMA((32,))],
-            compiler_params=pltpu.CompilerParams(vmem_limit_bytes=22 * 2**20),
-            name='grads',
-        )(h, gqkv, ctx, gmid, g, gpre, act, gyf, y, gx, vec, gb)
+            scratch_shapes=[pltpu.SemaphoreType.DMA((16,))],
+            compiler_params=pltpu.CompilerParams(vmem_limit_bytes=VMEM_B),
+            name='write',
+        )(*mids)
         (y, gx, gl1, bl1, gwqkv, gbqkv, gwout, gbo, gl2, bl2, gwup, gbup, gwdn, gbd) = outs
         gwqkv = jnp.transpose(gwqkv.reshape(HL, 3, HD, D), (3, 0, 1, 2))
         gbqkv = jnp.transpose(gbqkv, (1, 0, 2))

time: 56.5 us -> 42.3 us (0.75)
  local copies, waits for them, and re-layouts: 10.9 us -> 0 us
  Pallas kernels: 44.4 us -> 41.6 us
    unnamed x24 -> x0, local copies, waits for them, and re-layouts: 10.9 us -> none
    pallas_call x2, Pallas kernels: 44.4 us -> 41.6 us  [the longest x1 35.7 us: local_step(): pl.pallas_call(block_kernel, out_shape=(pltpu.VMEM((SL, D), BF), pltpu.VM...]
where the time goes in v3:
time: 42.3 us; the launch traced here: 42.2 us
  Pallas kernels  41.6 us (98%)
  between operations  0.66 us (2%)
    pallas_call x1, Pallas kernels, local_step(): pl.pallas_call(block_kernel, out_shape=(pltpu.VMEM((SL, D), BF), pltpu.VM...  35.7 us
    pallas_call x1, Pallas kernels, local_step(): pl.pallas_call(write_kernel, out_shape=(sds((SL, D), BF), sds((SL, D), BF...  5.84 us

profile of v3, /device:TPU:0, one launch (start us, length us, event | category | flops | bytes accessed | tf_op | source)
XLA Modules:
  0.0 42.2 jit_solution(18304581327688127374)
XLA Ops:
  0.7 35.7 %block.1 = (bf16[24,1536]{1,0:T(8,128)(2,1)S(1)}, bf16[24,1536]{1,0:T(8,128)(2,1)S(1)}, f32[8,1536]{1,0:T(8,128)S(1)}, f32[3,4,96]{2,1,0:T(4,128)S(1)}, bf16[115...) custom-call(bf16[24,1536]{1,0:T(8,128)(2,1)} %bitcast.13, ...), custom_call_target="tpu_custom_call" | custom-call | tf_op jit(solution)/shard_map/block/pallas_call | solution.py:390
  36.4 5.8 %write.1 = (bf16[24,1536]{1,0:T(8,128)(2,1)}, bf16[24,1536]{1,0:T(8,128)(2,1)}, f32[1536]{0:T(1024)}, f32[1536]{0:T(1024)}, bf16[1152,1536]{1,0:T(8,128)(2,1)}, ...) custom-call(bf16[24,1536]{1,0:T(8,128)(2,1)S(1)} %get-tuple-element., ...), custom_call_target="tpu_custom_call" | custom-call | tf_op jit(solution)/shard_map/write/pallas_call | solution.py:416

commit v4 on v3

--- a/solution.py
+++ b/solution.py
@@ -24,6 +24,7 @@
 CW = 256
 NCH = D // CW
 HCH = NCH // 2
+HW = D // 2
 
 
 def alibi_slopes(n_heads):
@@ -66,8 +67,9 @@
     t = lax.axis_index('tp')
     core = t % 2
     pt = t + 1 - 2 * core
-    ct = (t + 2) % TP
-    qt = (pt + 2) % TP
+    ct = TP - 1 - t
+    qt = TP - 1 - pt
+    half = (core + t // 2) % 2
 
     started = []
     counter = [0]
@@ -90,7 +92,7 @@
         c.start()
     w_cps = {}
     w_cps['qkv'] = [pltpu.make_async_copy(wqkv_hbm, wqkv, wsem.at[0])]
-    w_cps['out'] = [pltpu.make_async_copy(wout_hbm.at[:, pl.ds(k * CW, CW)], wout.at[k], wsem.at[1 + k]) for k in range(NCH)]
+    w_cps['out'] = [pltpu.make_async_copy(wout_hbm.at[:, pl.ds(k * HW, HW)], wout.at[k], wsem.at[1 + k]) for k in range(2)]
     w_cps['dn'] = [pltpu.make_async_copy(wdn_hbm, wdn, wsem.at[7])]
     w_cps['up'] = [pltpu.make_async_copy(wup_hbm, wup, wsem.at[8])]
 
@@ -164,12 +166,14 @@
 
     def exchange(part, ps, pr, hs, hr, cr):
         firsts = []
+        theirs = part(1 - half)
         for k in range(HCH):
-            ps[k] = part((1 - core) * HCH + k).astype(BF)
+            ps[k] = theirs[:, k * CW:(k + 1) * CW].astype(BF)
             firsts.append(send(ps.at[k], pr.at[k], pt))
+        ours = part(half)
         outs = []
         for k in range(HCH):
-            own = part(core * HCH + k)
+            own = ours[:, k * CW:(k + 1) * CW]
             firsts[k].wait_recv()
             hs[k] = (own + pr[k].astype(F32)).astype(BF)
             outs.append((send(hs.at[k], cr.at[k], ct), send(hs.at[k], hr.at[k], pt)))
@@ -201,11 +205,11 @@
 
     def gathered(outs, fwd, hs, hr, cr, fr, put):
         for k in range(HCH):
-            put(core * HCH + k, (hs[k].astype(F32) + cr[k].astype(F32)).astype(BF).astype(F32))
+            put(half * HCH + k, (hs[k].astype(F32) + cr[k].astype(F32)).astype(BF).astype(F32))
         for k in range(HCH):
             outs[k][1].wait_recv()
             fwd[k].wait_recv()
-            put((1 - core) * HCH + k, (hr[k].astype(F32) + fr[k].astype(F32)).astype(BF).astype(F32))
+            put((1 - half) * HCH + k, (hr[k].astype(F32) + fr[k].astype(F32)).astype(BF).astype(F32))
 
     a_fwd = forward(a_outs, a_cr, a_fr)
 
@@ -233,18 +237,16 @@
     gprev = gpre_ref[...]
 
     def part_g(kk):
-        return dot(gprev, wup[pl.ds(pl.multiple_of(kk * CW, CW), CW), :], 1, 1)
+        return dot(gprev, wup[pl.ds(pl.multiple_of(kk * HW, HW), HW), :], 1, 1)
 
     g_outs = exchange(part_g, b_ps, b_pr, b_hs, b_hr, b_cr)
 
-    def scatter_first(part, buf, pr, extra=None):
+    def scatter_first(part, buf, pr):
         for n in range(NCH):
             cols = slice(n * CW, (n + 1) * CW)
             v = part(n)
             for i in range(TP):
                 buf[i, :, cols] = v[i * SL:(i + 1) * SL, :].astype(BF)
-            if extra is not None:
-                extra(n, v)
         return (send(buf.at[qt], pr.at[1], pt), send(buf.at[pt], pr.at[0], pt))
 
     actv = act_ref[...]
@@ -289,33 +291,30 @@
     vec_ref[4:5, :] = gbo
 
     gmv = gmid_ref[...]
-    gctxT = dot(wout[0], gmv[:, :CW], 1, 1)
-    for k in range(1, NCH):
-        gctxT = gctxT + dot(wout[k], gmv[:, k * CW:(k + 1) * CW], 1, 1)
-    gctxT = gctxT.astype(BF)
-    ones = jnp.ones((8, S), BF)
-    for h in range(HL):
-        go = gctxT[h * HD:(h + 1) * HD, :]
-        p = probs[h]
-        gp = dot(head(h, 2), go, 0, 0).astype(BF).astype(F32)
-        gv_ = dot(go, p.astype(BF), 1, 1).astype(BF)
-        gs = (p * (gp - jnp.sum(gp * p, axis=0, keepdims=True))).astype(BF)
-        gq = (dot(head(h, 1), gs, 1, 0) * scale).astype(BF)
-        gk = (dot(head(h, 0), gs, 1, 1) * scale).astype(BF)
-        for e, val in enumerate((gq, gk, gv_)):
+    gctxT = (dot(wout[0], gmv[:, :HW], 1, 1) + dot(wout[1], gmv[:, HW:], 1, 1)).astype(BF)
+    heads = range(HL)
+    gos = [gctxT[h * HD:(h + 1) * HD, :] for h in heads]
+    gps = [dot(head(h, 2), gos[h], 0, 0).astype(BF).astype(F32) for h in heads]
+    gvs = [dot(gos[h], probs[h].astype(BF), 1, 1).astype(BF) for h in heads]
+    gss = [(probs[h] * (gps[h] - jnp.sum(gps[h] * probs[h], axis=0, keepdims=True))).astype(BF) for h in heads]
+    gqs = [(dot(head(h, 1), gss[h], 1, 0) * scale).astype(BF) for h in heads]
+    gks = [(dot(head(h, 0), gss[h], 1, 1) * scale).astype(BF) for h in heads]
+    for h in heads:
+        for e, val in enumerate((gqs[h], gks[h], gvs[h])):
             gqkv_ref[(h * 3 + e) * HD:(h * 3 + e + 1) * HD, :] = val
-            gbqkv_ref[e, h:h + 1, :] = dot(ones, val, 1, 1)[0:1, :]
 
     gqv = gqkv_ref[...]
 
-    def ln1_sums(n, v):
-        cols = slice(n * CW, (n + 1) * CW)
-        v = v.astype(BF).astype(F32)
-        ln_s[0:1, cols] = jnp.sum(v * xhat[:, cols], axis=0, keepdims=True)
-        ln_s[1:2, cols] = jnp.sum(v, axis=0, keepdims=True)
-
     ln_s, ln_pr, ln_hs, ln_cr = ln_x.at[0], ln_x.at[1], ln_x.at[2], ln_x.at[3]
-    r_first = scatter_first(lambda n: dot(gqv, wqkv[:, n * CW:(n + 1) * CW], 0, 0), ghp.at[1], r_pr, ln1_sums)
+    r_first = scatter_first(lambda n: dot(gqv, wqkv[:, n * CW:(n + 1) * CW], 0, 0), ghp.at[1], r_pr)
+    gg1 = jnp.zeros((1, D), F32)
+    gb1 = jnp.zeros((1, D), F32)
+    for i in range(TP):
+        v = ghp[1, i].astype(F32)
+        gg1 = gg1 + jnp.sum(v * xhat[i * SL:(i + 1) * SL, :], axis=0, keepdims=True)
+        gb1 = gb1 + jnp.sum(v, axis=0, keepdims=True)
+    ln_s[0:1, :] = gg1
+    ln_s[1:2, :] = gb1
     l_first = send(ln_s, ln_pr, pt)
 
     r_first[0].wait_recv()
@@ -325,6 +324,10 @@
     ln_hs[...] = ln_s[...] + ln_pr[...]
     l_out = send(ln_hs, ln_cr, ct)
 
+    ones = jnp.ones((8, S), BF)
+    for h in heads:
+        for e in range(3):
+            gbqkv_ref[e, h:h + 1, :] = dot(ones, gqkv_ref[(h * 3 + e) * HD:(h * 3 + e + 1) * HD, :], 1, 1)[0:1, :]
     gwout_ref[...] = dot(ctx_ref[...], gmv, 1, 0).astype(BF)
     for h in range(HL):
         rows = slice(h * 3 * HD, (h + 1) * 3 * HD)
@@ -386,7 +389,7 @@
     def local_step(x, g1, be1, w_qkv, b_qkv, w_out, b_out, g2, be2, w_up, b_up, w_down, b_down, grad_y):
         wq = jnp.transpose(w_qkv, (1, 2, 3, 0)).reshape(3 * HL * HD, D)
         bq = jnp.transpose(b_qkv, (1, 0, 2))
-        half = pltpu.VMEM((HCH, S, CW), BF)
+        part = pltpu.VMEM((HCH, S, CW), BF)
         mids = pl.pallas_call(
             block_kernel,
             out_shape=(pltpu.VMEM((SL, D), BF), pltpu.VMEM((SL, D), BF), pltpu.VMEM((8, D), F32), pltpu.VMEM((3, HL, HD), F32),
@@ -396,10 +399,10 @@
             scratch_shapes=[
                 pltpu.VMEM((S, D), BF), pltpu.VMEM((3 * HL * HD, S), BF), pltpu.VMEM((HL * HD, S), BF), pltpu.VMEM((S, D), BF),
                 pltpu.VMEM((S, D), BF), pltpu.VMEM((S, FL), BF), pltpu.VMEM((S, FL), BF), pltpu.VMEM((S, D), BF),
-                pltpu.VMEM((3 * HL * HD, D), BF), pltpu.VMEM((NCH, HL * HD, CW), BF), pltpu.VMEM((D, FL), BF), pltpu.VMEM((FL, D), BF),
+                pltpu.VMEM((3 * HL * HD, D), BF), pltpu.VMEM((2, HL * HD, HW), BF), pltpu.VMEM((D, FL), BF), pltpu.VMEM((FL, D), BF),
                 pltpu.VMEM((TP, SL, D), BF), pltpu.VMEM((TP, SL, D), BF), pltpu.VMEM((S, D), F32), pltpu.VMEM((S, D), F32),
                 pltpu.VMEM((S, 128), F32), pltpu.VMEM((3 * HL * HD, S), F32), pltpu.VMEM((3 * HL * HD, S), BF), pltpu.VMEM((HL, S, S), F32),
-                half, half, half, half, half, half, half, half, half, half, half, half,
+                *[part] * 12,
                 pltpu.VMEM((S, FL), BF), pltpu.VMEM((2, TP, SL, D), BF),
                 pltpu.VMEM((2, SL, D), BF), pltpu.VMEM((SL, D), BF), pltpu.VMEM((SL, D), BF),
                 pltpu.VMEM((2, SL, D), BF), pltpu.VMEM((SL, D), BF), pltpu.VMEM((SL, D), BF),

time: 42.3 us -> 41.8 us (0.988)
  Pallas kernels: 41.6 us -> 41 us
    pallas_call x1, Pallas kernels: 35.7 us -> 35.2 us  [local_step(): pl.pallas_call(block_kernel, out_shape=(pltpu.VMEM((SL, D), BF), pltpu.VM...]
where the time goes in v4:
time: 41.8 us; the launch traced here: 41.7 us
  Pallas kernels  41 us (98%)
  between operations  0.66 us (2%)
    pallas_call x1, Pallas kernels, local_step(): pl.pallas_call(block_kernel, out_shape=(pltpu.VMEM((SL, D), BF), pltpu.VM...  35.2 us
    pallas_call x1, Pallas kernels, local_step(): pl.pallas_call(write_kernel, out_shape=(sds((SL, D), BF), sds((SL, D), BF...  5.84 us

profile of v4, /device:TPU:0, one launch (start us, length us, event | category | flops | bytes accessed | tf_op | source)
XLA Modules:
  0.0 41.7 jit_solution(12006369681668126466)
XLA Ops:
  0.7 35.2 %block.1 = (bf16[24,1536]{1,0:T(8,128)(2,1)S(1)}, bf16[24,1536]{1,0:T(8,128)(2,1)S(1)}, f32[8,1536]{1,0:T(8,128)S(1)}, f32[3,4,96]{2,1,0:T(4,128)S(1)}, bf16[115...) custom-call(bf16[24,1536]{1,0:T(8,128)(2,1)} %bitcast.13, ...), custom_call_target="tpu_custom_call" | custom-call | tf_op jit(solution)/shard_map/block/pallas_call | solution.py:393
  35.8 5.8 %write.1 = (bf16[24,1536]{1,0:T(8,128)(2,1)}, bf16[24,1536]{1,0:T(8,128)(2,1)}, f32[1536]{0:T(1024)}, f32[1536]{0:T(1024)}, bf16[1152,1536]{1,0:T(8,128)(2,1)}, ...) custom-call(bf16[24,1536]{1,0:T(8,128)(2,1)S(1)} %get-tuple-element., ...), custom_call_target="tpu_custom_call" | custom-call | tf_op jit(solution)/shard_map/write/pallas_call | solution.py:419

commit v5 on v4

--- a/solution.py
+++ b/solution.py
@@ -56,32 +56,49 @@
     return cen, lax.rsqrt(var + EPS)
 
 
-def block_kernel(x_hbm, gy_hbm, g1_hbm, be1_hbm, g2_hbm, be2_hbm, bo_hbm, bd_hbm, bqkv_hbm, bup_hbm,
-                 wqkv_hbm, wout_hbm, wup_hbm, wdn_hbm,
-                 y_ref, gx_ref, vec_ref, gbqkv_ref, gwqkv_ref, gwout_ref, gwup_ref, gwdn_ref,
-                 h_ref, gqkv_ref, ctx_ref, gmid_ref, g_ref, gpre_ref, act_ref, gyf_ref,
-                 wqkv, wout, wup, wdn, xg, gyg, xf, xhat, rstd_s, biasT, qkvT, probs,
-                 a_ps, a_pr, a_hs, a_hr, a_cr, a_fr, b_ps, b_pr, b_hs, b_hr, b_cr, b_fr,
-                 gact, ghp, m_pr, m_hs, m_cr, r_pr, r_hs, r_cr, gm_f, ln_x, gg_f, par, bqkv_ref, g1_in, be1_in, g2_in, be2_in, bo_in, bd_in, bup_in,
-                 wsem, ssem, rsem, isem):
+def places():
     t = lax.axis_index('tp')
     core = t % 2
     pt = t + 1 - 2 * core
     ct = TP - 1 - t
     qt = TP - 1 - pt
     half = (core + t // 2) % 2
-
+    return t, pt, ct, qt, half
+
+
+def sender(ssem, rsem):
     started = []
-    counter = [0]
 
     def send(src, dst, dev):
-        i = counter[0]
-        counter[0] += 1
+        i = len(started)
         c = pltpu.make_async_remote_copy(src_ref=src, dst_ref=dst, send_sem=ssem.at[i], recv_sem=rsem.at[i],
                                          device_id={'tp': dev}, device_id_type=MESH)
         c.start()
         started.append(c)
         return c
+
+    return send, started
+
+
+def head_rows(h, e):
+    return slice((h * 3 + e) * HD, (h * 3 + e + 1) * HD)
+
+
+def row_blocks(buf, cols, v):
+    for i in range(TP):
+        buf[i, :, cols] = v[i * SL:(i + 1) * SL, :].astype(BF)
+
+
+def block_kernel(x_hbm, gy_hbm, g1_hbm, be1_hbm, g2_hbm, be2_hbm, bo_hbm, bd_hbm, bqkv_hbm, bup_hbm,
+                 wqkv_hbm, wout_hbm, wup_hbm, wdn_hbm,
+                 y_ref, vec_ref, gwup_ref, gwdn_ref, gqkv_ref, h_ref, ctx_ref, gmid_ref, mine_ref, xh_ref, gm_ref, rs_ref, g1_out, r_hs, ln_hs,
+                 wqkv, wout, xf, gm_f, gg_f, xhat, rstd_s, probs, qkvT, par, mp,
+                 wup, wdn, xg, gyg, biasT, a_ps, a_pr, a_hs, a_hr, a_cr, a_fr, b_ps, b_pr, b_hs, b_hr, b_cr, b_fr,
+                 gact, g_ref, gpre_ref, act_ref, gyf_ref, bqkv_ref, g1_in, be1_in, g2_in, be2_in, bo_in, bd_in, bup_in,
+                 rp, m_pr, m_hs, m_cr, r_pr, ln_x,
+                 wsem, ssem, rsem, isem):
+    t, pt, ct, qt, half = places()
+    send, started = sender(ssem, rsem)
 
     in_x = pltpu.make_async_copy(x_hbm, xg.at[t], isem.at[0])
     in_gy = pltpu.make_async_copy(gy_hbm, gyg.at[t], isem.at[1])
@@ -153,7 +170,7 @@
     j_f = j_pos.astype(F32)
 
     def head(h, e):
-        return qkvT[(h * 3 + e) * HD:(h * 3 + e + 1) * HD, :]
+        return qkvT[head_rows(h, e), :]
 
     for h in range(HL):
         slope = jnp.where(t == 0, slopes[h], jnp.where(t == 1, slopes[HL + h], jnp.where(t == 2, slopes[2 * HL + h], slopes[3 * HL + h]))).astype(F32)
@@ -164,19 +181,21 @@
         probs[h] = p
         ctx_ref[h * HD:(h + 1) * HD, :] = dot(head(h, 2), p.astype(BF), 1, 0).astype(BF)
 
-    def exchange(part, ps, pr, hs, hr, cr):
+    def exchange(part, groups, ps, pr, hs, hr, cr):
         firsts = []
-        theirs = part(1 - half)
-        for k in range(HCH):
-            ps[k] = theirs[:, k * CW:(k + 1) * CW].astype(BF)
-            firsts.append(send(ps.at[k], pr.at[k], pt))
-        ours = part(half)
+        for k0, k1 in groups:
+            theirs = part(1 - half, k0 * CW, k1 * CW)
+            for k in range(k0, k1):
+                ps[k] = theirs[:, (k - k0) * CW:(k - k0 + 1) * CW].astype(BF)
+                firsts.append(send(ps.at[k], pr.at[k], pt))
         outs = []
-        for k in range(HCH):
-            own = ours[:, k * CW:(k + 1) * CW]
-            firsts[k].wait_recv()
-            hs[k] = (own + pr[k].astype(F32)).astype(BF)
-            outs.append((send(hs.at[k], cr.at[k], ct), send(hs.at[k], hr.at[k], pt)))
+        for k0, k1 in groups:
+            ours = part(half, k0 * CW, k1 * CW)
+            for k in range(k0, k1):
+                own = ours[:, (k - k0) * CW:(k - k0 + 1) * CW]
+                firsts[k].wait_recv()
+                hs[k] = (own + pr[k].astype(F32)).astype(BF)
+                outs.append((send(hs.at[k], cr.at[k], ct), send(hs.at[k], hr.at[k], pt)))
         return outs
 
     def forward(outs, cr, fr):
@@ -189,7 +208,7 @@
     for c in w_cps['out']:
         c.wait()
     ctxT = ctx_ref[...]
-    a_outs = exchange(lambda kk: dot(ctxT, wout[kk], 0, 0), a_ps, a_pr, a_hs, a_hr, a_cr)
+    a_outs = exchange(lambda hh, c0, c1: dot(ctxT, wout[hh, :, c0:c1], 0, 0), ((0, HCH),), a_ps, a_pr, a_hs, a_hr, a_cr)
 
     y_p.wait_recv()
     y_f.wait_recv()
@@ -236,34 +255,28 @@
 
     gprev = gpre_ref[...]
 
-    def part_g(kk):
-        return dot(gprev, wup[pl.ds(pl.multiple_of(kk * HW, HW), HW), :], 1, 1)
-
-    g_outs = exchange(part_g, b_ps, b_pr, b_hs, b_hr, b_cr)
-
-    def scatter_first(part, buf, pr):
-        for n in range(NCH):
-            cols = slice(n * CW, (n + 1) * CW)
-            v = part(n)
-            for i in range(TP):
-                buf[i, :, cols] = v[i * SL:(i + 1) * SL, :].astype(BF)
-        return (send(buf.at[qt], pr.at[1], pt), send(buf.at[pt], pr.at[0], pt))
+    def part_g(hh, c0, c1):
+        return dot(gprev, wup[pl.ds(pl.multiple_of(hh * HW + c0, CW), c1 - c0), :], 1, 1)
+
+    g_outs = exchange(part_g, ((0, 1), (1, HCH)), b_ps, b_pr, b_hs, b_hr, b_cr)
 
     actv = act_ref[...]
-    m_first = scatter_first(lambda n: dot(actv, wdn[:, n * CW:(n + 1) * CW], 1, 0), ghp.at[0], m_pr)
-
+    for n in range(NCH):
+        cols = slice(n * CW, (n + 1) * CW)
+        row_blocks(mp, cols, dot(actv, wdn[:, cols], 1, 0))
+    m_first = (send(mp.at[qt], m_pr.at[1], pt), send(mp.at[pt], m_pr.at[0], pt))
     for n in range(NCH):
         gwdn_ref[n * CW:(n + 1) * CW, :] = dot(act_ref[:, n * CW:(n + 1) * CW], gyv, 0, 0).astype(BF)
-
-    m_first[0].wait_recv()
-    m_hs[...] = (ghp[0, ct].astype(F32) + m_pr[1].astype(F32)).astype(BF)
-    m_out = send(m_hs, m_cr, ct)
     g_fwd = []
     for k in range(HCH):
         g_outs[k][0].wait_recv()
         g_fwd.append(send(b_cr.at[k], b_fr.at[k], pt))
         for n in range(2 * k, 2 * k + 2):
             gwup_ref[n * CW:(n + 1) * CW, :] = dot(g_ref[:, n * CW:(n + 1) * CW], gprev, 0, 0).astype(BF)
+
+    m_first[0].wait_recv()
+    m_hs[...] = (mp[ct].astype(F32) + m_pr[1].astype(F32)).astype(BF)
+    m_out = send(m_hs, m_cr, ct)
 
     def put_g(kk, val):
         gg_f[:, pl.ds(pl.multiple_of(kk * CW, CW), CW)] = val
@@ -301,82 +314,97 @@
     gks = [(dot(head(h, 0), gss[h], 1, 1) * scale).astype(BF) for h in heads]
     for h in heads:
         for e, val in enumerate((gqs[h], gks[h], gvs[h])):
-            gqkv_ref[(h * 3 + e) * HD:(h * 3 + e + 1) * HD, :] = val
+            gqkv_ref[head_rows(h, e), :] = val
 
     gqv = gqkv_ref[...]
-
-    ln_s, ln_pr, ln_hs, ln_cr = ln_x.at[0], ln_x.at[1], ln_x.at[2], ln_x.at[3]
-    r_first = scatter_first(lambda n: dot(gqv, wqkv[:, n * CW:(n + 1) * CW], 0, 0), ghp.at[1], r_pr)
-    gg1 = jnp.zeros((1, D), F32)
-    gb1 = jnp.zeros((1, D), F32)
-    for i in range(TP):
-        v = ghp[1, i].astype(F32)
-        gg1 = gg1 + jnp.sum(v * xhat[i * SL:(i + 1) * SL, :], axis=0, keepdims=True)
-        gb1 = gb1 + jnp.sum(v, axis=0, keepdims=True)
-    ln_s[0:1, :] = gg1
-    ln_s[1:2, :] = gb1
+    r_first = []
+    for k in range(2):
+        row_blocks(rp.at[k], slice(0, HW), dot(gqv, wqkv[:, k * HW:(k + 1) * HW], 0, 0))
+        r_first.append((send(rp.at[k, qt], r_pr.at[k, 1], pt), send(rp.at[k, pt], r_pr.at[k, 0], pt)))
+
+    ln_s, ln_pr = ln_x.at[0], ln_x.at[1]
+    for k in range(2):
+        cols = slice(k * HW, (k + 1) * HW)
+        gg1 = jnp.zeros((1, HW), F32)
+        gb1 = jnp.zeros((1, HW), F32)
+        for i in range(TP):
+            v = rp[k, i].astype(F32)
+            gg1 = gg1 + jnp.sum(v * xhat[i * SL:(i + 1) * SL, cols], axis=0, keepdims=True)
+            gb1 = gb1 + jnp.sum(v, axis=0, keepdims=True)
+        ln_s[0:1, cols] = gg1
+        ln_s[1:2, cols] = gb1
     l_first = send(ln_s, ln_pr, pt)
 
-    r_first[0].wait_recv()
-    r_hs[...] = (ghp[1, ct].astype(F32) + r_pr[1].astype(F32)).astype(BF)
-    r_out = send(r_hs, r_cr, ct)
+    own = pl.ds(pl.multiple_of(t * SL, 8), SL)
+    xh_ref[...] = xhat[own, :]
+    gm_ref[...] = gm_f[own, :]
+    rs_ref[...] = rstd_s[own, :]
+    g1_out[...] = par[0:1, :]
+
+    for k in range(2):
+        cols = slice(k * HW, (k + 1) * HW)
+        r_first[k][0].wait_recv()
+        r_hs[:, cols] = (rp[k, ct].astype(F32) + r_pr[k, 1].astype(F32)).astype(BF)
+        r_first[k][1].wait_recv()
+        mine_ref[:, cols] = (rp[k, t].astype(F32) + r_pr[k, 0].astype(F32)).astype(BF)
     l_first.wait_recv()
     ln_hs[...] = ln_s[...] + ln_pr[...]
-    l_out = send(ln_hs, ln_cr, ct)
-
-    ones = jnp.ones((8, S), BF)
-    for h in heads:
-        for e in range(3):
-            gbqkv_ref[e, h:h + 1, :] = dot(ones, gqkv_ref[(h * 3 + e) * HD:(h * 3 + e + 1) * HD, :], 1, 1)[0:1, :]
-    gwout_ref[...] = dot(ctx_ref[...], gmv, 1, 0).astype(BF)
-    for h in range(HL):
-        rows = slice(h * 3 * HD, (h + 1) * 3 * HD)
-        gwqkv_ref[rows, :] = dot(gqkv_ref[rows, :], h_ref[...], 1, 0).astype(BF)
-    own = pl.ds(pl.multiple_of(t * SL, 8), SL)
     m_first[1].wait_recv()
     m_out.wait_recv()
-    m_sum = (ghp[0, t].astype(F32) + m_pr[0].astype(F32)).astype(BF).astype(F32) + m_cr[...].astype(F32)
+    m_sum = (mp[t].astype(F32) + m_pr[0].astype(F32)).astype(BF).astype(F32) + m_cr[...].astype(F32)
     y_ref[...] = (xf[own, :] + m_sum.astype(BF).astype(F32) + bd_ref[...]).astype(BF)
-
-    r_first[1].wait_recv()
-    mine = (ghp[1, t].astype(F32) + r_pr[0].astype(F32)).astype(BF).astype(F32)
-    r_out.wait_recv()
-    gh = (mine + r_cr[...].astype(F32)).astype(BF).astype(F32)
-    xh = xhat[own, :]
+    for c in started:
+        c.wait_send()
+
+
+N_SEND = 6 + 12 + 12 + 3 + 4 + 1
+VMEM_A = 36 * 2**20
+VMEM_B = 8 * 2**20
+VMEM_C = 4 * 2**20
+
+
+def write_kernel(yi_ref, vec_ref, up_ref, dn_ref, gqkv_ref, h_ref, ctx_ref, gmid_ref,
+                 y_ref, gwqkv_ref, gbqkv_ref, gwout_ref, gbo_ref, gl2_ref, bl2_ref, gwup_ref, gbup_ref, gwdn_ref, gbd_ref,
+                 s_qkv, s_out, sem):
+    cps = []
+
+    def out(src, dst, n=1):
+        rows = src.shape[0] // n
+        for k in range(n):
+            c = pltpu.make_async_copy(src.at[pl.ds(k * rows, rows)], dst.at[pl.ds(k * rows, rows)], sem.at[len(cps)])
+            c.start()
+            cps.append(c)
+
+    out(dn_ref, gwdn_ref, 4)
+    out(up_ref, gwup_ref, 4)
+    hv = h_ref[...]
+    s_out[...] = dot(ctx_ref[...], gmid_ref[...], 1, 0).astype(BF)
+    out(s_out, gwout_ref)
+    for n in range(HL):
+        rows = slice(n * 3 * HD, (n + 1) * 3 * HD)
+        s_qkv[rows, :] = dot(gqkv_ref[rows, :], hv, 1, 0).astype(BF)
+        out(s_qkv.at[rows], gwqkv_ref.at[rows])
+    y_ref[...] = yi_ref[...]
+    ones = jnp.ones((8, S), BF)
+    for h in range(HL):
+        for e in range(3):
+            gbqkv_ref[e, h:h + 1, :] = dot(ones, gqkv_ref[head_rows(h, e), :], 1, 1)[0:1, :]
+    for i, r in enumerate((gbd_ref, gbup_ref, gl2_ref, bl2_ref, gbo_ref)):
+        r[...] = vec_ref[i, :]
+    for c in cps:
+        c.wait()
+
+
+def last_kernel(mine_ref, xh_ref, gm_ref, rs_ref, g1_ref, rc_ref, ln_ref, lc_ref, gx_ref, gl1_ref, bl1_ref):
+    gh = (mine_ref[...].astype(F32) + rc_ref[...].astype(F32)).astype(BF).astype(F32)
+    xh = xh_ref[...]
     dxh = gh * g1_ref[...]
     m1 = jnp.mean(dxh, axis=-1, keepdims=True)
     m2 = jnp.mean(dxh * xh, axis=-1, keepdims=True)
-    gx_ref[...] = (gm_f[own, :] + rstd_s[own, 0:1] * (dxh - m1 - xh * m2)).astype(BF)
-    l_out.wait_recv()
-    vec_ref[6:8, :] = ln_hs[...] + ln_cr[...]
-    for c in started:
-        c.wait_send()
-
-
-N_SEND = 38
-VMEM_A = 34 * 2**20
-VMEM_B = 8 * 2**20
-
-
-def write_kernel(yi_ref, gxi_ref, vec_ref, gbi_ref, qkv_ref, out_ref, up_ref, dn_ref,
-                 y_ref, gx_ref, gl1_ref, bl1_ref, gwqkv_ref, gbqkv_ref, gwout_ref, gbo_ref, gl2_ref, bl2_ref,
-                 gwup_ref, gbup_ref, gwdn_ref, gbd_ref, sem):
-    cps = []
-    for src, dst in ((dn_ref, gwdn_ref), (up_ref, gwup_ref), (qkv_ref, gwqkv_ref), (out_ref, gwout_ref)):
-        rows = src.shape[0] // 4
-        for k in range(4):
-            part = pl.ds(k * rows, rows)
-            c = pltpu.make_async_copy(src.at[part], dst.at[part], sem.at[len(cps)])
-            c.start()
-            cps.append(c)
-    y_ref[...] = yi_ref[...]
-    gx_ref[...] = gxi_ref[...]
-    gbqkv_ref[...] = gbi_ref[...]
-    for i, r in enumerate((gbd_ref, gbup_ref, gl2_ref, bl2_ref, gbo_ref, None, gl1_ref, bl1_ref)):
-        if r is not None:
-            r[...] = vec_ref[i, :]
-    for c in cps:
-        c.wait()
+    gx_ref[...] = (gm_ref[...] + rs_ref[:, 0:1] * (dxh - m1 - xh * m2)).astype(BF)
+    ln = ln_ref[...] + lc_ref[...]
+    gl1_ref[...] = ln[0, :]
+    bl1_ref[...] = ln[1, :]
 
 
 def solution(mesh):
@@ -390,24 +418,25 @@
         wq = jnp.transpose(w_qkv, (1, 2, 3, 0)).reshape(3 * HL * HD, D)
         bq = jnp.transpose(b_qkv, (1, 0, 2))
         part = pltpu.VMEM((HCH, S, CW), BF)
+        vec1 = sds((D,), F32)
         mids = pl.pallas_call(
             block_kernel,
-            out_shape=(pltpu.VMEM((SL, D), BF), pltpu.VMEM((SL, D), BF), pltpu.VMEM((8, D), F32), pltpu.VMEM((3, HL, HD), F32),
-                       pltpu.VMEM((3 * HL * HD, D), BF), pltpu.VMEM((HL * HD, D), BF), pltpu.VMEM((D, FL), BF), pltpu.VMEM((FL, D), BF)),
+            out_shape=(pltpu.VMEM((SL, D), BF), pltpu.VMEM((8, D), F32), pltpu.VMEM((D, FL), BF), pltpu.VMEM((FL, D), BF),
+                       pltpu.VMEM((3 * HL * HD, S), BF), pltpu.VMEM((S, D), BF), pltpu.VMEM((HL * HD, S), BF), pltpu.VMEM((S, D), BF),
+                       pltpu.VMEM((SL, D), BF), pltpu.VMEM((SL, D), F32), pltpu.VMEM((SL, D), F32), pltpu.VMEM((SL, 128), F32),
+                       pltpu.VMEM((1, D), F32), sds((SL, D), BF), sds((2, D), F32)),
             in_specs=[ANY] * 14,
-            out_specs=(VM,) * 8,
+            out_specs=(VM,) * 15,
             scratch_shapes=[
-                pltpu.VMEM((S, D), BF), pltpu.VMEM((3 * HL * HD, S), BF), pltpu.VMEM((HL * HD, S), BF), pltpu.VMEM((S, D), BF),
-                pltpu.VMEM((S, D), BF), pltpu.VMEM((S, FL), BF), pltpu.VMEM((S, FL), BF), pltpu.VMEM((S, D), BF),
-                pltpu.VMEM((3 * HL * HD, D), BF), pltpu.VMEM((2, HL * HD, HW), BF), pltpu.VMEM((D, FL), BF), pltpu.VMEM((FL, D), BF),
-                pltpu.VMEM((TP, SL, D), BF), pltpu.VMEM((TP, SL, D), BF), pltpu.VMEM((S, D), F32), pltpu.VMEM((S, D), F32),
-                pltpu.VMEM((S, 128), F32), pltpu.VMEM((3 * HL * HD, S), F32), pltpu.VMEM((3 * HL * HD, S), BF), pltpu.VMEM((HL, S, S), F32),
-                *[part] * 12,
-                pltpu.VMEM((S, FL), BF), pltpu.VMEM((2, TP, SL, D), BF),
-                pltpu.VMEM((2, SL, D), BF), pltpu.VMEM((SL, D), BF), pltpu.VMEM((SL, D), BF),
-                pltpu.VMEM((2, SL, D), BF), pltpu.VMEM((SL, D), BF), pltpu.VMEM((SL, D), BF),
-                pltpu.VMEM((S, D), F32), pltpu.VMEM((4, 2, D), F32), pltpu.VMEM((S, D), F32), pltpu.VMEM((8, D), F32),
+                pltpu.VMEM((3 * HL * HD, D), BF), pltpu.VMEM((2, HL * HD, HW), BF), pltpu.VMEM((S, D), F32), pltpu.VMEM((S, D), F32),
+                pltpu.VMEM((S, D), F32), pltpu.VMEM((S, D), F32), pltpu.VMEM((S, 128), F32), pltpu.VMEM((HL, S, S), F32),
+                pltpu.VMEM((3 * HL * HD, S), BF), pltpu.VMEM((8, D), F32), pltpu.VMEM((TP, SL, D), BF),
+                pltpu.VMEM((D, FL), BF), pltpu.VMEM((FL, D), BF), pltpu.VMEM((TP, SL, D), BF), pltpu.VMEM((TP, SL, D), BF),
+                pltpu.VMEM((3 * HL * HD, S), F32), *[part] * 12,
+                pltpu.VMEM((S, FL), BF), pltpu.VMEM((S, D), BF), pltpu.VMEM((S, FL), BF), pltpu.VMEM((S, FL), BF), pltpu.VMEM((S, D), BF),
                 pltpu.VMEM((3, HL, HD), F32), *[pltpu.VMEM((D,), F32) for _ in range(7)],
+                pltpu.VMEM((2, TP, SL, HW), BF), pltpu.VMEM((2, SL, D), BF), pltpu.VMEM((SL, D), BF), pltpu.VMEM((SL, D), BF),
+                pltpu.VMEM((2, 2, SL, HW), BF), pltpu.VMEM((2, 2, D), F32),
                 pltpu.SemaphoreType.DMA((9,)), pltpu.SemaphoreType.DMA((N_SEND,)), pltpu.SemaphoreType.DMA((N_SEND,)),
                 pltpu.SemaphoreType.DMA((10,)),
             ],
@@ -415,18 +444,29 @@
             name='block',
         )(*(pltpu.with_memory_space_constraint(v, pltpu.HBM) for v in (
             x.reshape(SL, D), grad_y.reshape(SL, D), g1, be1, g2, be2, b_out, b_down, bq, b_up, wq, w_out, w_up, w_down)))
-        vec1 = sds((D,), F32)
-        outs = pl.pallas_call(
+        mine, xh, gm, rs, g1v, r_hs, ln_hs = mids[8:]
+        across = [(i, TP - 1 - i) for i in range(TP)]
+        r_cr = lax.ppermute(r_hs, 'tp', across)
+        ln_cr = lax.ppermute(ln_hs, 'tp', across)
+        y, gwqkv, gbqkv, gwout, gbo, gl2, bl2, gwup, gbup, gwdn, gbd = pl.pallas_call(
             write_kernel,
-            out_shape=(sds((SL, D), BF), sds((SL, D), BF), vec1, vec1, sds((3 * HL * HD, D), BF), sds((3, HL, HD), F32),
-                       sds((HL * HD, D), BF), vec1, vec1, vec1, sds((D, FL), BF), vec1, sds((FL, D), BF), vec1),
+            out_shape=(sds((SL, D), BF), sds((3 * HL * HD, D), BF), sds((3, HL, HD), F32), sds((HL * HD, D), BF), vec1, vec1, vec1,
+                       sds((D, FL), BF), vec1, sds((FL, D), BF), vec1),
             in_specs=[VM] * 8,
-            out_specs=(VM, VM, VM, VM, ANY, VM, ANY, VM, VM, VM, ANY, VM, ANY, VM),
-            scratch_shapes=[pltpu.SemaphoreType.DMA((16,))],
+            out_specs=(VM, ANY, VM, ANY, VM, VM, VM, ANY, VM, ANY, VM),
+            scratch_shapes=[pltpu.VMEM((3 * HL * HD, D), BF), pltpu.VMEM((HL * HD, D), BF), pltpu.SemaphoreType.DMA((16,))],
             compiler_params=pltpu.CompilerParams(vmem_limit_bytes=VMEM_B),
+            cost_estimate=pl.CostEstimate(flops=600_000_000, bytes_accessed=14_200_000, transcendentals=0),
             name='write',
-        )(*mids)
-        (y, gx, gl1, bl1, gwqkv, gbqkv, gwout, gbo, gl2, bl2, gwup, gbup, gwdn, gbd) = outs
+        )(*mids[:8])
+        gx, gl1, bl1 = pl.pallas_call(
+            last_kernel,
+            out_shape=(sds((SL, D), BF), vec1, vec1),
+            in_specs=[VM] * 8,
+            out_specs=(VM,) * 3,
+            compiler_params=pltpu.CompilerParams(vmem_limit_bytes=VMEM_C),
+            name='last',
+        )(mine, xh, gm, rs, g1v, r_cr, ln_hs, ln_cr)
         gwqkv = jnp.transpose(gwqkv.reshape(HL, 3, HD, D), (3, 0, 1, 2))
         gbqkv = jnp.transpose(gbqkv, (1, 0, 2))
         return (y.reshape(1, SL, D), gx.reshape(1, SL, D), gl1, bl1, gwqkv, gbqkv, gwout, gbo, gl2, bl2, gwup, gbup, gwdn, gbd)

time: 41.8 us -> 39.8 us (0.952)
  Pallas kernels: 41 us -> 37.3 us
  starting transfers between devices: 0 us -> 1.77 us
    pallas_call x1, Pallas kernels: 35.2 us -> 30.6 us  [local_step(): pl.pallas_call(block_kernel, out_shape=(pltpu.VMEM((SL, D), BF), pltpu.VM...]
    ppermute x0 -> x2, starting transfers between devices: none -> 1.77 us  [the longest x1 1.34 us: local_step(): r_cr = lax.ppermute(r_hs, 'tp', across)]
    pallas_call x1 -> x2, Pallas kernels: 5.84 us -> 6.68 us  [the longest x1 5.9 us: local_step(): pl.pallas_call(write_kernel, out_shape=(sds((SL, D), BF), sds((3 * HL * H...]
  transfers between devices with their start and end apart: 0 -> 2, of which waited for: 0 -> 0; matrix products, arithmetic and copies ran while one was open for 0% -> 0% of each run, Pallas kernels for 0% -> 15%
where the time goes in v5:
time: 39.8 us; the launch traced here: 39.7 us
  Pallas kernels  37.3 us (94%)
  starting transfers between devices  1.77 us (4%)
  between operations  0.68 us (2%)
    pallas_call x1, Pallas kernels, local_step(): pl.pallas_call(block_kernel, out_shape=(pltpu.VMEM((SL, D), BF), pltpu.VM...  30.6 us
    pallas_call x1, Pallas kernels, local_step(): pl.pallas_call(write_kernel, out_shape=(sds((SL, D), BF), sds((3 * HL * H...  5.9 us
    ppermute x1, starting transfers between devices, local_step(): r_cr = lax.ppermute(r_hs, 'tp', across)  1.34 us
  transfers between devices with their start and end apart: 2, of which 0 were waited for; matrix products, arithmetic and copies ran while one was open for 0% of the time, Pallas kernels for 15%

profile of v5, /device:TPU:0, one launch (start us, length us, event | category | flops | bytes accessed | tf_op | source)
XLA Modules:
  0.0 39.7 jit_solution(5408106516299060740)
XLA Ops:
  0.7 30.6 %block.1 = (bf16[24,1536]{1,0:T(8,128)(2,1)S(1)}, f32[8,1536]{1,0:T(8,128)S(1)}, bf16[1536,1536]{1,0:T(8,128)(2,1)S(1)}, bf16[1536,1536]{1,0:T(8,128)(2,1)S(1)},...) custom-call(bf16[24,1536]{1,0:T(8,128)(2,1)} %bitcast.13, ...), custom_call_target="tpu_custom_call" | custom-call | tf_op jit(solution)/shard_map/block/pallas_call | solution.py:422
  31.3 1.3 %collective-permute-start = (bf16[24,1536]{1,0:T(8,128)(2,1)S(1)}, bf16[24,1536]{1,0:T(8,128)(2,1)S(1)}, u32[]{:S(2)}, u32[]{:S(2)}) collective-permute-start(bf16[24,1536]{1,0:T(8,128)(2,1)S(1)} %get-tuple-element.57), channel_id=1, source_target_pairs={{0,3},{1,2},{2,1},{3,0},{4,7},{5,6},{6,5},{7,4}} | collective-permute-start | bytes 221192 | tf_op jit(solution)/shard_map/ppermute | solution.py:449
  32.6 0.4 %collective-permute-start.1 = (f32[2,1536]{1,0:T(2,128)S(1)}, f32[2,1536]{1,0:T(2,128)S(1)}, u32[]{:S(2)}, u32[]{:S(2)}) collective-permute-start(f32[2,1536]{1,0:T(2,128)S(1)} %get-tuple-element.58.ln_ref), channel_id=1, source_target_pairs={{0,3},{1,2},{2,1},{3,0},{4,7},{5,6},{6,5},{7,4}} | collective-permute-start | bytes 36872 | tf_op jit(solution)/shard_map/ppermute | solution.py:450
  33.0 5.9 %write.1 = (bf16[24,1536]{1,0:T(8,128)(2,1)}, bf16[1152,1536]{1,0:T(8,128)(2,1)}, f32[3,4,96]{2,1,0:T(4,128)}, bf16[384,1536]{1,0:T(8,128)(2,1)}, f32[1536]{0:T(...) custom-call(bf16[24,1536]{1,0:T(8,128)(2,1)S(1)} %get-tuple-element., ...), custom_call_target="tpu_custom_call" | custom-call | flops 600000000 | bytes 14200000 | tf_op jit(solution)/shard_map/write/pallas_call | solution.py:451
  38.9 0.0 collective-permute-done.1.lc_ref
  38.9 0.0 collective-permute-done.rc_ref
  39.0 0.8 %last.1 = (bf16[24,1536]{1,0:T(8,128)(2,1)}, f32[1536]{0:T(1024)}, f32[1536]{0:T(1024)}) custom-call(bf16[24,1536]{1,0:T(8,128)(2,1)S(1)} %get-tuple-element.52.mine_ref, f32[24,1536]{1,0:T(8,128)S(1)} %get-tuple-element.53.xh_ref, f32[24,1536]{1,0:T(8,128)S(1)} %get-tuple-element.54.gm_ref, f32[24,128]{1,0:T(8,128)S(1)} %get-tuple-element.55.rs_ref, ...), custom_call_target="tpu_custom_call" | custom-call | tf_op jit(solution)/shard_map/last/pallas_call | solution.py:462
Async XLA Ops:
  31.3 7.7 %collective-permute-start = (bf16[24,1536]{1,0:T(8,128)(2,1)S(1)}, bf16[24,1536]{1,0:T(8,128)(2,1)S(1)}, u32[]{:S(2)}, u32[]{:S(2)}) collective-permute-start(bf16[24,1536]{1,0:T(8,128)(2,1)S(1)} %get-tuple-element.57), channel_id=1, source_target_pairs={{0,3},{1,2},{2,1},{3,0},{4,7},{5,6},{6,5},{7,4}} | collective-permute-start | bytes 221192 | tf_op jit(solution)/shard_map/ppermute | solution.py:449
  32.6 6.3 %collective-permute-start.1 = (f32[2,1536]{1,0:T(2,128)S(1)}, f32[2,1536]{1,0:T(2,128)S(1)}, u32[]{:S(2)}, u32[]{:S(2)}) collective-permute-start(f32[2,1536]{1,0:T(2,128)S(1)} %get-tuple-element.58.ln_ref), channel_id=1, source_target_pairs={{0,3},{1,2},{2,1},{3,0},{4,7},{5,6},{6,5},{7,4}} | collective-permute-start | bytes 36872 | tf_op jit(solution)/shard_map/ppermute | solution.py:450

commit v6 on v5

--- a/solution.py
+++ b/solution.py
@@ -344,11 +344,17 @@
     for k in range(2):
         cols = slice(k * HW, (k + 1) * HW)
         r_first[k][0].wait_recv()
-        r_hs[:, cols] = (rp[k, ct].astype(F32) + r_pr[k, 1].astype(F32)).astype(BF)
+        r_hs[0:SL, cols] = (rp[k, ct].astype(F32) + r_pr[k, 1].astype(F32)).astype(BF)
         r_first[k][1].wait_recv()
         mine_ref[:, cols] = (rp[k, t].astype(F32) + r_pr[k, 0].astype(F32)).astype(BF)
     l_first.wait_recv()
-    ln_hs[...] = ln_s[...] + ln_pr[...]
+    ln = ln_s[...] + ln_pr[...]
+    ln_hs[...] = ln
+    ln_rows = []
+    for _ in range(3):
+        ln_rows.append(ln.astype(BF).astype(F32))
+        ln = ln - ln_rows[-1]
+    r_hs[SL:SL + 8, :] = jnp.concatenate(ln_rows + [jnp.zeros((2, D), F32)], axis=0).astype(BF)
     m_first[1].wait_recv()
     m_out.wait_recv()
     m_sum = (mp[t].astype(F32) + m_pr[0].astype(F32)).astype(BF).astype(F32) + m_cr[...].astype(F32)
@@ -365,7 +371,7 @@
 
 def write_kernel(yi_ref, vec_ref, up_ref, dn_ref, gqkv_ref, h_ref, ctx_ref, gmid_ref,
                  y_ref, gwqkv_ref, gbqkv_ref, gwout_ref, gbo_ref, gl2_ref, bl2_ref, gwup_ref, gbup_ref, gwdn_ref, gbd_ref,
-                 s_qkv, s_out, sem):
+                 s_qkv, s_out, s_gb, s0, s1, s2, s3, s4, sem):
     cps = []
 
     def out(src, dst, n=1):
@@ -377,6 +383,15 @@
 
     out(dn_ref, gwdn_ref, 4)
     out(up_ref, gwup_ref, 4)
+    out(yi_ref, y_ref)
+    for i, (sv, r) in enumerate(((s0, gbd_ref), (s1, gbup_ref), (s2, gl2_ref), (s3, bl2_ref), (s4, gbo_ref))):
+        sv[...] = vec_ref[i, :]
+        out(sv, r)
+    ones = jnp.ones((8, S), BF)
+    for h in range(HL):
+        for e in range(3):
+            s_gb[e, h:h + 1, :] = dot(ones, gqkv_ref[head_rows(h, e), :], 1, 1)[0:1, :]
+    out(s_gb, gbqkv_ref)
     hv = h_ref[...]
     s_out[...] = dot(ctx_ref[...], gmid_ref[...], 1, 0).astype(BF)
     out(s_out, gwout_ref)
@@ -384,25 +399,19 @@
         rows = slice(n * 3 * HD, (n + 1) * 3 * HD)
         s_qkv[rows, :] = dot(gqkv_ref[rows, :], hv, 1, 0).astype(BF)
         out(s_qkv.at[rows], gwqkv_ref.at[rows])
-    y_ref[...] = yi_ref[...]
-    ones = jnp.ones((8, S), BF)
-    for h in range(HL):
-        for e in range(3):
-            gbqkv_ref[e, h:h + 1, :] = dot(ones, gqkv_ref[head_rows(h, e), :], 1, 1)[0:1, :]
-    for i, r in enumerate((gbd_ref, gbup_ref, gl2_ref, bl2_ref, gbo_ref)):
-        r[...] = vec_ref[i, :]
     for c in cps:
         c.wait()
 
 
-def last_kernel(mine_ref, xh_ref, gm_ref, rs_ref, g1_ref, rc_ref, ln_ref, lc_ref, gx_ref, gl1_ref, bl1_ref):
-    gh = (mine_ref[...].astype(F32) + rc_ref[...].astype(F32)).astype(BF).astype(F32)
+def last_kernel(mine_ref, xh_ref, gm_ref, rs_ref, g1_ref, rc_ref, ln_ref, gx_ref, gl1_ref, bl1_ref):
+    gh = (mine_ref[...].astype(F32) + rc_ref[0:SL, :].astype(F32)).astype(BF).astype(F32)
     xh = xh_ref[...]
     dxh = gh * g1_ref[...]
     m1 = jnp.mean(dxh, axis=-1, keepdims=True)
     m2 = jnp.mean(dxh * xh, axis=-1, keepdims=True)
     gx_ref[...] = (gm_ref[...] + rs_ref[:, 0:1] * (dxh - m1 - xh * m2)).astype(BF)
-    ln = ln_ref[...] + lc_ref[...]
+    lc = rc_ref[SL:SL + 8, :].astype(F32)
+    ln = ln_ref[...] + (lc[0:2, :] + lc[2:4, :] + lc[4:6, :])
     gl1_ref[...] = ln[0, :]
     bl1_ref[...] = ln[1, :]
 
@@ -424,7 +433,7 @@
             out_shape=(pltpu.VMEM((SL, D), BF), pltpu.VMEM((8, D), F32), pltpu.VMEM((D, FL), BF), pltpu.VMEM((FL, D), BF),
                        pltpu.VMEM((3 * HL * HD, S), BF), pltpu.VMEM((S, D), BF), pltpu.VMEM((HL * HD, S), BF), pltpu.VMEM((S, D), BF),
                        pltpu.VMEM((SL, D), BF), pltpu.VMEM((SL, D), F32), pltpu.VMEM((SL, D), F32), pltpu.VMEM((SL, 128), F32),
-                       pltpu.VMEM((1, D), F32), sds((SL, D), BF), sds((2, D), F32)),
+                       pltpu.VMEM((1, D), F32), sds((SL + 8, D), BF), pltpu.VMEM((2, D), F32)),
             in_specs=[ANY] * 14,
             out_specs=(VM,) * 15,
             scratch_shapes=[
@@ -447,14 +456,14 @@
         mine, xh, gm, rs, g1v, r_hs, ln_hs = mids[8:]
         across = [(i, TP - 1 - i) for i in range(TP)]
         r_cr = lax.ppermute(r_hs, 'tp', across)
-        ln_cr = lax.ppermute(ln_hs, 'tp', across)
         y, gwqkv, gbqkv, gwout, gbo, gl2, bl2, gwup, gbup, gwdn, gbd = pl.pallas_call(
             write_kernel,
             out_shape=(sds((SL, D), BF), sds((3 * HL * HD, D), BF), sds((3, HL, HD), F32), sds((HL * HD, D), BF), vec1, vec1, vec1,
                        sds((D, FL), BF), vec1, sds((FL, D), BF), vec1),
             in_specs=[VM] * 8,
-            out_specs=(VM, ANY, VM, ANY, VM, VM, VM, ANY, VM, ANY, VM),
-            scratch_shapes=[pltpu.VMEM((3 * HL * HD, D), BF), pltpu.VMEM((HL * HD, D), BF), pltpu.SemaphoreType.DMA((16,))],
+            out_specs=(ANY,) * 11,
+            scratch_shapes=[pltpu.VMEM((3 * HL * HD, D), BF), pltpu.VMEM((HL * HD, D), BF), pltpu.VMEM((3, HL, HD), F32),
+                            *[pltpu.VMEM((D,), F32) for _ in range(5)], pltpu.SemaphoreType.DMA((20,))],
             compiler_params=pltpu.CompilerParams(vmem_limit_bytes=VMEM_B),
             cost_estimate=pl.CostEstimate(flops=600_000_000, bytes_accessed=14_200_000, transcendentals=0),
             name='write',
@@ -462,11 +471,11 @@
         gx, gl1, bl1 = pl.pallas_call(
             last_kernel,
             out_shape=(sds((SL, D), BF), vec1, vec1),
-            in_specs=[VM] * 8,
+            in_specs=[VM] * 7,
             out_specs=(VM,) * 3,
             compiler_params=pltpu.CompilerParams(vmem_limit_bytes=VMEM_C),
             name='last',
-        )(mine, xh, gm, rs, g1v, r_cr, ln_hs, ln_cr)
+        )(mine, xh, gm, rs, g1v, r_cr, ln_hs)
         gwqkv = jnp.transpose(gwqkv.reshape(HL, 3, HD, D), (3, 0, 1, 2))
         gbqkv = jnp.transpose(gbqkv, (1, 0, 2))
         return (y.reshape(1, SL, D), gx.reshape(1, SL, D), gl1, bl1, gwqkv, gbqkv, gwout, gbo, gl2, bl2, gwup, gbup, gwdn, gbd)

time: 39.8 us -> 38.8 us (0.975)
  Pallas kernels: 37.3 us -> 36.6 us
  starting transfers between devices: 1.77 us -> 1.35 us
    pallas_call x1, Pallas kernels: 5.9 us -> 5.26 us  [local_step(): pl.pallas_call(write_kernel, out_shape=(sds((SL, D), BF), sds((3 * HL * H...]
    ppermute x1 -> x0, starting transfers between devices: 0.43 us -> none  [local_step(): ln_cr = lax.ppermute(ln_hs, 'tp', across)]
  transfers between devices with their start and end apart: 2 -> 1, of which waited for: 0 -> 0; matrix products, arithmetic and copies ran while one was open for 0% -> 0% of each run, Pallas kernels for 15% -> 14%
where the time goes in v6:
time: 38.8 us; the launch traced here: 38.7 us
  Pallas kernels  36.6 us (94%)
  starting transfers between devices  1.35 us (3%)
  between operations  0.68 us (2%)
    pallas_call x1, Pallas kernels, local_step(): pl.pallas_call(block_kernel, out_shape=(pltpu.VMEM((SL, D), BF), pltpu.VM...  30.6 us
    pallas_call x1, Pallas kernels, local_step(): pl.pallas_call(write_kernel, out_shape=(sds((SL, D), BF), sds((3 * HL * H...  5.26 us
    ppermute x1, starting transfers between devices, local_step(): r_cr = lax.ppermute(r_hs, 'tp', across)  1.35 us
    pallas_call x1, Pallas kernels, local_step(): pl.pallas_call(last_kernel, out_shape=(sds((SL, D), BF), vec1, vec1), in_...  0.79 us
  transfers between devices with their start and end apart: 1, of which 0 were waited for; matrix products, arithmetic and copies ran while one was open for 0% of the time, Pallas kernels for 14%

profile of v6, /device:TPU:0, one launch (start us, length us, event | category | flops | bytes accessed | tf_op | source)
XLA Modules:
  0.0 38.7 jit_solution(1343751229182971263)
XLA Ops:
  0.7 30.6 %block.1 = (bf16[24,1536]{1,0:T(8,128)(2,1)S(1)}, f32[8,1536]{1,0:T(8,128)S(1)}, bf16[1536,1536]{1,0:T(8,128)(2,1)S(1)}, bf16[1536,1536]{1,0:T(8,128)(2,1)S(1)},...) custom-call(bf16[24,1536]{1,0:T(8,128)(2,1)} %bitcast.13, ...), custom_call_target="tpu_custom_call" | custom-call | tf_op jit(solution)/shard_map/block/pallas_call | solution.py:431
  31.3 1.4 %collective-permute-start = (bf16[32,1536]{1,0:T(8,128)(2,1)S(1)}, bf16[32,1536]{1,0:T(8,128)(2,1)S(1)}, u32[]{:S(2)}, u32[]{:S(2)}) collective-permute-start(bf16[32,1536]{1,0:T(8,128)(2,1)S(1)} %get-tuple-element.57), channel_id=1, source_target_pairs={{0,3},{1,2},{2,1},{3,0},{4,7},{5,6},{6,5},{7,4}} | collective-permute-start | bytes 294920 | tf_op jit(solution)/shard_map/ppermute | solution.py:458
  32.6 5.3 %write.1 = (bf16[24,1536]{1,0:T(8,128)(2,1)}, bf16[1152,1536]{1,0:T(8,128)(2,1)}, f32[3,4,96]{2,1,0:T(4,128)}, bf16[384,1536]{1,0:T(8,128)(2,1)}, f32[1536]{0:T(...) custom-call(bf16[24,1536]{1,0:T(8,128)(2,1)S(1)} %get-tuple-element., ...), custom_call_target="tpu_custom_call" | custom-call | flops 600000000 | bytes 14200000 | tf_op jit(solution)/shard_map/write/pallas_call | solution.py:459
  37.9 0.0 collective-permute-done.rc_ref
  37.9 0.8 %last.1 = (bf16[24,1536]{1,0:T(8,128)(2,1)}, f32[1536]{0:T(1024)}, f32[1536]{0:T(1024)}) custom-call(bf16[24,1536]{1,0:T(8,128)(2,1)S(1)} %get-tuple-element.52.mine_ref, f32[24,1536]{1,0:T(8,128)S(1)} %get-tuple-element.53.xh_ref, f32[24,1536]{1,0:T(8,128)S(1)} %get-tuple-element.54.gm_ref, f32[24,128]{1,0:T(8,128)S(1)} %get-tuple-element.55.rs_ref, ...), custom_call_target="tpu_custom_call" | custom-call | tf_op jit(solution)/shard_map/last/pallas_call | solution.py:471
Async XLA Ops:
  31.3 6.6 %collective-permute-start = (bf16[32,1536]{1,0:T(8,128)(2,1)S(1)}, bf16[32,1536]{1,0:T(8,128)(2,1)S(1)}, u32[]{:S(2)}, u32[]{:S(2)}) collective-permute-start(bf16[32,1536]{1,0:T(8,128)(2,1)S(1)} %get-tuple-element.57), channel_id=1, source_target_pairs={{0,3},{1,2},{2,1},{3,0},{4,7},{5,6},{6,5},{7,4}} | collective-permute-start | bytes 294920 | tf_op jit(solution)/shard_map/ppermute | solution.py:458

commit v7 on v6

--- a/solution.py
+++ b/solution.py
@@ -25,6 +25,8 @@
 NCH = D // CW
 HCH = NCH // 2
 HW = D // 2
+CUT = (0, 256, 512, 640, 768)
+NCUT = len(CUT) - 1
 
 
 def alibi_slopes(n_heads):
@@ -43,10 +45,10 @@
 def gelu_parts(u):
     k = math.sqrt(2.0 / math.pi)
     u2 = u * u
-    th = jnp.tanh(k * (u + 0.044715 * (u2 * u)))
-    half = 0.5 * (1.0 + th)
-    dk = k * (1.0 + 3.0 * 0.044715 * u2)
-    return u * half, half + 0.5 * u * (1.0 - th * th) * dk
+    th = jnp.tanh(u * (k + (k * 0.044715) * u2))
+    half = 0.5 + 0.5 * th
+    val = u * half
+    return val, half + val * (1.0 - th) * (k + (3.0 * 0.044715 * k) * u2)
 
 
 def rows_stats(v):
@@ -114,19 +116,16 @@
     w_cps['up'] = [pltpu.make_async_copy(wup_hbm, wup, wsem.at[8])]
 
     barrier = pltpu.get_barrier_semaphore()
-    for dev in (pt, ct):
+    for dev in (pt, ct, qt):
         pl.semaphore_signal(barrier, inc=1, device_id={'tp': dev}, device_id_type=MESH)
     for name in ('qkv', 'out', 'dn', 'up'):
         for c in w_cps[name]:
             c.start()
-    pl.semaphore_wait(barrier, 2)
+    pl.semaphore_wait(barrier, 3)
 
     in_x.wait()
     x_c = send(xg.at[t], xg.at[t], ct)
     x_p = send(xg.at[t], xg.at[t], pt)
-    in_gy.wait()
-    y_c = send(gyg.at[t], gyg.at[t], ct)
-    y_p = send(gyg.at[t], gyg.at[t], pt)
 
     for c in (in_b, *in_p):
         c.wait()
@@ -141,6 +140,9 @@
 
     x_c.wait_recv()
     x_f = send(xg.at[ct], xg.at[ct], pt)
+    in_gy.wait()
+    y_c = send(gyg.at[t], gyg.at[t], ct)
+    y_p = send(gyg.at[t], gyg.at[t], pt)
     x_p.wait_recv()
     x_f.wait_recv()
 
@@ -153,9 +155,6 @@
         rstd_s[r:r + 32, :] = jnp.broadcast_to(rstd, (32, 128))
         h_ref[r:r + 32, :] = (xh * g1_ref[...] + be1_ref[...]).astype(BF)
 
-    y_c.wait_recv()
-    y_f = send(gyg.at[ct], gyg.at[ct], pt)
-
     w_cps['qkv'][0].wait()
     hv = h_ref[...]
     for h in range(HL):
@@ -181,35 +180,39 @@
         probs[h] = p
         ctx_ref[h * HD:(h + 1) * HD, :] = dot(head(h, 2), p.astype(BF), 1, 0).astype(BF)
 
-    def exchange(part, groups, ps, pr, hs, hr, cr):
+    def exchange(part, groups, ps, pr, hs, hr, cr, fr):
         firsts = []
         for k0, k1 in groups:
-            theirs = part(1 - half, k0 * CW, k1 * CW)
+            cols = slice(CUT[k0], CUT[k1])
+            ps[:, cols] = part(1 - half, CUT[k0], CUT[k1]).astype(BF)
+            firsts.append(send(ps.at[:, cols], pr.at[:, cols], pt))
+        outs = []
+        for (k0, k1), first in zip(groups, firsts):
+            cols = slice(CUT[k0], CUT[k1])
+            ours = part(half, CUT[k0], CUT[k1])
+            first.wait_recv()
+            hs[:, cols] = (ours + pr[:, cols].astype(F32)).astype(BF)
             for k in range(k0, k1):
-                ps[k] = theirs[:, (k - k0) * CW:(k - k0 + 1) * CW].astype(BF)
-                firsts.append(send(ps.at[k], pr.at[k], pt))
-        outs = []
-        for k0, k1 in groups:
-            ours = part(half, k0 * CW, k1 * CW)
-            for k in range(k0, k1):
-                own = ours[:, (k - k0) * CW:(k - k0 + 1) * CW]
-                firsts[k].wait_recv()
-                hs[k] = (own + pr[k].astype(F32)).astype(BF)
-                outs.append((send(hs.at[k], cr.at[k], ct), send(hs.at[k], hr.at[k], pt)))
-        return outs
-
-    def forward(outs, cr, fr):
-        fwd = []
-        for k in range(HCH):
-            outs[k][0].wait_recv()
-            fwd.append(send(cr.at[k], fr.at[k], pt))
-        return fwd
+                c = slice(CUT[k], CUT[k + 1])
+                outs.append([send(hs.at[:, c], cr.at[:, c], ct)])
+                if k == NCUT - 1:
+                    outs[-1].append(send(hs.at[:, c], fr.at[:, c], qt))
+        local = send(hs, hr, pt)
+        return outs, local
+
+    def forward(out, k, cr, fr):
+        if k < NCUT - 1:
+            c = slice(CUT[k], CUT[k + 1])
+            out[0].wait_recv()
+            out.append(send(cr.at[:, c], fr.at[:, c], pt))
 
     for c in w_cps['out']:
         c.wait()
     ctxT = ctx_ref[...]
-    a_outs = exchange(lambda hh, c0, c1: dot(ctxT, wout[hh, :, c0:c1], 0, 0), ((0, HCH),), a_ps, a_pr, a_hs, a_hr, a_cr)
-
+    a_outs, a_local = exchange(lambda hh, c0, c1: dot(ctxT, wout[hh, :, c0:c1], 0, 0), ((0, NCUT),), a_ps, a_pr, a_hs, a_hr, a_cr, a_fr)
+
+    y_c.wait_recv()
+    y_f = send(gyg.at[ct], gyg.at[ct], pt)
     y_p.wait_recv()
     y_f.wait_recv()
     for i in range(TP):
@@ -222,21 +225,26 @@
         gact[:, n * CW:(n + 1) * CW] = dot(gyv, wdn[n * CW:(n + 1) * CW, :], 1, 1).astype(BF)
     vec_ref[0:1, :] = jnp.sum(gm_f[...], axis=0, keepdims=True)
 
-    def gathered(outs, fwd, hs, hr, cr, fr, put):
+    def gathered(outs, local, hs, hr, cr, fr, put):
+        outs[-1][0].wait_recv()
         for k in range(HCH):
-            put(half * HCH + k, (hs[k].astype(F32) + cr[k].astype(F32)).astype(BF).astype(F32))
+            c = slice(k * CW, (k + 1) * CW)
+            put(half * HCH + k, (hs[:, c].astype(F32) + cr[:, c].astype(F32)).astype(BF).astype(F32))
+        local.wait_recv()
+        for out in outs:
+            out[1].wait_recv()
         for k in range(HCH):
-            outs[k][1].wait_recv()
-            fwd[k].wait_recv()
-            put((1 - half) * HCH + k, (hr[k].astype(F32) + fr[k].astype(F32)).astype(BF).astype(F32))
-
-    a_fwd = forward(a_outs, a_cr, a_fr)
+            c = slice(k * CW, (k + 1) * CW)
+            put((1 - half) * HCH + k, (hr[:, c].astype(F32) + fr[:, c].astype(F32)).astype(BF).astype(F32))
+
+    for k, out in enumerate(a_outs):
+        forward(out, k, a_cr, a_fr)
 
     def put_x(kk, val):
         cols = pl.ds(pl.multiple_of(kk * CW, CW), CW)
         xf[:, cols] = xf[:, cols] + val + bo_ref[:, cols]
 
-    gathered(a_outs, a_fwd, a_hs, a_hr, a_cr, a_fr, put_x)
+    gathered(a_outs, a_local, a_hs, a_hr, a_cr, a_fr, put_x)
 
     for r in range(0, S, 32):
         cen, rstd = rows_stats(xf[r:r + 32, :])
@@ -258,7 +266,7 @@
     def part_g(hh, c0, c1):
         return dot(gprev, wup[pl.ds(pl.multiple_of(hh * HW + c0, CW), c1 - c0), :], 1, 1)
 
-    g_outs = exchange(part_g, ((0, 1), (1, HCH)), b_ps, b_pr, b_hs, b_hr, b_cr)
+    g_outs, g_local = exchange(part_g, ((0, 1), (1, NCUT)), b_ps, b_pr, b_hs, b_hr, b_cr, b_fr)
 
     actv = act_ref[...]
     for n in range(NCH):
@@ -267,10 +275,8 @@
     m_first = (send(mp.at[qt], m_pr.at[1], pt), send(mp.at[pt], m_pr.at[0], pt))
     for n in range(NCH):
         gwdn_ref[n * CW:(n + 1) * CW, :] = dot(act_ref[:, n * CW:(n + 1) * CW], gyv, 0, 0).astype(BF)
-    g_fwd = []
     for k in range(HCH):
-        g_outs[k][0].wait_recv()
-        g_fwd.append(send(b_cr.at[k], b_fr.at[k], pt))
+        forward(g_outs[k], k, b_cr, b_fr)
         for n in range(2 * k, 2 * k + 2):
             gwup_ref[n * CW:(n + 1) * CW, :] = dot(g_ref[:, n * CW:(n + 1) * CW], gprev, 0, 0).astype(BF)
 
@@ -281,7 +287,7 @@
     def put_g(kk, val):
         gg_f[:, pl.ds(pl.multiple_of(kk * CW, CW), CW)] = val
 
-    gathered(g_outs, g_fwd, b_hs, b_hr, b_cr, b_fr, put_g)
+    gathered(g_outs, g_local, b_hs, b_hr, b_cr, b_fr, put_g)
 
     gg2 = jnp.zeros((1, D), F32)
     gb2 = jnp.zeros((1, D), F32)
@@ -363,7 +369,7 @@
         c.wait_send()
 
 
-N_SEND = 6 + 12 + 12 + 3 + 4 + 1
+N_SEND = 6 + 2 * (2 + 4 + 1 + 1 + 3) + 3 + 4 + 1
 VMEM_A = 36 * 2**20
 VMEM_B = 8 * 2**20
 VMEM_C = 4 * 2**20
@@ -426,7 +432,7 @@
     def local_step(x, g1, be1, w_qkv, b_qkv, w_out, b_out, g2, be2, w_up, b_up, w_down, b_down, grad_y):
         wq = jnp.transpose(w_qkv, (1, 2, 3, 0)).reshape(3 * HL * HD, D)
         bq = jnp.transpose(b_qkv, (1, 0, 2))
-        part = pltpu.VMEM((HCH, S, CW), BF)
+        part = pltpu.VMEM((S, HW), BF)
         vec1 = sds((D,), F32)
         mids = pl.pallas_call(
             block_kernel,

time: 38.8 us -> 38.2 us (0.985)
  Pallas kernels: 36.6 us -> 36.1 us
    pallas_call x1, Pallas kernels: 30.6 us -> 30 us  [local_step(): pl.pallas_call(block_kernel, out_shape=(pltpu.VMEM((SL, D), BF), pltpu.VM...]
where the time goes in v7:
time: 38.2 us; the launch traced here: 38.1 us
  Pallas kernels  36.1 us (95%)
  starting transfers between devices  1.36 us (4%)
  between operations  0.68 us (2%)
    pallas_call x1, Pallas kernels, local_step(): pl.pallas_call(block_kernel, out_shape=(pltpu.VMEM((SL, D), BF), pltpu.VM...  30 us
    pallas_call x1, Pallas kernels, local_step(): pl.pallas_call(write_kernel, out_shape=(sds((SL, D), BF), sds((3 * HL * H...  5.26 us
    ppermute x1, starting transfers between devices, local_step(): r_cr = lax.ppermute(r_hs, 'tp', across)  1.36 us
    pallas_call x1, Pallas kernels, local_step(): pl.pallas_call(last_kernel, out_shape=(sds((SL, D), BF), vec1, vec1), in_...  0.79 us
  transfers between devices with their start and end apart: 1, of which 0 were waited for; matrix products, arithmetic and copies ran while one was open for 0% of the time, Pallas kernels for 14%

profile of v7, /device:TPU:0, one launch (start us, length us, event | category | flops | bytes accessed | tf_op | source)
XLA Modules:
  0.0 38.1 jit_solution(11958781714514985418)
XLA Ops:
  0.7 30.0 %block.1 = (bf16[24,1536]{1,0:T(8,128)(2,1)S(1)}, f32[8,1536]{1,0:T(8,128)S(1)}, bf16[1536,1536]{1,0:T(8,128)(2,1)S(1)}, bf16[1536,1536]{1,0:T(8,128)(2,1)S(1)},...) custom-call(bf16[24,1536]{1,0:T(8,128)(2,1)} %bitcast.13, ...), custom_call_target="tpu_custom_call" | custom-call | tf_op jit(solution)/shard_map/block/pallas_call | solution.py:437
  30.7 1.4 %collective-permute-start = (bf16[32,1536]{1,0:T(8,128)(2,1)S(1)}, bf16[32,1536]{1,0:T(8,128)(2,1)S(1)}, u32[]{:S(2)}, u32[]{:S(2)}) collective-permute-start(bf16[32,1536]{1,0:T(8,128)(2,1)S(1)} %get-tuple-element.57), channel_id=1, source_target_pairs={{0,3},{1,2},{2,1},{3,0},{4,7},{5,6},{6,5},{7,4}} | collective-permute-start | bytes 294920 | tf_op jit(solution)/shard_map/ppermute | solution.py:464
  32.1 5.3 %write.1 = (bf16[24,1536]{1,0:T(8,128)(2,1)}, bf16[1152,1536]{1,0:T(8,128)(2,1)}, f32[3,4,96]{2,1,0:T(4,128)}, bf16[384,1536]{1,0:T(8,128)(2,1)}, f32[1536]{0:T(...) custom-call(bf16[24,1536]{1,0:T(8,128)(2,1)S(1)} %get-tuple-element., ...), custom_call_target="tpu_custom_call" | custom-call | flops 600000000 | bytes 14200000 | tf_op jit(solution)/shard_map/write/pallas_call | solution.py:465
  37.3 0.0 collective-permute-done.rc_ref
  37.3 0.8 %last.1 = (bf16[24,1536]{1,0:T(8,128)(2,1)}, f32[1536]{0:T(1024)}, f32[1536]{0:T(1024)}) custom-call(bf16[24,1536]{1,0:T(8,128)(2,1)S(1)} %get-tuple-element.52.mine_ref, f32[24,1536]{1,0:T(8,128)S(1)} %get-tuple-element.53.xh_ref, f32[24,1536]{1,0:T(8,128)S(1)} %get-tuple-element.54.gm_ref, f32[24,128]{1,0:T(8,128)S(1)} %get-tuple-element.55.rs_ref, ...), custom_call_target="tpu_custom_call" | custom-call | tf_op jit(solution)/shard_map/last/pallas_call | solution.py:477
Async XLA Ops:
  30.7 6.6 %collective-permute-start = (bf16[32,1536]{1,0:T(8,128)(2,1)S(1)}, bf16[32,1536]{1,0:T(8,128)(2,1)S(1)}, u32[]{:S(2)}, u32[]{:S(2)}) collective-permute-start(bf16[32,1536]{1,0:T(8,128)(2,1)S(1)} %get-tuple-element.57), channel_id=1, source_target_pairs={{0,3},{1,2},{2,1},{3,0},{4,7},{5,6},{6,5},{7,4}} | collective-permute-start | bytes 294920 | tf_op jit(solution)/shard_map/ppermute | solution.py:464

commit v8 on v7

--- a/solution.py
+++ b/solution.py
@@ -138,12 +138,12 @@
             row = jnp.broadcast_to(bqkv_ref[e, h:h + 1, :], (S, HD))
             biasT[pl.ds((h * 3 + e) * HD, HD), :] = row.T
 
-    x_c.wait_recv()
-    x_f = send(xg.at[ct], xg.at[ct], pt)
+    x_p.wait_recv()
     in_gy.wait()
     y_c = send(gyg.at[t], gyg.at[t], ct)
     y_p = send(gyg.at[t], gyg.at[t], pt)
-    x_p.wait_recv()
+    x_c.wait_recv()
+    x_f = send(xg.at[ct], xg.at[ct], pt)
     x_f.wait_recv()
 
     for i in range(TP):
@@ -200,11 +200,19 @@
         local = send(hs, hr, pt)
         return outs, local
 
-    def forward(out, k, cr, fr):
+    def arrived(out, k, hs, cr, fr, put):
+        c = slice(CUT[k], CUT[k + 1])
+        out[0].wait_recv()
         if k < NCUT - 1:
+            out.append(send(cr.at[:, c], fr.at[:, c], pt))
+        put(half * HW + CUT[k], CUT[k + 1] - CUT[k], (hs[:, c].astype(F32) + cr[:, c].astype(F32)).astype(BF).astype(F32))
+
+    def passed_on(outs, local, hr, fr, put):
+        local.wait_recv()
+        for k, out in enumerate(outs):
             c = slice(CUT[k], CUT[k + 1])
-            out[0].wait_recv()
-            out.append(send(cr.at[:, c], fr.at[:, c], pt))
+            out[1].wait_recv()
+            put((1 - half) * HW + CUT[k], CUT[k + 1] - CUT[k], (hr[:, c].astype(F32) + fr[:, c].astype(F32)).astype(BF).astype(F32))
 
     for c in w_cps['out']:
         c.wait()
@@ -225,26 +233,13 @@
         gact[:, n * CW:(n + 1) * CW] = dot(gyv, wdn[n * CW:(n + 1) * CW, :], 1, 1).astype(BF)
     vec_ref[0:1, :] = jnp.sum(gm_f[...], axis=0, keepdims=True)
 
-    def gathered(outs, local, hs, hr, cr, fr, put):
-        outs[-1][0].wait_recv()
-        for k in range(HCH):
-            c = slice(k * CW, (k + 1) * CW)
-            put(half * HCH + k, (hs[:, c].astype(F32) + cr[:, c].astype(F32)).astype(BF).astype(F32))
-        local.wait_recv()
-        for out in outs:
-            out[1].wait_recv()
-        for k in range(HCH):
-            c = slice(k * CW, (k + 1) * CW)
-            put((1 - half) * HCH + k, (hr[:, c].astype(F32) + fr[:, c].astype(F32)).astype(BF).astype(F32))
+    def put_x(start, width, val):
+        cols = pl.ds(pl.multiple_of(start, 128), width)
+        xf[:, cols] = xf[:, cols] + val + bo_ref[:, cols]
 
     for k, out in enumerate(a_outs):
-        forward(out, k, a_cr, a_fr)
-
-    def put_x(kk, val):
-        cols = pl.ds(pl.multiple_of(kk * CW, CW), CW)
-        xf[:, cols] = xf[:, cols] + val + bo_ref[:, cols]
-
-    gathered(a_outs, a_local, a_hs, a_hr, a_cr, a_fr, put_x)
+        arrived(out, k, a_hs, a_cr, a_fr, put_x)
+    passed_on(a_outs, a_local, a_hr, a_fr, put_x)
 
     for r in range(0, S, 32):
         cen, rstd = rows_stats(xf[r:r + 32, :])
@@ -275,19 +270,20 @@
     m_first = (send(mp.at[qt], m_pr.at[1], pt), send(mp.at[pt], m_pr.at[0], pt))
     for n in range(NCH):
         gwdn_ref[n * CW:(n + 1) * CW, :] = dot(act_ref[:, n * CW:(n + 1) * CW], gyv, 0, 0).astype(BF)
+    def put_g(start, width, val):
+        gg_f[:, pl.ds(pl.multiple_of(start, 128), width)] = val
+
     for k in range(HCH):
-        forward(g_outs[k], k, b_cr, b_fr)
+        arrived(g_outs[k], k, b_hs, b_cr, b_fr, put_g)
         for n in range(2 * k, 2 * k + 2):
             gwup_ref[n * CW:(n + 1) * CW, :] = dot(g_ref[:, n * CW:(n + 1) * CW], gprev, 0, 0).astype(BF)
+    arrived(g_outs[-1], NCUT - 1, b_hs, b_cr, b_fr, put_g)
 
     m_first[0].wait_recv()
     m_hs[...] = (mp[ct].astype(F32) + m_pr[1].astype(F32)).astype(BF)
     m_out = send(m_hs, m_cr, ct)
 
-    def put_g(kk, val):
-        gg_f[:, pl.ds(pl.multiple_of(kk * CW, CW), CW)] = val
-
-    gathered(g_outs, g_local, b_hs, b_hr, b_cr, b_fr, put_g)
+    passed_on(g_outs, g_local, b_hr, b_fr, put_g)
 
     gg2 = jnp.zeros((1, D), F32)
     gb2 = jnp.zeros((1, D), F32)

time: 38.2 us -> 39 us (1.021)
  Pallas kernels: 36.1 us -> 36.5 us
where the time goes in v8:
time: 39 us; the launch traced here: 38.9 us
  Pallas kernels  36.5 us (94%)
  starting transfers between devices  1.71 us (4%)
  between operations  0.68 us (2%)
    pallas_call x1, Pallas kernels, local_step(): pl.pallas_call(block_kernel, out_shape=(pltpu.VMEM((SL, D), BF), pltpu.VM...  30.4 us
    pallas_call x1, Pallas kernels, local_step(): pl.pallas_call(write_kernel, out_shape=(sds((SL, D), BF), sds((3 * HL * H...  5.26 us
    ppermute x1, starting transfers between devices, local_step(): r_cr = lax.ppermute(r_hs, 'tp', across)  1.71 us
    pallas_call x1, Pallas kernels, local_step(): pl.pallas_call(last_kernel, out_shape=(sds((SL, D), BF), vec1, vec1), in_...  0.79 us
  transfers between devices with their start and end apart: 1, of which 0 were waited for; matrix products, arithmetic and copies ran while one was open for 0% of the time, Pallas kernels for 14%

profile of v8, /device:TPU:0, one launch (start us, length us, event | category | flops | bytes accessed | tf_op | source)
XLA Modules:
  0.0 38.9 jit_solution(9175176322304091275)
XLA Ops:
  0.7 30.4 %block.1 = (bf16[24,1536]{1,0:T(8,128)(2,1)S(1)}, f32[8,1536]{1,0:T(8,128)S(1)}, bf16[1536,1536]{1,0:T(8,128)(2,1)S(1)}, bf16[1536,1536]{1,0:T(8,128)(2,1)S(1)},...) custom-call(bf16[24,1536]{1,0:T(8,128)(2,1)} %bitcast.13, ...), custom_call_target="tpu_custom_call" | custom-call | tf_op jit(solution)/shard_map/block/pallas_call | solution.py:433
  31.1 1.7 %collective-permute-start = (bf16[32,1536]{1,0:T(8,128)(2,1)S(1)}, bf16[32,1536]{1,0:T(8,128)(2,1)S(1)}, u32[]{:S(2)}, u32[]{:S(2)}) collective-permute-start(bf16[32,1536]{1,0:T(8,128)(2,1)S(1)} %get-tuple-element.57), channel_id=1, source_target_pairs={{0,3},{1,2},{2,1},{3,0},{4,7},{5,6},{6,5},{7,4}} | collective-permute-start | bytes 294920 | tf_op jit(solution)/shard_map/ppermute | solution.py:460
  32.8 5.3 %write.1 = (bf16[24,1536]{1,0:T(8,128)(2,1)}, bf16[1152,1536]{1,0:T(8,128)(2,1)}, f32[3,4,96]{2,1,0:T(4,128)}, bf16[384,1536]{1,0:T(8,128)(2,1)}, f32[1536]{0:T(...) custom-call(bf16[24,1536]{1,0:T(8,128)(2,1)S(1)} %get-tuple-element., ...), custom_call_target="tpu_custom_call" | custom-call | flops 600000000 | bytes 14200000 | tf_op jit(solution)/shard_map/write/pallas_call | solution.py:461
  38.1 0.0 collective-permute-done.rc_ref
  38.1 0.8 %last.1 = (bf16[24,1536]{1,0:T(8,128)(2,1)}, f32[1536]{0:T(1024)}, f32[1536]{0:T(1024)}) custom-call(bf16[24,1536]{1,0:T(8,128)(2,1)S(1)} %get-tuple-element.52.mine_ref, f32[24,1536]{1,0:T(8,128)S(1)} %get-tuple-element.53.xh_ref, f32[24,1536]{1,0:T(8,128)S(1)} %get-tuple-element.54.gm_ref, f32[24,128]{1,0:T(8,128)S(1)} %get-tuple-element.55.rs_ref, ...), custom_call_target="tpu_custom_call" | custom-call | tf_op jit(solution)/shard_map/last/pallas_call | solution.py:473
Async XLA Ops:
  31.1 7.0 %collective-permute-start = (bf16[32,1536]{1,0:T(8,128)(2,1)S(1)}, bf16[32,1536]{1,0:T(8,128)(2,1)S(1)}, u32[]{:S(2)}, u32[]{:S(2)}) collective-permute-start(bf16[32,1536]{1,0:T(8,128)(2,1)S(1)} %get-tuple-element.57), channel_id=1, source_target_pairs={{0,3},{1,2},{2,1},{3,0},{4,7},{5,6},{6,5},{7,4}} | collective-permute-start | bytes 294920 | tf_op jit(solution)/shard_map/ppermute | solution.py:460

commit v9 on v7

--- a/solution.py
+++ b/solution.py
@@ -138,12 +138,12 @@
             row = jnp.broadcast_to(bqkv_ref[e, h:h + 1, :], (S, HD))
             biasT[pl.ds((h * 3 + e) * HD, HD), :] = row.T
 
-    x_c.wait_recv()
-    x_f = send(xg.at[ct], xg.at[ct], pt)
+    x_p.wait_recv()
     in_gy.wait()
     y_c = send(gyg.at[t], gyg.at[t], ct)
     y_p = send(gyg.at[t], gyg.at[t], pt)
-    x_p.wait_recv()
+    x_c.wait_recv()
+    x_f = send(xg.at[ct], xg.at[ct], pt)
     x_f.wait_recv()
 
     for i in range(TP):

time: 38.2 us -> 39 us (1.021)
  Pallas kernels: 36.1 us -> 36.5 us
    pallas_call x1, Pallas kernels: 30 us -> 30.5 us  [local_step(): pl.pallas_call(block_kernel, out_shape=(pltpu.VMEM((SL, D), BF), pltpu.VM...]
where the time goes in v9:
time: 39 us; the launch traced here: 38.9 us
  Pallas kernels  36.5 us (94%)
  starting transfers between devices  1.72 us (4%)
  between operations  0.68 us (2%)
    pallas_call x1, Pallas kernels, local_step(): pl.pallas_call(block_kernel, out_shape=(pltpu.VMEM((SL, D), BF), pltpu.VM...  30.5 us
    pallas_call x1, Pallas kernels, local_step(): pl.pallas_call(write_kernel, out_shape=(sds((SL, D), BF), sds((3 * HL * H...  5.26 us
    ppermute x1, starting transfers between devices, local_step(): r_cr = lax.ppermute(r_hs, 'tp', across)  1.72 us
    pallas_call x1, Pallas kernels, local_step(): pl.pallas_call(last_kernel, out_shape=(sds((SL, D), BF), vec1, vec1), in_...  0.79 us
  transfers between devices with their start and end apart: 1, of which 0 were waited for; matrix products, arithmetic and copies ran while one was open for 0% of the time, Pallas kernels for 14%

profile of v9, /device:TPU:0, one launch (start us, length us, event | category | flops | bytes accessed | tf_op | source)
XLA Modules:
  0.0 38.9 jit_solution(7233430148988538923)
XLA Ops:
  0.7 30.5 %block.1 = (bf16[24,1536]{1,0:T(8,128)(2,1)S(1)}, f32[8,1536]{1,0:T(8,128)S(1)}, bf16[1536,1536]{1,0:T(8,128)(2,1)S(1)}, bf16[1536,1536]{1,0:T(8,128)(2,1)S(1)},...) custom-call(bf16[24,1536]{1,0:T(8,128)(2,1)} %bitcast.13, ...), custom_call_target="tpu_custom_call" | custom-call | tf_op jit(solution)/shard_map/block/pallas_call | solution.py:437
  31.1 1.7 %collective-permute-start = (bf16[32,1536]{1,0:T(8,128)(2,1)S(1)}, bf16[32,1536]{1,0:T(8,128)(2,1)S(1)}, u32[]{:S(2)}, u32[]{:S(2)}) collective-permute-start(bf16[32,1536]{1,0:T(8,128)(2,1)S(1)} %get-tuple-element.57), channel_id=1, source_target_pairs={{0,3},{1,2},{2,1},{3,0},{4,7},{5,6},{6,5},{7,4}} | collective-permute-start | bytes 294920 | tf_op jit(solution)/shard_map/ppermute | solution.py:464
  32.8 5.3 %write.1 = (bf16[24,1536]{1,0:T(8,128)(2,1)}, bf16[1152,1536]{1,0:T(8,128)(2,1)}, f32[3,4,96]{2,1,0:T(4,128)}, bf16[384,1536]{1,0:T(8,128)(2,1)}, f32[1536]{0:T(...) custom-call(bf16[24,1536]{1,0:T(8,128)(2,1)S(1)} %get-tuple-element., ...), custom_call_target="tpu_custom_call" | custom-call | flops 600000000 | bytes 14200000 | tf_op jit(solution)/shard_map/write/pallas_call | solution.py:465
  38.1 0.0 collective-permute-done.rc_ref
  38.1 0.8 %last.1 = (bf16[24,1536]{1,0:T(8,128)(2,1)}, f32[1536]{0:T(1024)}, f32[1536]{0:T(1024)}) custom-call(bf16[24,1536]{1,0:T(8,128)(2,1)S(1)} %get-tuple-element.52.mine_ref, f32[24,1536]{1,0:T(8,128)S(1)} %get-tuple-element.53.xh_ref, f32[24,1536]{1,0:T(8,128)S(1)} %get-tuple-element.54.gm_ref, f32[24,128]{1,0:T(8,128)S(1)} %get-tuple-element.55.rs_ref, ...), custom_call_target="tpu_custom_call" | custom-call | tf_op jit(solution)/shard_map/last/pallas_call | solution.py:477
Async XLA Ops:
  31.1 7.0 %collective-permute-start = (bf16[32,1536]{1,0:T(8,128)(2,1)S(1)}, bf16[32,1536]{1,0:T(8,128)(2,1)S(1)}, u32[]{:S(2)}, u32[]{:S(2)}) collective-permute-start(bf16[32,1536]{1,0:T(8,128)(2,1)S(1)} %get-tuple-element.57), channel_id=1, source_target_pairs={{0,3},{1,2},{2,1},{3,0},{4,7},{5,6},{6,5},{7,4}} | collective-permute-start | bytes 294920 | tf_op jit(solution)/shard_map/ppermute | solution.py:464

commit v10 on v8

--- a/solution.py
+++ b/solution.py
@@ -25,7 +25,7 @@
 NCH = D // CW
 HCH = NCH // 2
 HW = D // 2
-CUT = (0, 256, 512, 640, 768)
+CUT = (0, 256, 512, 768)
 NCUT = len(CUT) - 1
 
 
@@ -116,12 +116,12 @@
     w_cps['up'] = [pltpu.make_async_copy(wup_hbm, wup, wsem.at[8])]
 
     barrier = pltpu.get_barrier_semaphore()
-    for dev in (pt, ct, qt):
+    for dev in (pt, ct):
         pl.semaphore_signal(barrier, inc=1, device_id={'tp': dev}, device_id_type=MESH)
     for name in ('qkv', 'out', 'dn', 'up'):
         for c in w_cps[name]:
             c.start()
-    pl.semaphore_wait(barrier, 3)
+    pl.semaphore_wait(barrier, 2)
 
     in_x.wait()
     x_c = send(xg.at[t], xg.at[t], ct)
@@ -138,12 +138,12 @@
             row = jnp.broadcast_to(bqkv_ref[e, h:h + 1, :], (S, HD))
             biasT[pl.ds((h * 3 + e) * HD, HD), :] = row.T
 
-    x_p.wait_recv()
+    x_c.wait_recv()
+    x_f = send(xg.at[ct], xg.at[ct], pt)
     in_gy.wait()
     y_c = send(gyg.at[t], gyg.at[t], ct)
     y_p = send(gyg.at[t], gyg.at[t], pt)
-    x_c.wait_recv()
-    x_f = send(xg.at[ct], xg.at[ct], pt)
+    x_p.wait_recv()
     x_f.wait_recv()
 
     for i in range(TP):
@@ -195,16 +195,13 @@
             for k in range(k0, k1):
                 c = slice(CUT[k], CUT[k + 1])
                 outs.append([send(hs.at[:, c], cr.at[:, c], ct)])
-                if k == NCUT - 1:
-                    outs[-1].append(send(hs.at[:, c], fr.at[:, c], qt))
         local = send(hs, hr, pt)
         return outs, local
 
     def arrived(out, k, hs, cr, fr, put):
         c = slice(CUT[k], CUT[k + 1])
         out[0].wait_recv()
-        if k < NCUT - 1:
-            out.append(send(cr.at[:, c], fr.at[:, c], pt))
+        out.append(send(cr.at[:, c], fr.at[:, c], pt))
         put(half * HW + CUT[k], CUT[k + 1] - CUT[k], (hs[:, c].astype(F32) + cr[:, c].astype(F32)).astype(BF).astype(F32))
 
     def passed_on(outs, local, hr, fr, put):
@@ -277,7 +274,6 @@
         arrived(g_outs[k], k, b_hs, b_cr, b_fr, put_g)
         for n in range(2 * k, 2 * k + 2):
             gwup_ref[n * CW:(n + 1) * CW, :] = dot(g_ref[:, n * CW:(n + 1) * CW], gprev, 0, 0).astype(BF)
-    arrived(g_outs[-1], NCUT - 1, b_hs, b_cr, b_fr, put_g)
 
     m_first[0].wait_recv()
     m_hs[...] = (mp[ct].astype(F32) + m_pr[1].astype(F32)).astype(BF)
@@ -365,7 +361,7 @@
         c.wait_send()
 
 
-N_SEND = 6 + 2 * (2 + 4 + 1 + 1 + 3) + 3 + 4 + 1
+N_SEND = 6 + 2 * (2 + 3 + 1 + 3) + 3 + 4 + 1
 VMEM_A = 36 * 2**20
 VMEM_B = 8 * 2**20
 VMEM_C = 4 * 2**20

time: 39 us -> 38.5 us (0.987)
  starting transfers between devices: 1.71 us -> 1.28 us
    ppermute x1, starting transfers between devices: 1.71 us -> 1.28 us  [local_step(): r_cr = lax.ppermute(r_hs, 'tp', across)]
where the time goes in v10:
time: 38.5 us
  Pallas kernels  36.5 us (95%)
  starting transfers between devices  1.28 us (3%)
  between operations  0.68 us (2%)
    pallas_call x1, Pallas kernels, local_step(): pl.pallas_call(block_kernel, out_shape=(pltpu.VMEM((SL, D), BF), pltpu.VM...  30.4 us
    pallas_call x1, Pallas kernels, local_step(): pl.pallas_call(write_kernel, out_shape=(sds((SL, D), BF), sds((3 * HL * H...  5.26 us
    ppermute x1, starting transfers between devices, local_step(): r_cr = lax.ppermute(r_hs, 'tp', across)  1.28 us
    pallas_call x1, Pallas kernels, local_step(): pl.pallas_call(last_kernel, out_shape=(sds((SL, D), BF), vec1, vec1), in_...  0.79 us
  transfers between devices with their start and end apart: 1, of which 0 were waited for; matrix products, arithmetic and copies ran while one was open for 0% of the time, Pallas kernels for 14%

profile of v10, /device:TPU:0, one launch (start us, length us, event | category | flops | bytes accessed | tf_op | source)
XLA Modules:
  0.0 38.5 jit_solution(7904153209661502139)
XLA Ops:
  0.7 30.4 %block.1 = (bf16[24,1536]{1,0:T(8,128)(2,1)S(1)}, f32[8,1536]{1,0:T(8,128)S(1)}, bf16[1536,1536]{1,0:T(8,128)(2,1)S(1)}, bf16[1536,1536]{1,0:T(8,128)(2,1)S(1)},...) custom-call(bf16[24,1536]{1,0:T(8,128)(2,1)} %bitcast.13, ...), custom_call_target="tpu_custom_call" | custom-call | tf_op jit(solution)/shard_map/block/pallas_call | solution.py:429
  31.1 1.3 %collective-permute-start = (bf16[32,1536]{1,0:T(8,128)(2,1)S(1)}, bf16[32,1536]{1,0:T(8,128)(2,1)S(1)}, u32[]{:S(2)}, u32[]{:S(2)}) collective-permute-start(bf16[32,1536]{1,0:T(8,128)(2,1)S(1)} %get-tuple-element.57), channel_id=1, source_target_pairs={{0,3},{1,2},{2,1},{3,0},{4,7},{5,6},{6,5},{7,4}} | collective-permute-start | bytes 294920 | tf_op jit(solution)/shard_map/ppermute | solution.py:456
  32.4 5.3 %write.1 = (bf16[24,1536]{1,0:T(8,128)(2,1)}, bf16[1152,1536]{1,0:T(8,128)(2,1)}, f32[3,4,96]{2,1,0:T(4,128)}, bf16[384,1536]{1,0:T(8,128)(2,1)}, f32[1536]{0:T(...) custom-call(bf16[24,1536]{1,0:T(8,128)(2,1)S(1)} %get-tuple-element., ...), custom_call_target="tpu_custom_call" | custom-call | flops 600000000 | bytes 14200000 | tf_op jit(solution)/shard_map/write/pallas_call | solution.py:457
  37.7 0.0 collective-permute-done.rc_ref
  37.7 0.8 %last.1 = (bf16[24,1536]{1,0:T(8,128)(2,1)}, f32[1536]{0:T(1024)}, f32[1536]{0:T(1024)}) custom-call(bf16[24,1536]{1,0:T(8,128)(2,1)S(1)} %get-tuple-element.52.mine_ref, f32[24,1536]{1,0:T(8,128)S(1)} %get-tuple-element.53.xh_ref, f32[24,1536]{1,0:T(8,128)S(1)} %get-tuple-element.54.gm_ref, f32[24,128]{1,0:T(8,128)S(1)} %get-tuple-element.55.rs_ref, ...), custom_call_target="tpu_custom_call" | custom-call | tf_op jit(solution)/shard_map/last/pallas_call | solution.py:469
Async XLA Ops:
  31.1 6.5 %collective-permute-start = (bf16[32,1536]{1,0:T(8,128)(2,1)S(1)}, bf16[32,1536]{1,0:T(8,128)(2,1)S(1)}, u32[]{:S(2)}, u32[]{:S(2)}) collective-permute-start(bf16[32,1536]{1,0:T(8,128)(2,1)S(1)} %get-tuple-element.57), channel_id=1, source_target_pairs={{0,3},{1,2},{2,1},{3,0},{4,7},{5,6},{6,5},{7,4}} | collective-permute-start | bytes 294920 | tf_op jit(solution)/shard_map/ppermute | solution.py:456

commit v11 on v8

--- a/solution.py
+++ b/solution.py
@@ -27,6 +27,7 @@
 HW = D // 2
 CUT = (0, 256, 512, 640, 768)
 NCUT = len(CUT) - 1
+XCUT = 1024
 
 
 def alibi_slopes(n_heads):
@@ -124,8 +125,10 @@
     pl.semaphore_wait(barrier, 3)
 
     in_x.wait()
-    x_c = send(xg.at[t], xg.at[t], ct)
+    lo, hi = slice(0, XCUT), slice(XCUT, D)
+    x_c = send(xg.at[t, :, lo], xg.at[t, :, lo], ct)
     x_p = send(xg.at[t], xg.at[t], pt)
+    x_d = [send(xg.at[t, :, hi], xg.at[t, :, hi], dev) for dev in (ct, qt)]
 
     for c in (in_b, *in_p):
         c.wait()
@@ -138,12 +141,14 @@
             row = jnp.broadcast_to(bqkv_ref[e, h:h + 1, :], (S, HD))
             biasT[pl.ds((h * 3 + e) * HD, HD), :] = row.T
 
-    x_p.wait_recv()
+    x_c.wait_recv()
+    x_f = send(xg.at[ct, :, lo], xg.at[ct, :, lo], pt)
     in_gy.wait()
     y_c = send(gyg.at[t], gyg.at[t], ct)
     y_p = send(gyg.at[t], gyg.at[t], pt)
-    x_c.wait_recv()
-    x_f = send(xg.at[ct], xg.at[ct], pt)
+    x_p.wait_recv()
+    for c in x_d:
+        c.wait_recv()
     x_f.wait_recv()
 
     for i in range(TP):
@@ -365,7 +370,7 @@
         c.wait_send()
 
 
-N_SEND = 6 + 2 * (2 + 4 + 1 + 1 + 3) + 3 + 4 + 1
+N_SEND = 8 + 2 * (2 + 4 + 1 + 1 + 3) + 3 + 4 + 1
 VMEM_A = 36 * 2**20
 VMEM_B = 8 * 2**20
 VMEM_C = 4 * 2**20

time: 39 us -> 38.3 us (0.982)
  Pallas kernels: 36.5 us -> 36 us
    pallas_call x1, Pallas kernels: 30.4 us -> 29.9 us  [local_step(): pl.pallas_call(block_kernel, out_shape=(pltpu.VMEM((SL, D), BF), pltpu.VM...]
where the time goes in v11:
time: 38.3 us; the launch traced here: 38.2 us
  Pallas kernels  36 us (94%)
  starting transfers between devices  1.6 us (4%)
  between operations  0.68 us (2%)
    pallas_call x1, Pallas kernels, local_step(): pl.pallas_call(block_kernel, out_shape=(pltpu.VMEM((SL, D), BF), pltpu.VM...  29.9 us
    pallas_call x1, Pallas kernels, local_step(): pl.pallas_call(write_kernel, out_shape=(sds((SL, D), BF), sds((3 * HL * H...  5.26 us
    ppermute x1, starting transfers between devices, local_step(): r_cr = lax.ppermute(r_hs, 'tp', across)  1.6 us
    pallas_call x1, Pallas kernels, local_step(): pl.pallas_call(last_kernel, out_shape=(sds((SL, D), BF), vec1, vec1), in_...  0.79 us
  transfers between devices with their start and end apart: 1, of which 0 were waited for; matrix products, arithmetic and copies ran while one was open for 0% of the time, Pallas kernels for 14%

profile of v11, /device:TPU:0, one launch (start us, length us, event | category | flops | bytes accessed | tf_op | source)
XLA Modules:
  0.0 38.2 jit_solution(3250261095328085371)
XLA Ops:
  0.7 29.9 %block.1 = (bf16[24,1536]{1,0:T(8,128)(2,1)S(1)}, f32[8,1536]{1,0:T(8,128)S(1)}, bf16[1536,1536]{1,0:T(8,128)(2,1)S(1)}, bf16[1536,1536]{1,0:T(8,128)(2,1)S(1)},...) custom-call(bf16[24,1536]{1,0:T(8,128)(2,1)} %bitcast.13, ...), custom_call_target="tpu_custom_call" | custom-call | tf_op jit(solution)/shard_map/block/pallas_call | solution.py:438
  30.6 1.6 %collective-permute-start = (bf16[32,1536]{1,0:T(8,128)(2,1)S(1)}, bf16[32,1536]{1,0:T(8,128)(2,1)S(1)}, u32[]{:S(2)}, u32[]{:S(2)}) collective-permute-start(bf16[32,1536]{1,0:T(8,128)(2,1)S(1)} %get-tuple-element.57), channel_id=1, source_target_pairs={{0,3},{1,2},{2,1},{3,0},{4,7},{5,6},{6,5},{7,4}} | collective-permute-start | bytes 294920 | tf_op jit(solution)/shard_map/ppermute | solution.py:465
  32.2 5.3 %write.1 = (bf16[24,1536]{1,0:T(8,128)(2,1)}, bf16[1152,1536]{1,0:T(8,128)(2,1)}, f32[3,4,96]{2,1,0:T(4,128)}, bf16[384,1536]{1,0:T(8,128)(2,1)}, f32[1536]{0:T(...) custom-call(bf16[24,1536]{1,0:T(8,128)(2,1)S(1)} %get-tuple-element., ...), custom_call_target="tpu_custom_call" | custom-call | flops 600000000 | bytes 14200000 | tf_op jit(solution)/shard_map/write/pallas_call | solution.py:466
  37.4 0.0 collective-permute-done.rc_ref
  37.5 0.8 %last.1 = (bf16[24,1536]{1,0:T(8,128)(2,1)}, f32[1536]{0:T(1024)}, f32[1536]{0:T(1024)}) custom-call(bf16[24,1536]{1,0:T(8,128)(2,1)S(1)} %get-tuple-element.52.mine_ref, f32[24,1536]{1,0:T(8,128)S(1)} %get-tuple-element.53.xh_ref, f32[24,1536]{1,0:T(8,128)S(1)} %get-tuple-element.54.gm_ref, f32[24,128]{1,0:T(8,128)S(1)} %get-tuple-element.55.rs_ref, ...), custom_call_target="tpu_custom_call" | custom-call | tf_op jit(solution)/shard_map/last/pallas_call | solution.py:478
Async XLA Ops:
  30.6 6.9 %collective-permute-start = (bf16[32,1536]{1,0:T(8,128)(2,1)S(1)}, bf16[32,1536]{1,0:T(8,128)(2,1)S(1)}, u32[]{:S(2)}, u32[]{:S(2)}) collective-permute-start(bf16[32,1536]{1,0:T(8,128)(2,1)S(1)} %get-tuple-element.57), channel_id=1, source_target_pairs={{0,3},{1,2},{2,1},{3,0},{4,7},{5,6},{6,5},{7,4}} | collective-permute-start | bytes 294920 | tf_op jit(solution)/shard_map/ppermute | solution.py:465

commit v12 on v8

--- a/solution.py
+++ b/solution.py
@@ -97,7 +97,7 @@
                  wqkv, wout, xf, gm_f, gg_f, xhat, rstd_s, probs, qkvT, par, mp,
                  wup, wdn, xg, gyg, biasT, a_ps, a_pr, a_hs, a_hr, a_cr, a_fr, b_ps, b_pr, b_hs, b_hr, b_cr, b_fr,
                  gact, g_ref, gpre_ref, act_ref, gyf_ref, bqkv_ref, g1_in, be1_in, g2_in, be2_in, bo_in, bd_in, bup_in,
-                 rp, m_pr, m_hs, m_cr, r_pr, ln_x,
+                 rp, m_pr, m_hs, m_cr, r_pr, ln_x, xh2, rstd2,
                  wsem, ssem, rsem, isem):
     t, pt, ct, qt, half = places()
     send, started = sender(ssem, rsem)
@@ -138,12 +138,12 @@
             row = jnp.broadcast_to(bqkv_ref[e, h:h + 1, :], (S, HD))
             biasT[pl.ds((h * 3 + e) * HD, HD), :] = row.T
 
-    x_p.wait_recv()
+    x_c.wait_recv()
+    x_f = send(xg.at[ct], xg.at[ct], pt)
     in_gy.wait()
     y_c = send(gyg.at[t], gyg.at[t], ct)
     y_p = send(gyg.at[t], gyg.at[t], pt)
-    x_c.wait_recv()
-    x_f = send(xg.at[ct], xg.at[ct], pt)
+    x_p.wait_recv()
     x_f.wait_recv()
 
     for i in range(TP):
@@ -243,7 +243,10 @@
 
     for r in range(0, S, 32):
         cen, rstd = rows_stats(xf[r:r + 32, :])
-        g_ref[r:r + 32, :] = (cen * rstd * g2_ref[...] + be2_ref[...]).astype(BF)
+        xh = cen * rstd
+        xh2[r:r + 32, :] = xh
+        rstd2[r:r + 32, :] = jnp.broadcast_to(rstd, (32, 128))
+        g_ref[r:r + 32, :] = (xh * g2_ref[...] + be2_ref[...]).astype(BF)
 
     w_cps['up'][0].wait()
     gv = g_ref[...]
@@ -285,25 +288,14 @@
 
     passed_on(g_outs, g_local, b_hr, b_fr, put_g)
 
-    gg2 = jnp.zeros((1, D), F32)
-    gb2 = jnp.zeros((1, D), F32)
-    gbo = jnp.zeros((1, D), F32)
     for r in range(0, S, 32):
-        cen, rstd = rows_stats(xf[r:r + 32, :])
-        xh = cen * rstd
-        gg = gg_f[r:r + 32, :]
-        gg2 = gg2 + jnp.sum(gg * xh, axis=0, keepdims=True)
-        gb2 = gb2 + jnp.sum(gg, axis=0, keepdims=True)
-        dxh = gg * g2_ref[...]
+        xh = xh2[r:r + 32, :]
+        dxh = gg_f[r:r + 32, :] * g2_ref[...]
         m1 = jnp.mean(dxh, axis=-1, keepdims=True)
         m2 = jnp.mean(dxh * xh, axis=-1, keepdims=True)
-        gm = gm_f[r:r + 32, :] + rstd * (dxh - m1 - xh * m2)
+        gm = gm_f[r:r + 32, :] + rstd2[r:r + 32, 0:1] * (dxh - m1 - xh * m2)
         gm_f[r:r + 32, :] = gm
-        gbo = gbo + jnp.sum(gm, axis=0, keepdims=True)
         gmid_ref[r:r + 32, :] = gm.astype(BF)
-    vec_ref[2:3, :] = gg2
-    vec_ref[3:4, :] = gb2
-    vec_ref[4:5, :] = gbo
 
     gmv = gmid_ref[...]
     gctxT = (dot(wout[0], gmv[:, :HW], 1, 1) + dot(wout[1], gmv[:, HW:], 1, 1)).astype(BF)
@@ -336,6 +328,10 @@
         ln_s[0:1, cols] = gg1
         ln_s[1:2, cols] = gb1
     l_first = send(ln_s, ln_pr, pt)
+
+    vec_ref[2:3, :] = jnp.sum(gg_f[...] * xh2[...], axis=0, keepdims=True)
+    vec_ref[3:4, :] = jnp.sum(gg_f[...], axis=0, keepdims=True)
+    vec_ref[4:5, :] = jnp.sum(gm_f[...], axis=0, keepdims=True)
 
     own = pl.ds(pl.multiple_of(t * SL, 8), SL)
     xh_ref[...] = xhat[own, :]
@@ -447,7 +443,7 @@
                 pltpu.VMEM((S, FL), BF), pltpu.VMEM((S, D), BF), pltpu.VMEM((S, FL), BF), pltpu.VMEM((S, FL), BF), pltpu.VMEM((S, D), BF),
                 pltpu.VMEM((3, HL, HD), F32), *[pltpu.VMEM((D,), F32) for _ in range(7)],
                 pltpu.VMEM((2, TP, SL, HW), BF), pltpu.VMEM((2, SL, D), BF), pltpu.VMEM((SL, D), BF), pltpu.VMEM((SL, D), BF),
-                pltpu.VMEM((2, 2, SL, HW), BF), pltpu.VMEM((2, 2, D), F32),
+                pltpu.VMEM((2, 2, SL, HW), BF), pltpu.VMEM((2, 2, D), F32), pltpu.VMEM((S, D), F32), pltpu.VMEM((S, 128), F32),
                 pltpu.SemaphoreType.DMA((9,)), pltpu.SemaphoreType.DMA((N_SEND,)), pltpu.SemaphoreType.DMA((N_SEND,)),
                 pltpu.SemaphoreType.DMA((10,)),
             ],

time: 39 us -> 37.9 us (0.972)
  Pallas kernels: 36.5 us -> 35.8 us
    pallas_call x1, Pallas kernels: 30.4 us -> 29.7 us  [local_step(): pl.pallas_call(block_kernel, out_shape=(pltpu.VMEM((SL, D), BF), pltpu.VM...]
where the time goes in v12:
time: 37.9 us; the launch traced here: 37.8 us
  Pallas kernels  35.8 us (94%)
  starting transfers between devices  1.33 us (4%)
  between operations  0.68 us (2%)
    pallas_call x1, Pallas kernels, local_step(): pl.pallas_call(block_kernel, out_shape=(pltpu.VMEM((SL, D), BF), pltpu.VM...  29.7 us
    pallas_call x1, Pallas kernels, local_step(): pl.pallas_call(write_kernel, out_shape=(sds((SL, D), BF), sds((3 * HL * H...  5.26 us
    ppermute x1, starting transfers between devices, local_step(): r_cr = lax.ppermute(r_hs, 'tp', across)  1.33 us
    pallas_call x1, Pallas kernels, local_step(): pl.pallas_call(last_kernel, out_shape=(sds((SL, D), BF), vec1, vec1), in_...  0.79 us
  transfers between devices with their start and end apart: 1, of which 0 were waited for; matrix products, arithmetic and copies ran while one was open for 0% of the time, Pallas kernels for 14%

profile of v12, /device:TPU:0, one launch (start us, length us, event | category | flops | bytes accessed | tf_op | source)
XLA Modules:
  0.0 37.8 jit_solution(7734897964003396736)
XLA Ops:
  0.7 29.7 %block.1 = (bf16[24,1536]{1,0:T(8,128)(2,1)S(1)}, f32[8,1536]{1,0:T(8,128)S(1)}, bf16[1536,1536]{1,0:T(8,128)(2,1)S(1)}, bf16[1536,1536]{1,0:T(8,128)(2,1)S(1)},...) custom-call(bf16[24,1536]{1,0:T(8,128)(2,1)} %bitcast.13, ...), custom_call_target="tpu_custom_call" | custom-call | tf_op jit(solution)/shard_map/block/pallas_call | solution.py:429
  30.4 1.3 %collective-permute-start = (bf16[32,1536]{1,0:T(8,128)(2,1)S(1)}, bf16[32,1536]{1,0:T(8,128)(2,1)S(1)}, u32[]{:S(2)}, u32[]{:S(2)}) collective-permute-start(bf16[32,1536]{1,0:T(8,128)(2,1)S(1)} %get-tuple-element.57), channel_id=1, source_target_pairs={{0,3},{1,2},{2,1},{3,0},{4,7},{5,6},{6,5},{7,4}} | collective-permute-start | bytes 294920 | tf_op jit(solution)/shard_map/ppermute | solution.py:456
  31.7 5.3 %write.1 = (bf16[24,1536]{1,0:T(8,128)(2,1)}, bf16[1152,1536]{1,0:T(8,128)(2,1)}, f32[3,4,96]{2,1,0:T(4,128)}, bf16[384,1536]{1,0:T(8,128)(2,1)}, f32[1536]{0:T(...) custom-call(bf16[24,1536]{1,0:T(8,128)(2,1)S(1)} %get-tuple-element., ...), custom_call_target="tpu_custom_call" | custom-call | flops 600000000 | bytes 14200000 | tf_op jit(solution)/shard_map/write/pallas_call | solution.py:457
  37.0 0.0 collective-permute-done.rc_ref
  37.0 0.8 %last.1 = (bf16[24,1536]{1,0:T(8,128)(2,1)}, f32[1536]{0:T(1024)}, f32[1536]{0:T(1024)}) custom-call(bf16[24,1536]{1,0:T(8,128)(2,1)S(1)} %get-tuple-element.52.mine_ref, f32[24,1536]{1,0:T(8,128)S(1)} %get-tuple-element.53.xh_ref, f32[24,1536]{1,0:T(8,128)S(1)} %get-tuple-element.54.gm_ref, f32[24,128]{1,0:T(8,128)S(1)} %get-tuple-element.55.rs_ref, ...), custom_call_target="tpu_custom_call" | custom-call | tf_op jit(solution)/shard_map/last/pallas_call | solution.py:469
Async XLA Ops:
  30.4 6.6 %collective-permute-start = (bf16[32,1536]{1,0:T(8,128)(2,1)S(1)}, bf16[32,1536]{1,0:T(8,128)(2,1)S(1)}, u32[]{:S(2)}, u32[]{:S(2)}) collective-permute-start(bf16[32,1536]{1,0:T(8,128)(2,1)S(1)} %get-tuple-element.57), channel_id=1, source_target_pairs={{0,3},{1,2},{2,1},{3,0},{4,7},{5,6},{6,5},{7,4}} | collective-permute-start | bytes 294920 | tf_op jit(solution)/shard_map/ppermute | solution.py:456

commit v13 on v12

--- a/solution.py
+++ b/solution.py
@@ -25,7 +25,8 @@
 NCH = D // CW
 HCH = NCH // 2
 HW = D // 2
-CUT = (0, 256, 512, 640, 768)
+UW = 128
+CUT = (128, 384, 640, 768)
 NCUT = len(CUT) - 1
 
 
@@ -82,6 +83,10 @@
     return send, started
 
 
+def columns(start, width):
+    return pl.ds(start if isinstance(start, int) else pl.multiple_of(start, 128), width)
+
+
 def head_rows(h, e):
     return slice((h * 3 + e) * HD, (h * 3 + e + 1) * HD)
 
@@ -97,7 +102,7 @@
                  wqkv, wout, xf, gm_f, gg_f, xhat, rstd_s, probs, qkvT, par, mp,
                  wup, wdn, xg, gyg, biasT, a_ps, a_pr, a_hs, a_hr, a_cr, a_fr, b_ps, b_pr, b_hs, b_hr, b_cr, b_fr,
                  gact, g_ref, gpre_ref, act_ref, gyf_ref, bqkv_ref, g1_in, be1_in, g2_in, be2_in, bo_in, bd_in, bup_in,
-                 rp, m_pr, m_hs, m_cr, r_pr, ln_x, xh2, rstd2,
+                 rp, m_pr, m_hs, m_cr, r_pr, ln_x, xh2, rstd2, a_un, b_un,
                  wsem, ssem, rsem, isem):
     t, pt, ct, qt, half = places()
     send, started = sender(ssem, rsem)
@@ -180,12 +185,16 @@
         probs[h] = p
         ctx_ref[h * HD:(h + 1) * HD, :] = dot(head(h, 2), p.astype(BF), 1, 0).astype(BF)
 
-    def exchange(part, groups, ps, pr, hs, hr, cr, fr):
+    def exchange(part, groups, ps, pr, hs, hr, cr, fr, un):
         firsts = []
         for k0, k1 in groups:
             cols = slice(CUT[k0], CUT[k1])
             ps[:, cols] = part(1 - half, CUT[k0], CUT[k1]).astype(BF)
             firsts.append(send(ps.at[:, cols], pr.at[:, cols], pt))
+            if k0 == 0:
+                for hh in range(2):
+                    un[0, hh] = part(hh, 0, UW).astype(BF)
+                early = [send(un.at[0], un.at[2], ct), send(un.at[0], un.at[1], pt)]
         outs = []
         for (k0, k1), first in zip(groups, firsts):
             cols = slice(CUT[k0], CUT[k1])
@@ -197,8 +206,19 @@
                 outs.append([send(hs.at[:, c], cr.at[:, c], ct)])
                 if k == NCUT - 1:
                     outs[-1].append(send(hs.at[:, c], fr.at[:, c], qt))
-        local = send(hs, hr, pt)
-        return outs, local
+        local = send(hs.at[:, UW:], hr.at[:, UW:], pt)
+        return outs, local, early
+
+    def early_arrived(early, un):
+        early[0].wait_recv()
+        early.append(send(un.at[2], un.at[3], pt))
+
+    def early_added(early, un, put):
+        early[1].wait_recv()
+        early[2].wait_recv()
+        for hh in range(2):
+            chips = [un[k, hh].astype(F32) + un[k + 1, hh].astype(F32) for k in (0, 2)]
+            put(hh * HW, UW, (chips[0] + chips[1]).astype(BF).astype(F32))
 
     def arrived(out, k, hs, cr, fr, put):
         c = slice(CUT[k], CUT[k + 1])
@@ -217,7 +237,7 @@
     for c in w_cps['out']:
         c.wait()
     ctxT = ctx_ref[...]
-    a_outs, a_local = exchange(lambda hh, c0, c1: dot(ctxT, wout[hh, :, c0:c1], 0, 0), ((0, NCUT),), a_ps, a_pr, a_hs, a_hr, a_cr, a_fr)
+    a_outs, a_local, a_early = exchange(lambda hh, c0, c1: dot(ctxT, wout[hh, :, c0:c1], 0, 0), ((0, NCUT),), a_ps, a_pr, a_hs, a_hr, a_cr, a_fr, a_un)
 
     y_c.wait_recv()
     y_f = send(gyg.at[ct], gyg.at[ct], pt)
@@ -234,11 +254,13 @@
     vec_ref[0:1, :] = jnp.sum(gm_f[...], axis=0, keepdims=True)
 
     def put_x(start, width, val):
-        cols = pl.ds(pl.multiple_of(start, 128), width)
+        cols = columns(start, width)
         xf[:, cols] = xf[:, cols] + val + bo_ref[:, cols]
 
+    early_arrived(a_early, a_un)
     for k, out in enumerate(a_outs):
         arrived(out, k, a_hs, a_cr, a_fr, put_x)
+    early_added(a_early, a_un, put_x)
     passed_on(a_outs, a_local, a_hr, a_fr, put_x)
 
     for r in range(0, S, 32):
@@ -262,9 +284,9 @@
     gprev = gpre_ref[...]
 
     def part_g(hh, c0, c1):
-        return dot(gprev, wup[pl.ds(pl.multiple_of(hh * HW + c0, CW), c1 - c0), :], 1, 1)
-
-    g_outs, g_local = exchange(part_g, ((0, 1), (1, NCUT)), b_ps, b_pr, b_hs, b_hr, b_cr, b_fr)
+        return dot(gprev, wup[columns(hh * HW + c0, c1 - c0), :], 1, 1)
+
+    g_outs, g_local, g_early = exchange(part_g, ((0, 1), (1, NCUT)), b_ps, b_pr, b_hs, b_hr, b_cr, b_fr, b_un)
 
     actv = act_ref[...]
     for n in range(NCH):
@@ -274,13 +296,14 @@
     for n in range(NCH):
         gwdn_ref[n * CW:(n + 1) * CW, :] = dot(act_ref[:, n * CW:(n + 1) * CW], gyv, 0, 0).astype(BF)
     def put_g(start, width, val):
-        gg_f[:, pl.ds(pl.multiple_of(start, 128), width)] = val
-
-    for k in range(HCH):
-        arrived(g_outs[k], k, b_hs, b_cr, b_fr, put_g)
-        for n in range(2 * k, 2 * k + 2):
-            gwup_ref[n * CW:(n + 1) * CW, :] = dot(g_ref[:, n * CW:(n + 1) * CW], gprev, 0, 0).astype(BF)
-    arrived(g_outs[-1], NCUT - 1, b_hs, b_cr, b_fr, put_g)
+        gg_f[:, columns(start, width)] = val
+
+    early_arrived(g_early, b_un)
+    for n in range(NCH):
+        gwup_ref[n * CW:(n + 1) * CW, :] = dot(g_ref[:, n * CW:(n + 1) * CW], gprev, 0, 0).astype(BF)
+        if n % 2:
+            arrived(g_outs[n // 2], n // 2, b_hs, b_cr, b_fr, put_g)
+    early_added(g_early, b_un, put_g)
 
     m_first[0].wait_recv()
     m_hs[...] = (mp[ct].astype(F32) + m_pr[1].astype(F32)).astype(BF)
@@ -361,7 +384,7 @@
         c.wait_send()
 
 
-N_SEND = 6 + 2 * (2 + 4 + 1 + 1 + 3) + 3 + 4 + 1
+N_SEND = 37
 VMEM_A = 36 * 2**20
 VMEM_B = 8 * 2**20
 VMEM_C = 4 * 2**20
@@ -444,6 +467,7 @@
                 pltpu.VMEM((3, HL, HD), F32), *[pltpu.VMEM((D,), F32) for _ in range(7)],
                 pltpu.VMEM((2, TP, SL, HW), BF), pltpu.VMEM((2, SL, D), BF), pltpu.VMEM((SL, D), BF), pltpu.VMEM((SL, D), BF),
                 pltpu.VMEM((2, 2, SL, HW), BF), pltpu.VMEM((2, 2, D), F32), pltpu.VMEM((S, D), F32), pltpu.VMEM((S, 128), F32),
+                pltpu.VMEM((4, 2, S, UW), BF), pltpu.VMEM((4, 2, S, UW), BF),
                 pltpu.SemaphoreType.DMA((9,)), pltpu.SemaphoreType.DMA((N_SEND,)), pltpu.SemaphoreType.DMA((N_SEND,)),
                 pltpu.SemaphoreType.DMA((10,)),
             ],

time: 37.9 us -> 36.9 us (0.974)
  Pallas kernels: 35.8 us -> 35.1 us
    pallas_call x1, Pallas kernels: 29.7 us -> 29.1 us  [local_step(): pl.pallas_call(block_kernel, out_shape=(pltpu.VMEM((SL, D), BF), pltpu.VM...]
where the time goes in v13:
time: 36.9 us; the launch traced here: 36.8 us
  Pallas kernels  35.1 us (95%)
  starting transfers between devices  0.98 us (3%)
  between operations  0.68 us (2%)
    pallas_call x1, Pallas kernels, local_step(): pl.pallas_call(block_kernel, out_shape=(pltpu.VMEM((SL, D), BF), pltpu.VM...  29.1 us
    pallas_call x1, Pallas kernels, local_step(): pl.pallas_call(write_kernel, out_shape=(sds((SL, D), BF), sds((3 * HL * H...  5.26 us
    ppermute x1, starting transfers between devices, local_step(): r_cr = lax.ppermute(r_hs, 'tp', across)  0.98 us
    pallas_call x1, Pallas kernels, local_step(): pl.pallas_call(last_kernel, out_shape=(sds((SL, D), BF), vec1, vec1), in_...  0.79 us
  transfers between devices with their start and end apart: 1, of which 0 were waited for; matrix products, arithmetic and copies ran while one was open for 0% of the time, Pallas kernels for 14%

profile of v13, /device:TPU:0, one launch (start us, length us, event | category | flops | bytes accessed | tf_op | source)
XLA Modules:
  0.0 36.8 jit_solution(1270026779077684790)
XLA Ops:
  0.7 29.1 %block.1 = (bf16[24,1536]{1,0:T(8,128)(2,1)S(1)}, f32[8,1536]{1,0:T(8,128)S(1)}, bf16[1536,1536]{1,0:T(8,128)(2,1)S(1)}, bf16[1536,1536]{1,0:T(8,128)(2,1)S(1)},...) custom-call(bf16[24,1536]{1,0:T(8,128)(2,1)} %bitcast.13, ...), custom_call_target="tpu_custom_call" | custom-call | tf_op jit(solution)/shard_map/block/pallas_call | solution.py:452
  29.7 1.0 %collective-permute-start = (bf16[32,1536]{1,0:T(8,128)(2,1)S(1)}, bf16[32,1536]{1,0:T(8,128)(2,1)S(1)}, u32[]{:S(2)}, u32[]{:S(2)}) collective-permute-start(bf16[32,1536]{1,0:T(8,128)(2,1)S(1)} %get-tuple-element.57), channel_id=1, source_target_pairs={{0,3},{1,2},{2,1},{3,0},{4,7},{5,6},{6,5},{7,4}} | collective-permute-start | bytes 294920 | tf_op jit(solution)/shard_map/ppermute | solution.py:480
  30.7 5.3 %write.1 = (bf16[24,1536]{1,0:T(8,128)(2,1)}, bf16[1152,1536]{1,0:T(8,128)(2,1)}, f32[3,4,96]{2,1,0:T(4,128)}, bf16[384,1536]{1,0:T(8,128)(2,1)}, f32[1536]{0:T(...) custom-call(bf16[24,1536]{1,0:T(8,128)(2,1)S(1)} %get-tuple-element., ...), custom_call_target="tpu_custom_call" | custom-call | flops 600000000 | bytes 14200000 | tf_op jit(solution)/shard_map/write/pallas_call | solution.py:481
  36.0 0.0 collective-permute-done.rc_ref
  36.0 0.8 %last.1 = (bf16[24,1536]{1,0:T(8,128)(2,1)}, f32[1536]{0:T(1024)}, f32[1536]{0:T(1024)}) custom-call(bf16[24,1536]{1,0:T(8,128)(2,1)S(1)} %get-tuple-element.52.mine_ref, f32[24,1536]{1,0:T(8,128)S(1)} %get-tuple-element.53.xh_ref, f32[24,1536]{1,0:T(8,128)S(1)} %get-tuple-element.54.gm_ref, f32[24,128]{1,0:T(8,128)S(1)} %get-tuple-element.55.rs_ref, ...), custom_call_target="tpu_custom_call" | custom-call | tf_op jit(solution)/shard_map/last/pallas_call | solution.py:493
Async XLA Ops:
  29.7 6.2 %collective-permute-start = (bf16[32,1536]{1,0:T(8,128)(2,1)S(1)}, bf16[32,1536]{1,0:T(8,128)(2,1)S(1)}, u32[]{:S(2)}, u32[]{:S(2)}) collective-permute-start(bf16[32,1536]{1,0:T(8,128)(2,1)S(1)} %get-tuple-element.57), channel_id=1, source_target_pairs={{0,3},{1,2},{2,1},{3,0},{4,7},{5,6},{6,5},{7,4}} | collective-permute-start | bytes 294920 | tf_op jit(solution)/shard_map/ppermute | solution.py:480

commit v14 on v13

--- a/solution.py
+++ b/solution.py
@@ -162,8 +162,8 @@
 
     w_cps['qkv'][0].wait()
     hv = h_ref[...]
-    for h in range(HL):
-        rows = slice(h * 3 * HD, (h + 1) * 3 * HD)
+    for h in range(2):
+        rows = slice(h * 6 * HD, (h + 1) * 6 * HD)
         qkvT[rows, :] = (dot(wqkv[rows, :], hv, 1, 1) + biasT[rows, :]).astype(BF)
 
     scale = HD ** -0.5
@@ -272,8 +272,8 @@
 
     w_cps['up'][0].wait()
     gv = g_ref[...]
-    for n in range(NCH):
-        cols = slice(n * CW, (n + 1) * CW)
+    for n in range(NCH // 2):
+        cols = slice(n * 2 * CW, (n + 1) * 2 * CW)
         pre = dot(gv, wup[:, cols], 1, 0) + bup_ref[:, cols]
         val, der = gelu_parts(pre)
         act_ref[:, cols] = val.astype(BF)

time: 36.9 us -> 37 us (level)
  no operation moved by 1% of the time
where the time goes in v14:
time: 37 us; the launch traced here: 36.9 us
  Pallas kernels  35.3 us (95%)
  starting transfers between devices  0.97 us (3%)
  between operations  0.68 us (2%)
    pallas_call x1, Pallas kernels, local_step(): pl.pallas_call(block_kernel, out_shape=(pltpu.VMEM((SL, D), BF), pltpu.VM...  29.2 us
    pallas_call x1, Pallas kernels, local_step(): pl.pallas_call(write_kernel, out_shape=(sds((SL, D), BF), sds((3 * HL * H...  5.26 us
    ppermute x1, starting transfers between devices, local_step(): r_cr = lax.ppermute(r_hs, 'tp', across)  0.97 us
    pallas_call x1, Pallas kernels, local_step(): pl.pallas_call(last_kernel, out_shape=(sds((SL, D), BF), vec1, vec1), in_...  0.79 us
  transfers between devices with their start and end apart: 1, of which 0 were waited for; matrix products, arithmetic and copies ran while one was open for 0% of the time, Pallas kernels for 14%

profile of v14, /device:TPU:0, one launch (start us, length us, event | category | flops | bytes accessed | tf_op | source)
XLA Modules:
  0.0 36.9 jit_solution(8955636343242531560)
XLA Ops:
  0.7 29.2 %block.1 = (bf16[24,1536]{1,0:T(8,128)(2,1)S(1)}, f32[8,1536]{1,0:T(8,128)S(1)}, bf16[1536,1536]{1,0:T(8,128)(2,1)S(1)}, bf16[1536,1536]{1,0:T(8,128)(2,1)S(1)},...) custom-call(bf16[24,1536]{1,0:T(8,128)(2,1)} %bitcast.13, ...), custom_call_target="tpu_custom_call" | custom-call | tf_op jit(solution)/shard_map/block/pallas_call | solution.py:452
  29.9 1.0 %collective-permute-start = (bf16[32,1536]{1,0:T(8,128)(2,1)S(1)}, bf16[32,1536]{1,0:T(8,128)(2,1)S(1)}, u32[]{:S(2)}, u32[]{:S(2)}) collective-permute-start(bf16[32,1536]{1,0:T(8,128)(2,1)S(1)} %get-tuple-element.57), channel_id=1, source_target_pairs={{0,3},{1,2},{2,1},{3,0},{4,7},{5,6},{6,5},{7,4}} | collective-permute-start | bytes 294920 | tf_op jit(solution)/shard_map/ppermute | solution.py:480
  30.9 5.3 %write.1 = (bf16[24,1536]{1,0:T(8,128)(2,1)}, bf16[1152,1536]{1,0:T(8,128)(2,1)}, f32[3,4,96]{2,1,0:T(4,128)}, bf16[384,1536]{1,0:T(8,128)(2,1)}, f32[1536]{0:T(...) custom-call(bf16[24,1536]{1,0:T(8,128)(2,1)S(1)} %get-tuple-element., ...), custom_call_target="tpu_custom_call" | custom-call | flops 600000000 | bytes 14200000 | tf_op jit(solution)/shard_map/write/pallas_call | solution.py:481
  36.1 0.0 collective-permute-done.rc_ref
  36.1 0.8 %last.1 = (bf16[24,1536]{1,0:T(8,128)(2,1)}, f32[1536]{0:T(1024)}, f32[1536]{0:T(1024)}) custom-call(bf16[24,1536]{1,0:T(8,128)(2,1)S(1)} %get-tuple-element.52.mine_ref, f32[24,1536]{1,0:T(8,128)S(1)} %get-tuple-element.53.xh_ref, f32[24,1536]{1,0:T(8,128)S(1)} %get-tuple-element.54.gm_ref, f32[24,128]{1,0:T(8,128)S(1)} %get-tuple-element.55.rs_ref, ...), custom_call_target="tpu_custom_call" | custom-call | tf_op jit(solution)/shard_map/last/pallas_call | solution.py:493
Async XLA Ops:
  29.9 6.2 %collective-permute-start = (bf16[32,1536]{1,0:T(8,128)(2,1)S(1)}, bf16[32,1536]{1,0:T(8,128)(2,1)S(1)}, u32[]{:S(2)}, u32[]{:S(2)}) collective-permute-start(bf16[32,1536]{1,0:T(8,128)(2,1)S(1)} %get-tuple-element.57), channel_id=1, source_target_pairs={{0,3},{1,2},{2,1},{3,0},{4,7},{5,6},{6,5},{7,4}} | collective-permute-start | bytes 294920 | tf_op jit(solution)/shard_map/ppermute | solution.py:480

commit v15 on v13

--- a/solution.py
+++ b/solution.py
@@ -335,8 +335,9 @@
 
     gqv = gqkv_ref[...]
     r_first = []
+    for n in range(NCH):
+        row_blocks(rp.at[n // HCH], slice(n % HCH * CW, (n % HCH + 1) * CW), dot(gqv, wqkv[:, n * CW:(n + 1) * CW], 0, 0))
     for k in range(2):
-        row_blocks(rp.at[k], slice(0, HW), dot(gqv, wqkv[:, k * HW:(k + 1) * HW], 0, 0))
         r_first.append((send(rp.at[k, qt], r_pr.at[k, 1], pt), send(rp.at[k, pt], r_pr.at[k, 0], pt)))
 
     ln_s, ln_pr = ln_x.at[0], ln_x.at[1]
@@ -424,17 +425,25 @@
         c.wait()
 
 
-def last_kernel(mine_ref, xh_ref, gm_ref, rs_ref, g1_ref, rc_ref, ln_ref, gx_ref, gl1_ref, bl1_ref):
+def last_kernel(mine_ref, xh_ref, gm_ref, rs_ref, g1_ref, rc_ref, ln_ref, gx_hbm, gl1_hbm, bl1_hbm, gx_ref, gl1_ref, bl1_ref, sem):
+    lc = rc_ref[SL:SL + 8, :].astype(F32)
+    ln = ln_ref[...] + (lc[0:2, :] + lc[2:4, :] + lc[4:6, :])
+    gl1_ref[...] = ln[0, :]
+    bl1_ref[...] = ln[1, :]
+    cps = [pltpu.make_async_copy(gl1_ref, gl1_hbm, sem.at[0]), pltpu.make_async_copy(bl1_ref, bl1_hbm, sem.at[1]),
+           pltpu.make_async_copy(gx_ref, gx_hbm, sem.at[2])]
+    cps[0].start()
+    cps[1].start()
+
     gh = (mine_ref[...].astype(F32) + rc_ref[0:SL, :].astype(F32)).astype(BF).astype(F32)
     xh = xh_ref[...]
     dxh = gh * g1_ref[...]
     m1 = jnp.mean(dxh, axis=-1, keepdims=True)
     m2 = jnp.mean(dxh * xh, axis=-1, keepdims=True)
     gx_ref[...] = (gm_ref[...] + rs_ref[:, 0:1] * (dxh - m1 - xh * m2)).astype(BF)
-    lc = rc_ref[SL:SL + 8, :].astype(F32)
-    ln = ln_ref[...] + (lc[0:2, :] + lc[2:4, :] + lc[4:6, :])
-    gl1_ref[...] = ln[0, :]
-    bl1_ref[...] = ln[1, :]
+    cps[2].start()
+    for c in cps:
+        c.wait()
 
 
 def solution(mesh):
@@ -494,7 +503,8 @@
             last_kernel,
             out_shape=(sds((SL, D), BF), vec1, vec1),
             in_specs=[VM] * 7,
-            out_specs=(VM,) * 3,
+            out_specs=(ANY,) * 3,
+            scratch_shapes=[pltpu.VMEM((SL, D), BF), pltpu.VMEM((D,), F32), pltpu.VMEM((D,), F32), pltpu.SemaphoreType.DMA((3,))],
             compiler_params=pltpu.CompilerParams(vmem_limit_bytes=VMEM_C),
             name='last',
         )(mine, xh, gm, rs, g1v, r_cr, ln_hs)

time: 36.9 us -> 36.8 us (level)
  no operation moved by 1% of the time
where the time goes in v15:
time: 36.8 us; the launch traced here: 36.7 us
  Pallas kernels  35 us (95%)
  starting transfers between devices  1.01 us (3%)
  between operations  0.68 us (2%)
    pallas_call x1, Pallas kernels, local_step(): pl.pallas_call(block_kernel, out_shape=(pltpu.VMEM((SL, D), BF), pltpu.VM...  29 us
    pallas_call x1, Pallas kernels, local_step(): pl.pallas_call(write_kernel, out_shape=(sds((SL, D), BF), sds((3 * HL * H...  5.26 us
    ppermute x1, starting transfers between devices, local_step(): r_cr = lax.ppermute(r_hs, 'tp', across)  1.01 us
    pallas_call x1, Pallas kernels, local_step(): pl.pallas_call(last_kernel, out_shape=(sds((SL, D), BF), vec1, vec1), in_...  0.81 us
  transfers between devices with their start and end apart: 1, of which 0 were waited for; matrix products, arithmetic and copies ran while one was open for 0% of the time, Pallas kernels for 14%

profile of v15, /device:TPU:0, one launch (start us, length us, event | category | flops | bytes accessed | tf_op | source)
XLA Modules:
  0.0 36.7 jit_solution(13672267413238716941)
XLA Ops:
  0.7 29.0 %block.1 = (bf16[24,1536]{1,0:T(8,128)(2,1)S(1)}, f32[8,1536]{1,0:T(8,128)S(1)}, bf16[1536,1536]{1,0:T(8,128)(2,1)S(1)}, bf16[1536,1536]{1,0:T(8,128)(2,1)S(1)},...) custom-call(bf16[24,1536]{1,0:T(8,128)(2,1)} %bitcast.13, ...), custom_call_target="tpu_custom_call" | custom-call | tf_op jit(solution)/shard_map/block/pallas_call | solution.py:461
  29.6 1.0 %collective-permute-start = (bf16[32,1536]{1,0:T(8,128)(2,1)S(1)}, bf16[32,1536]{1,0:T(8,128)(2,1)S(1)}, u32[]{:S(2)}, u32[]{:S(2)}) collective-permute-start(bf16[32,1536]{1,0:T(8,128)(2,1)S(1)} %get-tuple-element.57), channel_id=1, source_target_pairs={{0,3},{1,2},{2,1},{3,0},{4,7},{5,6},{6,5},{7,4}} | collective-permute-start | bytes 294920 | tf_op jit(solution)/shard_map/ppermute | solution.py:489
  30.6 5.3 %write.1 = (bf16[24,1536]{1,0:T(8,128)(2,1)}, bf16[1152,1536]{1,0:T(8,128)(2,1)}, f32[3,4,96]{2,1,0:T(4,128)}, bf16[384,1536]{1,0:T(8,128)(2,1)}, f32[1536]{0:T(...) custom-call(bf16[24,1536]{1,0:T(8,128)(2,1)S(1)} %get-tuple-element., ...), custom_call_target="tpu_custom_call" | custom-call | flops 600000000 | bytes 14200000 | tf_op jit(solution)/shard_map/write/pallas_call | solution.py:490
  35.9 0.0 collective-permute-done.rc_ref
  35.9 0.8 %last.1 = (bf16[24,1536]{1,0:T(8,128)(2,1)}, f32[1536]{0:T(1024)}, f32[1536]{0:T(1024)}) custom-call(bf16[24,1536]{1,0:T(8,128)(2,1)S(1)} %get-tuple-element.52.mine_ref, f32[24,1536]{1,0:T(8,128)S(1)} %get-tuple-element.53.xh_ref, f32[24,1536]{1,0:T(8,128)S(1)} %get-tuple-element.54.gm_ref, f32[24,128]{1,0:T(8,128)S(1)} %get-tuple-element.55.rs_ref, ...), custom_call_target="tpu_custom_call" | custom-call | tf_op jit(solution)/shard_map/last/pallas_call | solution.py:502
Async XLA Ops:
  29.6 6.3 %collective-permute-start = (bf16[32,1536]{1,0:T(8,128)(2,1)S(1)}, bf16[32,1536]{1,0:T(8,128)(2,1)S(1)}, u32[]{:S(2)}, u32[]{:S(2)}) collective-permute-start(bf16[32,1536]{1,0:T(8,128)(2,1)S(1)} %get-tuple-element.57), channel_id=1, source_target_pairs={{0,3},{1,2},{2,1},{3,0},{4,7},{5,6},{6,5},{7,4}} | collective-permute-start | bytes 294920 | tf_op jit(solution)/shard_map/ppermute | solution.py:489

commit v16 on v13

--- a/solution.py
+++ b/solution.py
@@ -335,21 +335,17 @@
 
     gqv = gqkv_ref[...]
     r_first = []
+    ln_s, ln_pr = ln_x.at[0], ln_x.at[1]
+    for n in range(NCH):
+        cols = slice(n * CW, (n + 1) * CW)
+        v = dot(gqv, wqkv[:, cols], 0, 0)
+        row_blocks(rp.at[n // HCH], slice(n % HCH * CW, (n % HCH + 1) * CW), v)
+        v = v.astype(BF).astype(F32)
+        ln_s[0:1, cols] = jnp.sum(v * xhat[:, cols], axis=0, keepdims=True)
+        ln_s[1:2, cols] = jnp.sum(v, axis=0, keepdims=True)
     for k in range(2):
-        row_blocks(rp.at[k], slice(0, HW), dot(gqv, wqkv[:, k * HW:(k + 1) * HW], 0, 0))
         r_first.append((send(rp.at[k, qt], r_pr.at[k, 1], pt), send(rp.at[k, pt], r_pr.at[k, 0], pt)))
 
-    ln_s, ln_pr = ln_x.at[0], ln_x.at[1]
-    for k in range(2):
-        cols = slice(k * HW, (k + 1) * HW)
-        gg1 = jnp.zeros((1, HW), F32)
-        gb1 = jnp.zeros((1, HW), F32)
-        for i in range(TP):
-            v = rp[k, i].astype(F32)
-            gg1 = gg1 + jnp.sum(v * xhat[i * SL:(i + 1) * SL, cols], axis=0, keepdims=True)
-            gb1 = gb1 + jnp.sum(v, axis=0, keepdims=True)
-        ln_s[0:1, cols] = gg1
-        ln_s[1:2, cols] = gb1
     l_first = send(ln_s, ln_pr, pt)
 
     vec_ref[2:3, :] = jnp.sum(gg_f[...] * xh2[...], axis=0, keepdims=True)

time: 36.9 us -> 36.8 us (level)
  no operation moved by 1% of the time
where the time goes in v16:
time: 36.8 us; the launch traced here: 36.7 us
  Pallas kernels  35 us (95%)
  starting transfers between devices  1.01 us (3%)
  between operations  0.68 us (2%)
    pallas_call x1, Pallas kernels, local_step(): pl.pallas_call(block_kernel, out_shape=(pltpu.VMEM((SL, D), BF), pltpu.VM...  29 us
    pallas_call x1, Pallas kernels, local_step(): pl.pallas_call(write_kernel, out_shape=(sds((SL, D), BF), sds((3 * HL * H...  5.26 us
    ppermute x1, starting transfers between devices, local_step(): r_cr = lax.ppermute(r_hs, 'tp', across)  1.01 us
    pallas_call x1, Pallas kernels, local_step(): pl.pallas_call(last_kernel, out_shape=(sds((SL, D), BF), vec1, vec1), in_...  0.79 us
  transfers between devices with their start and end apart: 1, of which 0 were waited for; matrix products, arithmetic and copies ran while one was open for 0% of the time, Pallas kernels for 14%

profile of v16, /device:TPU:0, one launch (start us, length us, event | category | flops | bytes accessed | tf_op | source)
XLA Modules:
  0.0 36.7 jit_solution(18221398348219304092)
XLA Ops:
  0.7 29.0 %block.1 = (bf16[24,1536]{1,0:T(8,128)(2,1)S(1)}, f32[8,1536]{1,0:T(8,128)S(1)}, bf16[1536,1536]{1,0:T(8,128)(2,1)S(1)}, bf16[1536,1536]{1,0:T(8,128)(2,1)S(1)},...) custom-call(bf16[24,1536]{1,0:T(8,128)(2,1)} %bitcast.13, ...), custom_call_target="tpu_custom_call" | custom-call | tf_op jit(solution)/shard_map/block/pallas_call | solution.py:448
  29.6 1.0 %collective-permute-start = (bf16[32,1536]{1,0:T(8,128)(2,1)S(1)}, bf16[32,1536]{1,0:T(8,128)(2,1)S(1)}, u32[]{:S(2)}, u32[]{:S(2)}) collective-permute-start(bf16[32,1536]{1,0:T(8,128)(2,1)S(1)} %get-tuple-element.57), channel_id=1, source_target_pairs={{0,3},{1,2},{2,1},{3,0},{4,7},{5,6},{6,5},{7,4}} | collective-permute-start | bytes 294920 | tf_op jit(solution)/shard_map/ppermute | solution.py:476
  30.7 5.3 %write.1 = (bf16[24,1536]{1,0:T(8,128)(2,1)}, bf16[1152,1536]{1,0:T(8,128)(2,1)}, f32[3,4,96]{2,1,0:T(4,128)}, bf16[384,1536]{1,0:T(8,128)(2,1)}, f32[1536]{0:T(...) custom-call(bf16[24,1536]{1,0:T(8,128)(2,1)S(1)} %get-tuple-element., ...), custom_call_target="tpu_custom_call" | custom-call | flops 600000000 | bytes 14200000 | tf_op jit(solution)/shard_map/write/pallas_call | solution.py:477
  35.9 0.0 collective-permute-done.rc_ref
  35.9 0.8 %last.1 = (bf16[24,1536]{1,0:T(8,128)(2,1)}, f32[1536]{0:T(1024)}, f32[1536]{0:T(1024)}) custom-call(bf16[24,1536]{1,0:T(8,128)(2,1)S(1)} %get-tuple-element.52.mine_ref, f32[24,1536]{1,0:T(8,128)S(1)} %get-tuple-element.53.xh_ref, f32[24,1536]{1,0:T(8,128)S(1)} %get-tuple-element.54.gm_ref, f32[24,128]{1,0:T(8,128)S(1)} %get-tuple-element.55.rs_ref, ...), custom_call_target="tpu_custom_call" | custom-call | tf_op jit(solution)/shard_map/last/pallas_call | solution.py:489
Async XLA Ops:
  29.6 6.3 %collective-permute-start = (bf16[32,1536]{1,0:T(8,128)(2,1)S(1)}, bf16[32,1536]{1,0:T(8,128)(2,1)S(1)}, u32[]{:S(2)}, u32[]{:S(2)}) collective-permute-start(bf16[32,1536]{1,0:T(8,128)(2,1)S(1)} %get-tuple-element.57), channel_id=1, source_target_pairs={{0,3},{1,2},{2,1},{3,0},{4,7},{5,6},{6,5},{7,4}} | collective-permute-start | bytes 294920 | tf_op jit(solution)/shard_map/ppermute | solution.py:476

commit v17 on v16

--- a/solution.py
+++ b/solution.py
@@ -303,11 +303,12 @@
         gwup_ref[n * CW:(n + 1) * CW, :] = dot(g_ref[:, n * CW:(n + 1) * CW], gprev, 0, 0).astype(BF)
         if n % 2:
             arrived(g_outs[n // 2], n // 2, b_hs, b_cr, b_fr, put_g)
+        if n == HCH:
+            m_first[0].wait_recv()
+            m_hs[...] = (mp[ct].astype(F32) + m_pr[1].astype(F32)).astype(BF)
+            m_out = send(m_hs, m_cr, ct)
     early_added(g_early, b_un, put_g)
 
-    m_first[0].wait_recv()
-    m_hs[...] = (mp[ct].astype(F32) + m_pr[1].astype(F32)).astype(BF)
-    m_out = send(m_hs, m_cr, ct)
 
     passed_on(g_outs, g_local, b_hr, b_fr, put_g)
 
@@ -357,6 +358,11 @@
     gm_ref[...] = gm_f[own, :]
     rs_ref[...] = rstd_s[own, :]
     g1_out[...] = par[0:1, :]
+
+    m_first[1].wait_recv()
+    m_out.wait_recv()
+    m_sum = (mp[t].astype(F32) + m_pr[0].astype(F32)).astype(BF).astype(F32) + m_cr[...].astype(F32)
+    y_ref[...] = (xf[own, :] + m_sum.astype(BF).astype(F32) + bd_ref[...]).astype(BF)
 
     for k in range(2):
         cols = slice(k * HW, (k + 1) * HW)
@@ -372,10 +378,6 @@
         ln_rows.append(ln.astype(BF).astype(F32))
         ln = ln - ln_rows[-1]
     r_hs[SL:SL + 8, :] = jnp.concatenate(ln_rows + [jnp.zeros((2, D), F32)], axis=0).astype(BF)
-    m_first[1].wait_recv()
-    m_out.wait_recv()
-    m_sum = (mp[t].astype(F32) + m_pr[0].astype(F32)).astype(BF).astype(F32) + m_cr[...].astype(F32)
-    y_ref[...] = (xf[own, :] + m_sum.astype(BF).astype(F32) + bd_ref[...]).astype(BF)
     for c in started:
         c.wait_send()
 

time: 36.8 us -> 36.7 us (level)
  no operation moved by 1% of the time
where the time goes in v17:
time: 36.7 us; the launch traced here: 36.6 us
  Pallas kernels  34.9 us (95%)
  starting transfers between devices  1.02 us (3%)
  between operations  0.68 us (2%)
    pallas_call x1, Pallas kernels, local_step(): pl.pallas_call(block_kernel, out_shape=(pltpu.VMEM((SL, D), BF), pltpu.VM...  28.9 us
    pallas_call x1, Pallas kernels, local_step(): pl.pallas_call(write_kernel, out_shape=(sds((SL, D), BF), sds((3 * HL * H...  5.26 us
    ppermute x1, starting transfers between devices, local_step(): r_cr = lax.ppermute(r_hs, 'tp', across)  1.02 us
    pallas_call x1, Pallas kernels, local_step(): pl.pallas_call(last_kernel, out_shape=(sds((SL, D), BF), vec1, vec1), in_...  0.79 us
  transfers between devices with their start and end apart: 1, of which 0 were waited for; matrix products, arithmetic and copies ran while one was open for 0% of the time, Pallas kernels for 14%

profile of v17, /device:TPU:0, one launch (start us, length us, event | category | flops | bytes accessed | tf_op | source)
XLA Modules:
  0.0 36.6 jit_solution(9473364214450344086)
XLA Ops:
  0.7 28.9 %block.1 = (bf16[24,1536]{1,0:T(8,128)(2,1)S(1)}, f32[8,1536]{1,0:T(8,128)S(1)}, bf16[1536,1536]{1,0:T(8,128)(2,1)S(1)}, bf16[1536,1536]{1,0:T(8,128)(2,1)S(1)},...) custom-call(bf16[24,1536]{1,0:T(8,128)(2,1)} %bitcast.13, ...), custom_call_target="tpu_custom_call" | custom-call | tf_op jit(solution)/shard_map/block/pallas_call | solution.py:450
  29.6 1.0 %collective-permute-start = (bf16[32,1536]{1,0:T(8,128)(2,1)S(1)}, bf16[32,1536]{1,0:T(8,128)(2,1)S(1)}, u32[]{:S(2)}, u32[]{:S(2)}) collective-permute-start(bf16[32,1536]{1,0:T(8,128)(2,1)S(1)} %get-tuple-element.57), channel_id=1, source_target_pairs={{0,3},{1,2},{2,1},{3,0},{4,7},{5,6},{6,5},{7,4}} | collective-permute-start | bytes 294920 | tf_op jit(solution)/shard_map/ppermute | solution.py:478
  30.6 5.3 %write.1 = (bf16[24,1536]{1,0:T(8,128)(2,1)}, bf16[1152,1536]{1,0:T(8,128)(2,1)}, f32[3,4,96]{2,1,0:T(4,128)}, bf16[384,1536]{1,0:T(8,128)(2,1)}, f32[1536]{0:T(...) custom-call(bf16[24,1536]{1,0:T(8,128)(2,1)S(1)} %get-tuple-element., ...), custom_call_target="tpu_custom_call" | custom-call | flops 600000000 | bytes 14200000 | tf_op jit(solution)/shard_map/write/pallas_call | solution.py:479
  35.9 0.0 collective-permute-done.rc_ref
  35.9 0.8 %last.1 = (bf16[24,1536]{1,0:T(8,128)(2,1)}, f32[1536]{0:T(1024)}, f32[1536]{0:T(1024)}) custom-call(bf16[24,1536]{1,0:T(8,128)(2,1)S(1)} %get-tuple-element.52.mine_ref, f32[24,1536]{1,0:T(8,128)S(1)} %get-tuple-element.53.xh_ref, f32[24,1536]{1,0:T(8,128)S(1)} %get-tuple-element.54.gm_ref, f32[24,128]{1,0:T(8,128)S(1)} %get-tuple-element.55.rs_ref, ...), custom_call_target="tpu_custom_call" | custom-call | tf_op jit(solution)/shard_map/last/pallas_call | solution.py:491
Async XLA Ops:
  29.6 6.3 %collective-permute-start = (bf16[32,1536]{1,0:T(8,128)(2,1)S(1)}, bf16[32,1536]{1,0:T(8,128)(2,1)S(1)}, u32[]{:S(2)}, u32[]{:S(2)}) collective-permute-start(bf16[32,1536]{1,0:T(8,128)(2,1)S(1)} %get-tuple-element.57), channel_id=1, source_target_pairs={{0,3},{1,2},{2,1},{3,0},{4,7},{5,6},{6,5},{7,4}} | collective-permute-start | bytes 294920 | tf_op jit(solution)/shard_map/ppermute | solution.py:478
